TPU v7x, 32 devices: a whole 2x2x4 slice. The times are simulated.
32 devices in a mesh: dp: 2 (over core), ctx: 4 (over y, x), tp: 4 (over z).
Axes of the slice: x: 2, y: 2, z: 4, core: 2. Of those that a mesh axis runs over, the one named last changes fastest.
Arguments:
- layer_in: bfloat16 [4096, 2304], P(('dp', 'ctx', 'tp')), may hold values from -6 to 6
- cotangent: bfloat16 [4096, 2304], P(('dp', 'ctx', 'tp')), may hold values from -6 to 6
- norm_gains: float32 [4, 2304], replicated, may hold values from 0.25 to 1.75
- w_query: bfloat16 [2304, 2048], P('dp', 'tp'), may hold values from -1.25 to 1.25
- w_key: bfloat16 [2304, 1024], P('dp', 'tp'), may hold values from -0.125 to 0.125
- w_value: bfloat16 [2304, 1024], P('dp', 'tp'), may hold values from -0.125 to 0.125
- w_out: bfloat16 [2048, 2304], P('tp', 'dp'), may hold values from -0.125 to 0.125
- w_gate: bfloat16 [2304, 9216], P('dp', 'tp'), may hold values from -0.125 to 0.125
- w_up: bfloat16 [2304, 9216], P('dp', 'tp'), may hold values from -0.125 to 0.125
- w_down: bfloat16 [9216, 2304], P('tp', 'dp'), may hold values from -0.0625 to 0.0625
Outputs:
- layer_out: bfloat16 [4096, 2304], P(('dp', 'ctx', 'tp'))
- input_grad: float32 [4096, 2304], P(('dp', 'ctx', 'tp'))
- gain_grads: float32 [4, 2304], P(None, ('dp', 'ctx', 'tp'))
- grad_query: float32 [2304, 2048], P(('dp', 'ctx'), 'tp')
- grad_key: float32 [2304, 1024], P(('dp', 'ctx'), 'tp')
- grad_value: float32 [2304, 1024], P(('dp', 'ctx'), 'tp')
- grad_out: float32 [2048, 2304], P('tp', ('dp', 'ctx'))
- grad_gate: float32 [2304, 9216], P(('dp', 'ctx'), 'tp')
- grad_up: float32 [2304, 9216], P(('dp', 'ctx'), 'tp')
- grad_down: float32 [9216, 2304], P('tp', ('dp', 'ctx'))
All inputs are finite; a program needn't handle non-finite values.
Results may differ from a plain program's by a relative error of at most 0.028.
The roundings to bfloat16 on the way count: a program that leaves them out, or rounds other values in their place, can miss the bound.
Values may be sent and summed in bfloat16 or wider, within the bound.
A program may use at most 256 MiB of HBM per device.

v0:
```python
import jax
import jax.numpy as jnp
from jax import lax
from jax.sharding import PartitionSpec as P

HEAD = 256


EPS = 1e-06
CAP = 50.0
THETA = 10000.0


def rms_scale(values, gain_row):
    return values * lax.rsqrt(jnp.mean(values * values, axis=-1, keepdims=True) + EPS) * gain_row


def glu_product(gate_proj, up_proj):
    return jax.nn.gelu(gate_proj, approximate=True) * up_proj


def rope_tables(positions, head_width):
    half_width = head_width // 2
    frequency = THETA ** (-(jnp.arange(half_width, dtype=jnp.float32) * 2.0) / head_width)
    angles = positions.astype(jnp.float32)[:, None] * frequency[None, :]
    cosine = jnp.concatenate([jnp.cos(angles), jnp.cos(angles)], axis=1)
    sine_table = jnp.concatenate([jnp.sin(angles), jnp.sin(angles)], axis=1)
    return (cosine, sine_table)


def rotate(values, cosine, sine_table, sine_sign):
    half_width = values.shape[-1] // 2
    turned = jnp.concatenate([-values[..., half_width:], values[..., :half_width]], axis=-1)
    return values * cosine[:, None, :] + turned * (sine_sign * sine_table)[:, None, :]


def inner_rows(former, latter):
    return lax.dot_general(
        former, latter, (((0,), (0,)), ((), ())), preferred_element_type=jnp.float32
    )


def times_transposed(former, latter):
    return lax.dot_general(
        former, latter, (((1,), (1,)), ((), ())), preferred_element_type=jnp.float32
    )


def fetch_weights(query_part, key_part, value_part, out_part, gate_part, up_part, down_part):
    return (
        lax.all_gather(query_part, "dp", axis=0, tiled=True),
        lax.all_gather(key_part, "dp", axis=0, tiled=True),
        lax.all_gather(value_part, "dp", axis=0, tiled=True),
        lax.all_gather(out_part, "dp", axis=1, tiled=True),
        lax.all_gather(gate_part, "dp", axis=0, tiled=True),
        lax.all_gather(up_part, "dp", axis=0, tiled=True),
        lax.all_gather(down_part, "dp", axis=1, tiled=True),
    )


def spread_rows(rows_part):
    return lax.all_gather(rows_part, "tp", axis=0, tiled=True)


def spread_grads(rows_part):
    return lax.all_gather(rows_part, "tp", axis=0, tiled=True)


def collect_rows(term_fn, row_total):
    return lax.psum_scatter(
        term_fn(jnp.int32(0), row_total * lax.axis_size("tp")).astype(jnp.bfloat16),
        "tp",
        scatter_dimension=0,
        tiled=True,
    ).astype(jnp.float32)


def shards(layer_in, cotangent, norm_gains, w_query, w_key, w_value, w_out, w_gate, w_up, w_down):
    tp_count = lax.axis_size("tp")
    ctx_count = lax.axis_size("ctx")
    local_rows = layer_in.shape[0]
    block_rows = local_rows * tp_count
    seq_rows = block_rows * ctx_count
    positions = lax.axis_index("ctx") * block_rows + jnp.arange(block_rows, dtype=jnp.int32)
    last_pos = positions[block_rows - 1]
    cosine, sine_table = rope_tables(positions, HEAD)
    score_scale = HEAD ** (-0.5)
    fetched = fetch_weights(w_query, w_key, w_value, w_out, w_gate, w_up, w_down)
    query_full, key_full, value_full, out_full, gate_full, up_full, down_full = fetched
    query_heads = query_full.shape[1] // HEAD
    key_heads = key_full.shape[1] // HEAD
    group_size = query_heads // key_heads
    input_float = layer_in.astype(jnp.float32)
    normed_one = rms_scale(input_float, norm_gains[0]).astype(jnp.bfloat16)
    rows_one = spread_rows(normed_one)
    query_proj = jnp.dot(rows_one, query_full, preferred_element_type=jnp.float32).reshape(
        block_rows, query_heads, HEAD
    )
    query_rot = (
        rotate(query_proj, cosine, sine_table, 1.0)
        .astype(jnp.bfloat16)
        .reshape(block_rows, key_heads, group_size, HEAD)
    )
    key_proj = jnp.dot(rows_one, key_full, preferred_element_type=jnp.float32).reshape(
        block_rows, key_heads, HEAD
    )
    key_rot = rotate(key_proj, cosine, sine_table, 1.0).astype(jnp.bfloat16)
    value_rows = (
        jnp.dot(rows_one, value_full, preferred_element_type=jnp.float32)
        .astype(jnp.bfloat16)
        .reshape(block_rows, key_heads, HEAD)
    )

    def scores_for(key_block):
        piece_len = key_block.shape[0]
        raw_scores = (
            jnp.einsum("bkgh,lkh->kgbl", query_rot, key_block, preferred_element_type=jnp.float32)
            * score_scale
        )
        capped = CAP * jnp.tanh(raw_scores / CAP)
        key_pos = jnp.arange(piece_len, dtype=jnp.int32)
        allowed = key_pos[None, :] <= positions[:, None]
        return (capped, allowed)

    accum_zero = jnp.zeros((block_rows, key_heads, group_size, HEAD), jnp.float32)
    totals_zero = jnp.zeros((key_heads, group_size, block_rows), jnp.float32)
    accumulated = accum_zero
    totals = totals_zero
    key_block = lax.all_gather(key_rot, "ctx", axis=0, tiled=True)
    value_block = lax.all_gather(value_rows, "ctx", axis=0, tiled=True)

    def attend_compute_piece():
        capped, allowed = scores_for(key_block)
        exp_scores = jnp.where(allowed, jnp.exp(capped), 0.0)
        weights = exp_scores.astype(jnp.bfloat16)
        summed = jnp.einsum(
            "kgbl,lkh->bkgh", weights, value_block, preferred_element_type=jnp.float32
        )
        return (summed, jnp.sum(exp_scores, axis=-1))

    def attend_keep_piece():
        return (accumulated, totals)

    accumulated, totals = lax.cond(
        jnp.int32(0) <= last_pos, attend_compute_piece, attend_keep_piece
    )
    head_rows = (accumulated / jnp.transpose(totals, (2, 0, 1))[..., None]).astype(jnp.bfloat16)
    log_totals = jnp.log(totals)
    head_flat = head_rows.reshape(block_rows, query_heads * HEAD)

    def attention_term(row_start, row_count):
        return jnp.dot(head_flat, out_full, preferred_element_type=jnp.float32)

    attention = collect_rows(attention_term, local_rows)
    middle = input_float + rms_scale(attention, norm_gains[1])
    normed_two = rms_scale(middle, norm_gains[2]).astype(jnp.bfloat16)
    rows_two = spread_rows(normed_two)
    gate_proj = jnp.dot(rows_two, gate_full, preferred_element_type=jnp.float32)
    up_proj = jnp.dot(rows_two, up_full, preferred_element_type=jnp.float32)
    hidden = glu_product(gate_proj, up_proj).astype(jnp.bfloat16)

    def branch_term(row_start, row_count):
        return jnp.dot(hidden, down_full, preferred_element_type=jnp.float32)

    branch_two = collect_rows(branch_term, local_rows)
    layer_out = (middle + rms_scale(branch_two, norm_gains[3])).astype(jnp.bfloat16)
    refetched = fetch_weights(w_query, w_key, w_value, w_out, w_gate, w_up, w_down)
    query_full, key_full, value_full, out_full, gate_full, up_full, down_full = refetched
    seed_rows = cotangent.astype(jnp.float32)
    unused_three, back_three = jax.vjp(rms_scale, branch_two, norm_gains[3])
    branch_delta, gain_three = back_three(seed_rows)
    branch_rows = spread_grads(branch_delta.astype(jnp.bfloat16))
    grad_down = inner_rows(hidden, branch_rows)
    hidden_delta = times_transposed(branch_rows, down_full)
    unused_glu, back_glu = jax.vjp(glu_product, gate_proj, up_proj)
    gate_delta, up_delta = back_glu(hidden_delta)
    gate_half = gate_delta.astype(jnp.bfloat16)
    up_half = up_delta.astype(jnp.bfloat16)
    grad_gate = inner_rows(rows_two, gate_half)
    grad_up = inner_rows(rows_two, up_half)

    def normed_two_term(row_start, row_count):
        first_term = times_transposed(gate_half, gate_full)
        return first_term + times_transposed(up_half, up_full)

    normed_delta_two = collect_rows(normed_two_term, local_rows)
    unused_two, back_two = jax.vjp(rms_scale, middle, norm_gains[2])
    middle_part_delta, gain_two = back_two(normed_delta_two)
    middle_delta = seed_rows + middle_part_delta
    unused_one, back_one = jax.vjp(rms_scale, attention, norm_gains[1])
    attention_delta, gain_one = back_one(middle_delta)
    attention_rows = spread_grads(attention_delta.astype(jnp.bfloat16))
    grad_out = inner_rows(head_flat, attention_rows)
    heads_delta = (
        times_transposed(attention_rows, out_full)
        .astype(jnp.bfloat16)
        .reshape(block_rows, key_heads, group_size, HEAD)
    )
    row_delta = jnp.einsum(
        "bkgh,bkgh->kgb", heads_delta, head_rows, preferred_element_type=jnp.float32
    )
    buffer_zero = jnp.zeros((seq_rows, key_heads, HEAD), jnp.float32)
    key_buffer = buffer_zero
    value_buffer = buffer_zero
    back_key_block = lax.all_gather(key_rot, "ctx", axis=0, tiled=True)
    back_value_block = lax.all_gather(value_rows, "ctx", axis=0, tiled=True)

    def back_compute_piece():
        capped, allowed = scores_for(back_key_block)
        prob_rows = jnp.where(allowed, jnp.exp(capped - log_totals[..., None]), 0.0)
        value_part = jnp.einsum(
            "kgbl,bkgh->lkh",
            prob_rows.astype(jnp.bfloat16),
            heads_delta,
            preferred_element_type=jnp.float32,
        )
        prob_delta = jnp.einsum(
            "bkgh,lkh->kgbl", heads_delta, back_value_block, preferred_element_type=jnp.float32
        )
        score_grad = prob_rows * (prob_delta - row_delta[..., None]) * (1.0 - (capped / CAP) ** 2)
        score_half = score_grad.astype(jnp.bfloat16)
        query_part = (
            jnp.einsum(
                "kgbl,lkh->bkgh", score_half, back_key_block, preferred_element_type=jnp.float32
            )
            * score_scale
        )
        key_part = (
            jnp.einsum("kgbl,bkgh->lkh", score_half, query_rot, preferred_element_type=jnp.float32)
            * score_scale
        )
        return (query_part, key_part, value_part)

    def back_keep_piece():
        return (accum_zero, key_buffer, value_buffer)

    query_grad, key_buffer, value_buffer = lax.cond(
        jnp.int32(0) <= last_pos, back_compute_piece, back_keep_piece
    )
    key_grad, value_grad = (
        lax.psum_scatter(
            key_buffer.astype(jnp.bfloat16), "ctx", scatter_dimension=0, tiled=True
        ).astype(jnp.float32),
        lax.psum_scatter(
            value_buffer.astype(jnp.bfloat16), "ctx", scatter_dimension=0, tiled=True
        ).astype(jnp.float32),
    )
    query_delta = (
        rotate(query_grad.reshape(block_rows, query_heads, HEAD), cosine, sine_table, -1.0)
        .astype(jnp.bfloat16)
        .reshape(block_rows, query_heads * HEAD)
    )
    key_delta = (
        rotate(key_grad, cosine, sine_table, -1.0)
        .astype(jnp.bfloat16)
        .reshape(block_rows, key_heads * HEAD)
    )
    value_delta = value_grad.astype(jnp.bfloat16).reshape(block_rows, key_heads * HEAD)
    grad_query = inner_rows(rows_one, query_delta)
    grad_key = inner_rows(rows_one, key_delta)
    grad_value = inner_rows(rows_one, value_delta)

    def normed_one_term(row_start, row_count):
        first_term = times_transposed(query_delta, query_full)
        second_term = times_transposed(key_delta, key_full)
        return first_term + second_term + times_transposed(value_delta, value_full)

    normed_delta_one = collect_rows(normed_one_term, local_rows)
    unused_zero, back_zero = jax.vjp(rms_scale, input_float, norm_gains[0])
    input_delta, gain_zero = back_zero(normed_delta_one)
    input_grad = middle_delta + input_delta
    gain_terms = jnp.stack([gain_zero, gain_one, gain_two, gain_three])
    gain_grads = lax.psum_scatter(gain_terms, ("dp", "ctx", "tp"), scatter_dimension=1, tiled=True)
    summed = (
        lax.psum_scatter(
            grad_query.astype(jnp.bfloat16), ("dp", "ctx"), scatter_dimension=0, tiled=True
        ).astype(jnp.float32),
        lax.psum_scatter(
            grad_key.astype(jnp.bfloat16), ("dp", "ctx"), scatter_dimension=0, tiled=True
        ).astype(jnp.float32),
        lax.psum_scatter(
            grad_value.astype(jnp.bfloat16), ("dp", "ctx"), scatter_dimension=0, tiled=True
        ).astype(jnp.float32),
        lax.psum_scatter(
            grad_out.astype(jnp.bfloat16), ("dp", "ctx"), scatter_dimension=1, tiled=True
        ).astype(jnp.float32),
        lax.psum_scatter(
            grad_gate.astype(jnp.bfloat16), ("dp", "ctx"), scatter_dimension=0, tiled=True
        ).astype(jnp.float32),
        lax.psum_scatter(
            grad_up.astype(jnp.bfloat16), ("dp", "ctx"), scatter_dimension=0, tiled=True
        ).astype(jnp.float32),
        lax.psum_scatter(
            grad_down.astype(jnp.bfloat16), ("dp", "ctx"), scatter_dimension=1, tiled=True
        ).astype(jnp.float32),
    )
    grad_query, grad_key, grad_value, grad_out, grad_gate, grad_up, grad_down = summed
    return (
        layer_out,
        input_grad,
        gain_grads,
        grad_query,
        grad_key,
        grad_value,
        grad_out,
        grad_gate,
        grad_up,
        grad_down,
    )


def solution(mesh):
    return jax.shard_map(
        shards,
        mesh=mesh,
        in_specs=(
            P(("dp", "ctx", "tp"), None),
            P(("dp", "ctx", "tp"), None),
            P(),
            P("dp", "tp"),
            P("dp", "tp"),
            P("dp", "tp"),
            P("tp", "dp"),
            P("dp", "tp"),
            P("dp", "tp"),
            P("tp", "dp"),
        ),
        out_specs=(
            P(("dp", "ctx", "tp"), None),
            P(("dp", "ctx", "tp"), None),
            P(None, ("dp", "ctx", "tp")),
            P(("dp", "ctx"), "tp"),
            P(("dp", "ctx"), "tp"),
            P(("dp", "ctx"), "tp"),
            P("tp", ("dp", "ctx")),
            P(("dp", "ctx"), "tp"),
            P(("dp", "ctx"), "tp"),
            P("tp", ("dp", "ctx")),
        ),
        check_vma=False,
    )
```

profile of v0, /device:TPU:0, one launch (start us, length us, event | category | flops | bytes accessed | tf_op | source)
XLA Modules:
  0.0 1176.5 jit_solution(1673402376015951335)
XLA Ops:
  13.8 7.7 all-gather.22.cloned.1.call-done
  21.5 53.3 %all-gather.16.cloned.1.call-done = bf16[512,2304]{1,0:T(8,128)(2,1)} async-done(((bf16[128,2304]{1,0:T(8,128)(2,1)}), bf16[512,2304]{1,0:T(8,128)(2,1)}) %all-gather.16.cloned.1.call-update) | async-done | bytes 2359312 | tf_op jit(solution)/shard_map/all_gather | solution.py:62
  74.9 3.5 convolution_convert_fusion.10
  80.2 4.2 all-gather.18.cloned.1.call-done
  84.4 2.8 fusion.110
  90.9 7.1 all-gather.20.cloned.1.call-done
  98.0 3.8 fusion.111
  108.5 19.4 %all-gather.40.cloned.1.call-done = bf16[2048,256]{1,0:T(8,128)(2,1)} async-done(((bf16[512,256]{1,0:T(8,128)(2,1)}), bf16[2048,256]{1,0:T(8,128)(2,1)}) %all-gather.40.cloned.1.call-update) | async-done | bytes 1048592 | tf_op jit(solution)/shard_map/all_gather | solution.py:130
  128.0 28.7 %all-gather.38.cloned.1.call-done = bf16[2048,256]{0,1:T(8,128)(2,1)} async-done(((bf16[512,256]{0,1:T(8,128)(2,1)}), bf16[2048,256]{0,1:T(8,128)(2,1)}) %all-gather.38.cloned.1.call-update) | async-done | bytes 1048592 | tf_op jit(solution)/shard_map/all_gather | solution.py:129
  156.6 10.3 conditional.2
  157.4 5.5 fusion
  163.0 2.9 fusion.6
  169.1 4.5 convolution_convert_fusion.6
  174.7 48.0 %reduce-scatter.15.cloned.1.call-done = bf16[128,2304]{1,0:T(8,128)(2,1)} async-done(((bf16[512,2304]{1,0:T(8,128)(2,1)}), bf16[128,2304]{1,0:T(8,128)(2,1)}) %reduce-scatter.15.cloned.1.call-update) | async-done | bytes 589840 | tf_op jit(solution)/shard_map/reduce_scatter | solution.py:70
  225.5 2.3 multiply_convert_fusion.2
  229.1 17.3 %all-gather.28.cloned.1.call-done = bf16[2304,2304]{1,0:T(8,128)(2,1)} async-done(((bf16[1152,2304]{1,0:T(8,128)(2,1)}), bf16[2304,2304]{1,0:T(8,128)(2,1)}) %all-gather.28.cloned.1.call-update) | async-done | bytes 10616848 | tf_op jit(solution)/shard_map/all_gather | solution.py:55
  246.4 53.2 %all-gather.26.cloned.1.call-done = bf16[512,2304]{1,0:T(8,128)(2,1)} async-done(((bf16[128,2304]{1,0:T(8,128)(2,1)}), bf16[512,2304]{1,0:T(8,128)(2,1)}) %all-gather.26.cloned.1.call-update) | async-done | bytes 2359312 | tf_op jit(solution)/shard_map/all_gather | solution.py:62
  299.6 11.8 %fusion.112 = f32[512,2304]{1,0:T(8,128)} fusion(bf16[512,2304]{1,0:T(8,128)(2,1)} %all-gather.26.cloned.1.call-done, bf16[2304,2304]{1,0:T(8,128)(2,1)} %all-gather.28.cloned.1.call-done), kind=kOutput, calls=%fused_computation.185 | convolution fusion | flops 5435817984 | bytes 17694720 | tf_op jit(solution)/shard_map/dot_general | solution.py:158
  311.4 11.4 all-gather.30.cloned.1.call-done
  322.8 13.0 %multiply_convert_fusion.1 = (bf16[512,2304]{1,0:T(8,128)(2,1)}, f32[512,2304]{1,0:T(8,128)}) fusion(f32[512,2304]{1,0:T(8,128)} %fusion.112, bf16[512,2304]{1,0:T(8,128)(2,1)S(1)} %copy-done.38, bf16[2304,2304]{1,0:T(8,128)(2,1)} %all-gather.30.cloned.1.call-done), kind=kOutput, calls=%fused_computation.64 | convolution fusion | flops 5447614464 | bytes 24772608 | tf_op jit(solution)/shard_map/dot_general | solution.py:159
  335.8 12.4 %all-gather.32.cloned.1.call-done = bf16[2304,2304]{1,0:T(8,128)(2,1)} async-done(((bf16[2304,1152]{1,0:T(8,128)(2,1)}), bf16[2304,2304]{1,0:T(8,128)(2,1)}) %all-gather.32.cloned.1.call-update) | async-done | bytes 10616848 | tf_op jit(solution)/shard_map/all_gather | solution.py:57
  348.1 11.2 convolution_convert_fusion.5
  359.4 49.0 %reduce-scatter.17.cloned.1.call-done = bf16[128,2304]{1,0:T(8,128)(2,1)} async-done(((bf16[512,2304]{1,0:T(8,128)(2,1)}), bf16[128,2304]{1,0:T(8,128)(2,1)}) %reduce-scatter.17.cloned.1.call-update) | async-done | bytes 589840 | tf_op jit(solution)/shard_map/reduce_scatter | solution.py:70
  409.7 2.3 fusion.80
  412.0 2.2 fusion.81
  414.7 49.1 %all-gather.34.cloned.1.call-done = bf16[512,2304]{1,0:T(8,128)(2,1)} async-done(((bf16[128,2304]{1,0:T(8,128)(2,1)}), bf16[512,2304]{1,0:T(8,128)(2,1)}) %all-gather.34.cloned.1.call-update) | async-done | bytes 2359312 | tf_op jit(solution)/shard_map/all_gather | solution.py:66
  463.8 14.3 %multiply_convert_fusion = (bf16[512,2304]{1,0:T(8,128)(2,1)S(1)}, bf16[512,2304]{1,0:T(8,128)(2,1)S(1)}) fusion(f32[512,2304]{1,0:T(8,128)} %fusion.112, f32[512,2304]{1,0:T(8,128)} %get-tuple-element.147, bf16[512,2304]{1,0:T(8,128)(2,1)} %all-gather.34.cloned.1.call-done, bf16[2304,2304]{1,0:T(8,128)(2,1)} %all-gather.32.cloned.1.call-done), kind=kOutput, calls=%fused_computation.63 | convolution fusion | flops 5464129536 | bytes 27131904 | tf_op jit(solution)/shard_map/dot_general | solution.py:44
  478.1 9.8 fusion.113
  488.0 10.9 fusion.64
  499.0 46.6 %reduce-scatter.19.cloned.1.call-done = bf16[128,2304]{1,0:T(8,128)(2,1)} async-done(((bf16[512,2304]{1,0:T(8,128)(2,1)}), bf16[128,2304]{1,0:T(8,128)(2,1)}) %reduce-scatter.19.cloned.1.call-update) | async-done | bytes 589840 | tf_op jit(solution)/shard_map/reduce_scatter | solution.py:70
  545.6 2.3 fusion.78
  547.9 3.7 fusion.76
  552.9 49.5 %all-gather.36.cloned.1.call-done = bf16[512,2304]{1,0:T(8,128)(2,1)} async-done(((bf16[128,2304]{1,0:T(8,128)(2,1)}), bf16[512,2304]{1,0:T(8,128)(2,1)}) %all-gather.36.cloned.1.call-update) | async-done | bytes 2359312 | tf_op jit(solution)/shard_map/all_gather | solution.py:66
  602.3 3.9 convolution_convert_fusion.9
  606.4 18.5 %conditional.3 = (bf16[2048,1,256]{2,0,1:T(8,128)(2,1)}, bf16[2048,1,256]{2,0,1:T(8,128)(2,1)}, f32[512,1,2,256]{0,3,2,1:T(8,128)S(1)}) conditional(s32[]{:T(128)} %bitcast.40, () %tuple.28, (s32[512]{0:T(512)S(1)}, bf16[2048,1,256]{0,2,1:T(8,128)(2,1)S(1)}, bf16[512,1,2,256]{3,0,2,1:T(8,128)(2,1)}, f32[1,2,512]{2,1,0:T(2,128)S(1)}, ...), branch_computations={%region_13.14_spmd, %region_14.15_spmd.clone} | conditional | flops 5403048960 | bytes 53495832 | solution.py:237
  607.7 2.4 fusion.48
  610.1 3.4 fusion.29
  613.5 4.3 fusion.16
  617.8 2.3 fusion.44
  620.1 3.3 fusion.38
  624.9 2.3 copy.66
  627.9 4.5 convolution_convert_fusion.3
  635.2 2.9 convolution_convert_fusion.4
  638.1 16.0 %reduce-scatter.21.cloned.1.call-done = bf16[512,1,256]{0,2,1:T(8,128)(2,1)} async-done(((bf16[2048,1,256]{0,2,1:T(8,128)(2,1)}), bf16[512,1,256]{0,2,1:T(8,128)(2,1)}) %reduce-scatter.21.cloned.1.call-update) | async-done | bytes 262160 | tf_op jit(solution)/shard_map/reduce_scatter | solution.py:241
  659.5 25.9 %reduce-scatter.23.cloned.1.call-done = bf16[512,1,256]{2,0,1:T(8,128)(2,1)} async-done(((bf16[2048,1,256]{2,0,1:T(8,128)(2,1)}), bf16[512,1,256]{2,0,1:T(8,128)(2,1)}) %reduce-scatter.23.cloned.1.call-update) | async-done | bytes 262160 | tf_op jit(solution)/shard_map/reduce_scatter | solution.py:244
  685.4 3.6 convolution_convert_fusion.7
  689.1 2.2 fusion.101
  692.8 2.2 fusion.63
  695.1 10.6 convolution_convert_fusion
  706.1 10.3 convolution_convert_fusion.1
  716.4 10.4 convolution_convert_fusion.2
  727.6 3.6 reduce-scatter.33.cloned.1.call-done
  733.0 44.3 %reduce-scatter.27.cloned.1.call-done = bf16[288,512]{1,0:T(8,128)(2,1)} async-done(((bf16[2304,512]{1,0:T(8,128)(2,1)}), bf16[288,512]{1,0:T(8,128)(2,1)}) %reduce-scatter.27.cloned.1.call-update) | async-done | bytes 294928 | tf_op jit(solution)/shard_map/reduce_scatter | solution.py:275
  779.1 38.7 %reduce-scatter.29.cloned.1.call-done = bf16[288,256]{1,0:T(8,128)(2,1)} async-done(((bf16[2304,256]{1,0:T(8,128)(2,1)}), bf16[288,256]{1,0:T(8,128)(2,1)}) %reduce-scatter.29.cloned.1.call-update) | async-done | bytes 147472 | tf_op jit(solution)/shard_map/reduce_scatter | solution.py:278
  819.4 38.3 %reduce-scatter.31.cloned.1.call-done = bf16[288,256]{1,0:T(8,128)(2,1)} async-done(((bf16[2304,256]{1,0:T(8,128)(2,1)}), bf16[288,256]{1,0:T(8,128)(2,1)}) %reduce-scatter.31.cloned.1.call-update) | async-done | bytes 147472 | tf_op jit(solution)/shard_map/reduce_scatter | solution.py:281
  859.4 49.0 %reduce-scatter.25.cloned.1.call-done = bf16[128,2304]{1,0:T(8,128)(2,1)} async-done(((bf16[512,2304]{1,0:T(8,128)(2,1)}), bf16[128,2304]{1,0:T(8,128)(2,1)}) %reduce-scatter.25.cloned.1.call-update) | async-done | bytes 589840 | tf_op jit(solution)/shard_map/reduce_scatter | solution.py:70
  910.1 40.4 %all-reduce = f32[4,2304]{1,0:T(4,128)S(1)} all-reduce(f32[4,2304]{1,0:T(4,128)S(1)} %pad_maximum_fusion.2), channel_id=10, replica_groups=mesh['dp'=2,'ctx'=4,'tp'=4] {'dp','ctx','tp'}, use_global_device_ids=true, to_apply=%region_23.24.clone | all-reduce | flops 9216 | bytes 73728
  951.3 2.4 fusion.83
  953.7 40.7 %reduce-scatter.39.cloned.1.call-done = bf16[2304,288]{0,1:T(8,128)(2,1)} async-done(((bf16[2304,2304]{0,1:T(8,128)(2,1)}), bf16[2304,288]{0,1:T(8,128)(2,1)}) %reduce-scatter.39.cloned.1.call-update) | async-done | bytes 1327120 | tf_op jit(solution)/shard_map/reduce_scatter | solution.py:293
  994.3 3.0 convert_element_type.207
  997.3 83.1 %reduce-scatter.37.cloned.1.call-done = bf16[288,2304]{1,0:T(8,128)(2,1)} async-done(((bf16[2304,2304]{1,0:T(8,128)(2,1)}), bf16[288,2304]{1,0:T(8,128)(2,1)}) %reduce-scatter.37.cloned.1.call-update) | async-done | bytes 1327120 | tf_op jit(solution)/shard_map/reduce_scatter | solution.py:290
  1080.5 3.0 convert_element_type.205
  1083.5 83.0 %reduce-scatter.35.cloned.1.call-done = bf16[288,2304]{1,0:T(8,128)(2,1)} async-done(((bf16[2304,2304]{1,0:T(8,128)(2,1)}), bf16[288,2304]{1,0:T(8,128)(2,1)}) %reduce-scatter.35.cloned.1.call-update) | async-done | bytes 1327120 | tf_op jit(solution)/shard_map/reduce_scatter | solution.py:287
  1166.5 3.0 convert_element_type.203
  (197 shorter events, 53.9 us)
Async XLA Ops:
  7.2 14.3 %all-gather.22.cloned.1.call-start = ((), (), s32[]{:S(2)}) async-start(), calls=%async_computation.16 | async-start | bytes 1769472 | tf_op jit(solution)/shard_map/all_gather | solution.py:53
  7.9 66.9 %all-gather.16.cloned.1.call-start = ((), (), s32[]{:S(2)}) async-start(), calls=%async_computation.13 | async-start | bytes 2949120 | tf_op jit(solution)/shard_map/all_gather | solution.py:62
  9.0 1.3 copy-start.16
  9.0 216.5 %copy-start.19 = (f32[2304]{0:T(1024)}, f32[2304]{0:T(1024)S(1)}, u32[]{:S(2)}) copy-start(f32[2304]{0:T(1024)S(1)} %get-tuple-element.124) | copy-start | bytes 27652
  9.0 403.0 %copy-start.18 = (f32[2304]{0:T(1024)}, f32[2304]{0:T(1024)S(1)}, u32[]{:S(2)}) copy-start(f32[2304]{0:T(1024)S(1)} %get-tuple-element.121) | copy-start | bytes 27652
  10.3 68.0 %copy-start.32 = (f32[128]{0:T(128)}, f32[128]{0:T(128)S(1)}, u32[]{:S(2)}) copy-start(f32[128]{0:T(128)S(1)} %fusion.88) | copy-start | bytes 1540
  10.3 68.0 %copy-start.26 = (f32[128]{0:T(128)}, f32[128]{0:T(128)S(1)}, u32[]{:S(2)}) copy-start(f32[128]{0:T(128)S(1)} %fusion.105) | copy-start | bytes 1540
  12.4 72.0 %all-gather.18.cloned.1.call-start = ((), (), s32[]{:S(2)}) async-start(), calls=%async_computation.14 | async-start | bytes 1769472 | tf_op jit(solution)/shard_map/all_gather | solution.py:52
  13.2 84.8 %all-gather.20.cloned.1.call-start = ((), (), s32[]{:S(2)}) async-start(), calls=%async_computation.15 | async-start | bytes 3538944 | tf_op jit(solution)/shard_map/all_gather | solution.py:51
  13.8 114.2 %all-gather.40.cloned.1.call-start = ((), (), s32[]{:S(2)}) async-start(), calls=%async_computation.38 | async-start | bytes 1310720 | tf_op jit(solution)/shard_map/all_gather | solution.py:130
  78.3 78.3 %all-gather.38.cloned.1.call-start = ((), (), s32[]{:S(2)}) async-start(), calls=%async_computation.37 | async-start | bytes 1310720 | tf_op jit(solution)/shard_map/all_gather | solution.py:129
  80.2 7.1 copy-start.8
  88.4 13.3 %copy-start.4 = (f32[512,256]{0,1:T(8,128)}, f32[512,256]{0,1:T(8,128)S(1)}, u32[]{:S(2)}) copy-start(f32[512,256]{0,1:T(8,128)S(1)} %get-tuple-element.141) | copy-start | bytes 1572868
  88.5 80.6 %all-gather.24.cloned.1.call-start = ((), (), s32[]{:S(2)}) async-start(), calls=%async_computation.17 | async-start | bytes 3538944 | tf_op jit(solution)/shard_map/all_gather | solution.py:54
  89.2 133.5 %reduce-scatter.15.cloned.1.call-start = ((), (), s32[]{:S(2)}) async-start(), calls=%async_computation.18 | async-start | bytes 2949120 | tf_op jit(solution)/shard_map/reduce_scatter | solution.py:70
  157.4 5.5 copy-start.40
  166.9 6.7 copy-start.30
  168.7 4.9 copy-start.13
  173.6 50.3 %copy-start = (bf16[128,2304]{1,0:T(8,128)(2,1)S(1)}, bf16[128,2304]{1,0:T(8,128)(2,1)}, u32[]{:S(2)}) copy-start(bf16[128,2304]{1,0:T(8,128)(2,1)} %param.14) | copy-start | bytes 1769476
  173.7 72.8 %all-gather.28.cloned.1.call-start = ((), (), s32[]{:S(2)}) async-start(), calls=%async_computation.20 | async-start | bytes 15925248 | tf_op jit(solution)/shard_map/all_gather | solution.py:55
  174.4 125.2 %all-gather.26.cloned.1.call-start = ((), (), s32[]{:S(2)}) async-start(), calls=%async_computation.19 | async-start | bytes 2949120 | tf_op jit(solution)/shard_map/all_gather | solution.py:62
  223.9 4.6 copy-start.34
  224.0 321.6 %copy-start.24 = (f32[128]{0:T(128)}, f32[128]{0:T(128)S(1)}, u32[]{:S(2)}) copy-start(f32[128]{0:T(128)S(1)} %fusion.106) | copy-start | bytes 1540
  225.5 320.1 %copy-start.29 = (f32[128]{0:T(128)}, f32[128]{0:T(128)S(1)}, u32[]{:S(2)}) copy-start(f32[128]{0:T(128)S(1)} %fusion.107) | copy-start | bytes 1540
  227.8 95.0 %all-gather.30.cloned.1.call-start = ((), (), s32[]{:S(2)}) async-start(), calls=%async_computation.21 | async-start | bytes 15925248 | tf_op jit(solution)/shard_map/all_gather | solution.py:56
  228.5 119.6 %all-gather.32.cloned.1.call-start = ((), (), s32[]{:S(2)}) async-start(), calls=%async_computation.22 | async-start | bytes 15925248 | tf_op jit(solution)/shard_map/all_gather | solution.py:57
  229.1 179.3 %reduce-scatter.17.cloned.1.call-start = ((), (), s32[]{:S(2)}) async-start(), calls=%async_computation.23 | async-start | bytes 2949120 | tf_op jit(solution)/shard_map/reduce_scatter | solution.py:70
  299.6 23.1 %copy-start.38 = (bf16[512,2304]{1,0:T(8,128)(2,1)S(1)}, bf16[512,2304]{1,0:T(8,128)(2,1)}, u32[]{:S(2)}) copy-start(bf16[512,2304]{1,0:T(8,128)(2,1)} %all-gather.26.cloned.1.call-done) | copy-start | bytes 7077892
  359.4 50.3 %copy-start.3 = (bf16[128,2304]{1,0:T(8,128)(2,1)S(1)}, bf16[128,2304]{1,0:T(8,128)(2,1)}, u32[]{:S(2)}) copy-start(bf16[128,2304]{1,0:T(8,128)(2,1)} %param.15) | copy-start | bytes 1769476
  359.4 104.4 %all-gather.34.cloned.1.call-start = ((), (), s32[]{:S(2)}) async-start(), calls=%async_computation.24 | async-start | bytes 2949120 | tf_op jit(solution)/shard_map/all_gather | solution.py:66
  409.7 68.4 %copy-start.28 = (f32[128]{0:T(128)}, f32[128]{0:T(128)S(1)}, u32[]{:S(2)}) copy-start(f32[128]{0:T(128)S(1)} %fusion.108) | copy-start | bytes 1540
  414.3 131.3 %reduce-scatter.19.cloned.1.call-start = ((), (), s32[]{:S(2)}) async-start(), calls=%async_computation.25 | async-start | bytes 2949120 | tf_op jit(solution)/shard_map/reduce_scatter | solution.py:70
  478.1 9.8 copy-start.41
  478.1 9.8 copy-start.42
  498.9 46.7 %copy-start.1 = (bf16[128,2304]{1,0:T(8,128)(2,1)S(1)}, bf16[128,2304]{1,0:T(8,128)(2,1)}, u32[]{:S(2)}) copy-start(bf16[128,2304]{1,0:T(8,128)(2,1)} %reduce-scatter.15.cloned.1.call-done) | copy-start | bytes 1769476
  498.9 46.7 %copy-start.20 = (f32[2304]{0:T(1024)S(1)}, f32[2304]{0:T(1024)}, u32[]{:S(2)}) copy-start(f32[2304]{0:T(1024)} %copy-done.19) | copy-start | bytes 27652
  498.9 49.0 %copy-start.2 = (bf16[128,2304]{1,0:T(8,128)(2,1)S(1)}, bf16[128,2304]{1,0:T(8,128)(2,1)}, u32[]{:S(2)}) copy-start(bf16[128,2304]{1,0:T(8,128)(2,1)} %reduce-scatter.17.cloned.1.call-done) | copy-start | bytes 1769476
  499.0 103.4 %all-gather.36.cloned.1.call-start = ((), (), s32[]{:S(2)}) async-start(), calls=%async_computation.26 | async-start | bytes 2949120 | tf_op jit(solution)/shard_map/all_gather | solution.py:66
  547.9 3.7 copy-start.35
  547.9 3.7 copy-start.25
  552.8 101.3 %reduce-scatter.21.cloned.1.call-start = ((), (), s32[]{:S(2)}) async-start(), calls=%async_computation.27 | async-start | bytes 1310720 | tf_op jit(solution)/shard_map/reduce_scatter | solution.py:241
  552.9 53.5 %copy-start.31 = (f32[1,2,512]{2,1,0:T(2,128)S(1)}, f32[1,2,512]{2,1,0:T(2,128)}, u32[]{:S(2)}) copy-start(f32[1,2,512]{2,1,0:T(2,128)} %copy-done.30) | copy-start | bytes 12292
  602.3 4.1 copy-start.6
  602.3 4.1 copy-start.12
  602.3 4.1 copy-start.39
  624.9 3.0 copy-start.14
  627.3 58.1 %reduce-scatter.23.cloned.1.call-start = ((), (), s32[]{:S(2)}) async-start(), calls=%async_computation.28 | async-start | bytes 1310720 | tf_op jit(solution)/shard_map/reduce_scatter | solution.py:244
  627.9 103.2 %reduce-scatter.33.cloned.1.call-start = ((), (), s32[]{:S(2)}) async-start(), calls=%async_computation.33 | async-start | bytes 2654208 | tf_op jit(solution)/shard_map/reduce_scatter | solution.py:284
  632.4 144.8 %reduce-scatter.27.cloned.1.call-start = ((), (), s32[]{:S(2)}) async-start(), calls=%async_computation.30 | async-start | bytes 2654208 | tf_op jit(solution)/shard_map/reduce_scatter | solution.py:275
  633.5 1.7 copy-start.36
  638.1 18.2 %copy-start.9 = (f32[512,128]{0,1:T(8,128)S(1)}, f32[512,128]{0,1:T(8,128)}, u32[]{:S(2)}) copy-start(f32[512,128]{0,1:T(8,128)} %copy-done.8) | copy-start | bytes 786436
  638.1 179.7 %reduce-scatter.29.cloned.1.call-start = ((), (), s32[]{:S(2)}) async-start(), calls=%async_computation.31 | async-start | bytes 1327104 | tf_op jit(solution)/shard_map/reduce_scatter | solution.py:278
  654.1 3.5 copy-start.37
  659.5 198.2 %reduce-scatter.31.cloned.1.call-start = ((), (), s32[]{:S(2)}) async-start(), calls=%async_computation.32 | async-start | bytes 1327104 | tf_op jit(solution)/shard_map/reduce_scatter | solution.py:281
  689.0 219.3 %reduce-scatter.25.cloned.1.call-start = ((), (), s32[]{:S(2)}) async-start(), calls=%async_computation.29 | async-start | bytes 2949120 | tf_op jit(solution)/shard_map/reduce_scatter | solution.py:70
  689.1 2.3 copy-start.7
  691.3 1.5 copy-start.11
  691.3 1.5 copy-start.15
  695.1 299.3 %reduce-scatter.39.cloned.1.call-start = ((), (), s32[]{:S(2)}) async-start(), calls=%async_computation.36 | async-start | bytes 11943936 | tf_op jit(solution)/shard_map/reduce_scatter | solution.py:293
  705.8 374.7 %reduce-scatter.37.cloned.1.call-start = ((), (), s32[]{:S(2)}) async-start(), calls=%async_computation.35 | async-start | bytes 11943936 | tf_op jit(solution)/shard_map/reduce_scatter | solution.py:290
  716.4 450.1 %reduce-scatter.35.cloned.1.call-start = ((), (), s32[]{:S(2)}) async-start(), calls=%async_computation.34 | async-start | bytes 11943936 | tf_op jit(solution)/shard_map/reduce_scatter | solution.py:287
  726.8 181.5 %copy-start.17 = (f32[2304]{0:T(1024)S(1)}, f32[2304]{0:T(1024)}, u32[]{:S(2)}) copy-start(f32[2304]{0:T(1024)} %copy-done.16) | copy-start | bytes 27652
  726.8 181.5 %copy-start.27 = (f32[128]{0:T(128)S(1)}, f32[128]{0:T(128)}, u32[]{:S(2)}) copy-start(f32[128]{0:T(128)} %copy-done.26) | copy-start | bytes 1540
  726.9 224.4 %copy-start.33 = (f32[128]{0:T(128)S(1)}, f32[128]{0:T(128)}, u32[]{:S(2)}) copy-start(f32[128]{0:T(128)} %copy-done.32) | copy-start | bytes 1540
  (5 other events, 4.3 us)
Sparse Core Ops, SparseCore 0:
  9.5 11.9 all-gather.21
  23.7 51.1 all-gather.15
  76.4 7.9 all-gather.17
  85.8 12.1 all-gather.19
  100.3 27.6 all-gather.39
  130.2 26.3 all-gather.37
  158.2 10.9 all-gather.23
  173.8 48.8 reduce-scatter.14
  224.2 22.1 all-gather.27
  248.4 51.1 all-gather.25
  301.2 21.5 all-gather.29
  324.2 23.9 all-gather.31
  359.5 48.8 reduce-scatter.16
  414.4 49.3 all-gather.33
  499.1 46.4 reduce-scatter.18
  552.9 49.3 all-gather.35
  627.4 26.6 reduce-scatter.20
  657.5 27.9 reduce-scatter.22
  688.8 42.3 reduce-scatter.32
  734.9 42.3 reduce-scatter.26
  781.1 36.6 reduce-scatter.28
  821.0 36.6 reduce-scatter.30
  860.6 47.6 reduce-scatter.24
  911.7 82.5 reduce-scatter.38
  997.9 82.5 reduce-scatter.36
  1083.9 82.5 reduce-scatter.34
where the time goes:
time: 1190 us; the launch traced here: 1180 us
  waiting for transfers between devices  885 us (74%)
  matrix products  164 us (14%)
  other arithmetic  53.4 us (4%)
  blocking collectives  40.4 us (3%)
  local copies, waits for them, and re-layouts  16 us (1%)
  between operations  15.8 us (1%)
    reduce_scatter x4, waiting for transfers between devices, collect_rows(): lax.psum_scatter(term_fn(jnp.int32(0), row_total * lax.axis_size('tp')).a...  193 us
    all_gather x2, waiting for transfers between devices, spread_rows(): return lax.all_gather(rows_part, 'tp', axis=0, tiled=True)  107 us
    all_gather x2, waiting for transfers between devices, spread_grads(): return lax.all_gather(rows_part, 'tp', axis=0, tiled=True)  98.5 us
    reduce_scatter x1, waiting for transfers between devices, shards(): lax.psum_scatter(grad_up.astype(jnp.bfloat16), ('dp', 'ctx'), scatter_dim...  83.1 us
    reduce_scatter x1, waiting for transfers between devices, shards(): lax.psum_scatter(grad_gate.astype(jnp.bfloat16), ('dp', 'ctx'), scatter_d...  83 us
    dot_general x7, matrix products, times_transposed(): lax.dot_general(former, latter, (((1,), (1,)), ((), ())), preferred_eleme...  44.9 us
    reduce_scatter x1, waiting for transfers between devices, shards(): lax.psum_scatter(grad_query.astype(jnp.bfloat16), ('dp', 'ctx'), scatter_...  44.3 us
    dot_general x7, matrix products, inner_rows(): lax.dot_general(former, latter, (((0,), (0,)), ((), ())), preferred_eleme...  44.1 us
  transfers between devices with their start and end apart: 26, of which 26 were waited for; matrix products, arithmetic and copies ran while one was open for 12% of the time, Pallas kernels for 0%

commit v1 on v0

--- a/solution.py
+++ b/solution.py
@@ -1,22 +1,476 @@
+import functools
+
 import jax
 import jax.numpy as jnp
 from jax import lax
+from jax.experimental import pallas as pl
+from jax.experimental.pallas import tpu as pltpu
 from jax.sharding import PartitionSpec as P
 
 HEAD = 256
-
-
 EPS = 1e-06
 CAP = 50.0
 THETA = 10000.0
+MESH = pl.DeviceIdType.MESH
+BF = jnp.bfloat16
+F32 = jnp.float32
+
+
+def tile_of(width):
+    for tile in (768, 512, 256, 128):
+        if width % tile == 0:
+            return tile
+    return width
+
+
+def inverse_rms(values):
+    return lax.rsqrt(jnp.mean(values * values, axis=-1, keepdims=True) + EPS)
+
+
+def rms_back(values, scale, gain, delta):
+    weighted = delta * gain
+    inner = jnp.mean(weighted * values, axis=-1, keepdims=True)
+    grad = scale * weighted - values * (scale * scale * scale * inner)
+    return grad, jnp.sum(delta * values * scale, axis=0, keepdims=True)
+
+
+def dot_nt(former, latter):
+    return lax.dot_general(former, latter, (((1,), (1,)), ((), ())), preferred_element_type=F32)
+
+
+def dot_nn(former, latter):
+    return jnp.dot(former, latter, preferred_element_type=F32)
+
+
+def barrier(count_of, peers):
+    sem = pltpu.get_barrier_semaphore()
+    for present, device_id in peers:
+
+        @pl.when(present)
+        def _():
+            pl.semaphore_signal(sem, inc=1, device_id=device_id, device_id_type=MESH)
+
+    pl.semaphore_wait(sem, count_of)
+
+
+def core_kernel(
+    T, C, NDP,
+    x_ref, ct_ref, gain_ref, heads_ref, wo_ref, wg_ref, wu_ref, wd_ref,
+    out_ref, mdelta_ref, gsum_ref, hdelta_ref,
+    rows_pair, hid_pair, branch_pair, gate_pair, up_pair, attn_pair, head_pair,
+    wo_v, wg_v, wu_v, wd_v, X, Pb, Rb, hid, Ab, Bb, att, mid, acc,
+    w_sem, rs_send, rs_recv, ag_send, ag_recv, pair_sem,
+):
+    t = lax.axis_index("tp")
+    dp = lax.axis_index("dp")
+    D = x_ref.shape[1]
+    rc = x_ref.shape[0] // C
+    Dh = D // NDP
+    F = wg_v.shape[1]
+    M = T * rc
+    has_left, has_right = t > 0, t < T - 1
+    left, right = {"tp": jnp.maximum(t - 1, 0)}, {"tp": jnp.minimum(t + 1, T - 1)}
+    partners = [{"dp": lax.rem(dp + o, NDP)} for o in range(1, NDP)]
+
+    barrier(
+        has_left.astype(jnp.int32) + has_right.astype(jnp.int32) + (NDP - 1),
+        [(has_left, left), (has_right, right)] + [(t >= 0, p) for p in partners],
+    )
+
+    rows_at = pl.ds(pl.multiple_of(dp * Dh, 128), Dh)
+    weights = [
+        (wo_ref, lambda: wo_v.at[:, rows_at]),
+        (wg_ref, lambda: wg_v.at[rows_at]),
+        (wu_ref, lambda: wu_v.at[rows_at]),
+        (wd_ref, lambda: wd_v.at[:, rows_at]),
+    ]
+
+    def weight_copies(i):
+        src, dst = weights[i]
+        copies = [pltpu.make_async_copy(src, dst(), w_sem.at[0, i])]
+        for o, partner in enumerate(partners):
+            copies.append(
+                pltpu.make_async_remote_copy(
+                    src, dst(), w_sem.at[1 + 2 * o, i], w_sem.at[2 + 2 * o, i],
+                    device_id=partner, device_id_type=MESH,
+                )
+            )
+        return copies
+
+    for i in range(4):
+        for copy in weight_copies(i):
+            copy.start()
+
+    def weight_wait(i):
+        src, dst = weights[i]
+        for o, copy in enumerate(weight_copies(i)):
+            if o == 0:
+                copy.wait()
+            else:
+                copy.wait_recv()
+
+    def pair_copies(kind, s, src, half, dst):
+        def cut(owner):
+            if half:
+                return src.at[..., pl.ds(pl.multiple_of(owner * Dh, 128), Dh)]
+            return src
+
+        copies = [pltpu.make_async_copy(cut(dp), dst.at[dp, s], pair_sem.at[0, kind, s])]
+        for o, partner in enumerate(partners):
+            copies.append(
+                pltpu.make_async_remote_copy(
+                    cut(partner["dp"]), dst.at[dp, s],
+                    pair_sem.at[1 + 2 * o, kind, s], pair_sem.at[2 + 2 * o, kind, s],
+                    device_id=partner, device_id_type=MESH,
+                )
+            )
+        return copies
+
+    def pair_of(kind, s):
+        return pair_copies(
+            kind, s,
+            *[
+                (X.at[s], True, rows_pair),
+                (hid.at[s], False, hid_pair),
+                (X.at[s], True, branch_pair),
+                (Ab.at[s], False, gate_pair),
+                (Bb.at[s], False, up_pair),
+                (X.at[s], True, attn_pair),
+                (heads_ref.at[:, s], False, head_pair),
+            ][kind],
+        )
+
+    def pair_start(kind, s):
+        for copy in pair_of(kind, s):
+            copy.start()
+
+    def pair_sent(kind, s):
+        for o, copy in enumerate(pair_of(kind, s)):
+            if o == 0:
+                copy.wait()
+            else:
+                copy.wait_send()
+
+    def pair_received(kind, s):
+        for copy in pair_of(kind, s)[1:]:
+            copy.wait_recv()
+
+    def rs_copy(s, side, k, j):
+        if side == 0:
+            slot, peer = j, right
+        else:
+            slot, peer = jnp.where(j == t - 1, T, j), left
+        return pltpu.make_async_remote_copy(
+            Pb.at[s, j], Rb.at[s, slot], rs_send.at[s, side, k], rs_recv.at[s, side, k],
+            device_id=peer, device_id_type=MESH,
+        )
+
+    def rs_block(side, k):
+        return (T - 1 - k + t) if side == 0 else (k - (T - 1 - t))
+
+    def rs_sends(side, k):
+        return (t <= k) if side == 0 else (T - 1 - t <= k)
+
+    def ag_copy(s, side, k, j):
+        return pltpu.make_async_remote_copy(
+            X.at[s, j], X.at[s, j], ag_send.at[s, side, k], ag_recv.at[s, side, k],
+            device_id=right if side == 0 else left, device_id_type=MESH,
+        )
+
+    def ag_block(side, k):
+        return (t - k) if side == 0 else (t + k)
+
+    def ag_sends(side, k):
+        return (t >= k) & has_right if side == 0 else (t + k <= T - 1) & has_left
+
+    def rs_start(s):
+        for side in (0, 1):
+
+            @pl.when(rs_sends(side, 0))
+            def _():
+                rs_copy(s, side, 0, rs_block(side, 0)).start()
+
+    def rs_step(s, k):
+        for side in (0, 1):
+            j = rs_block(side, k)
+            came = has_left if side == 0 else has_right
+
+            @pl.when(rs_sends(side, k))
+            def _():
+                @pl.when(came)
+                def _():
+                    rs_copy(s, side, k - 1, j).wait_recv()
+                    Pb[s, j] = (Pb[s, j].astype(F32) + Rb[s, j].astype(F32)).astype(BF)
+
+                rs_copy(s, side, k, j).start()
+
+    def rs_sent(s):
+        for side in (0, 1):
+            for k in range(T - 1):
+
+                @pl.when(rs_sends(side, k))
+                def _():
+                    rs_copy(s, side, k, rs_block(side, k)).wait_send()
+
+    def rs_finish(s):
+        acc[...] = Pb[s, t].astype(F32)
+
+        @pl.when(has_left)
+        def _():
+            rs_copy(s, 0, T - 2, t).wait_recv()
+            acc[...] += Rb[s, t].astype(F32)
+
+        @pl.when(has_right)
+        def _():
+            rs_copy(s, 1, T - 2, t).wait_recv()
+            acc[...] += Rb[s, T].astype(F32)
+
+    def ag_start(s):
+        for side in (0, 1):
+
+            @pl.when(ag_sends(side, 0))
+            def _():
+                ag_copy(s, side, 0, t).start()
+
+    def ag_step(s, k):
+        for side in (0, 1):
+            j = ag_block(side, k)
+            there = (j >= 0) if side == 0 else (j <= T - 1)
+
+            @pl.when(there)
+            def _():
+                ag_copy(s, side, k - 1, j).wait_recv()
+                if k <= T - 2:
+
+                    @pl.when(has_right if side == 0 else has_left)
+                    def _():
+                        ag_copy(s, side, k, j).start()
+
+    def ag_sent(s):
+        for side in (0, 1):
+            for k in range(T - 1):
+
+                @pl.when(ag_sends(side, k))
+                def _():
+                    ag_copy(s, side, k, ag_block(side, k)).wait_send()
+
+    def local_rows(n, s):
+        own = pl.ds(pl.multiple_of(s * rc, rc), rc)
+        total = acc[...]
+
+        @pl.when(n == 0)
+        def _():
+            att[s] = total
+            middle = x_ref[own].astype(F32) + total * inverse_rms(total) * gain_ref[1:2]
+            mid[s] = middle
+            X[s, t] = (middle * inverse_rms(middle) * gain_ref[2:3]).astype(BF)
+
+        @pl.when(n == 1)
+        def _():
+            scale = inverse_rms(total)
+            out_ref[own] = (mid[s] + total * scale * gain_ref[3:4]).astype(BF)
+            grad, terms = rms_back(total, scale, gain_ref[3:4], ct_ref[own].astype(F32))
+            gsum_ref[2:3] += terms
+            X[s, t] = grad.astype(BF)
+
+        @pl.when(n == 2)
+        def _():
+            middle, attention = mid[s], att[s]
+            grad, terms = rms_back(middle, inverse_rms(middle), gain_ref[2:3], total)
+            gsum_ref[1:2] += terms
+            middle_delta = ct_ref[own].astype(F32) + grad
+            mdelta_ref[own] = middle_delta
+            grad, terms = rms_back(attention, inverse_rms(attention), gain_ref[1:2], middle_delta)
+            gsum_ref[0:1] += terms
+            X[s, t] = grad.astype(BF)
+
+    def comm(tau, w, a):
+        back = tau - a
+
+        @pl.when((back >= 0) & (back < 3 * C))
+        def _():
+            n, s = back // C, lax.rem(back, C)
+            if w <= T - 2:
+                rs_step(s, w)
+            elif w == T - 1:
+                rs_finish(s)
+                local_rows(n, s)
+                ag_start(s)
+            else:
+                ag_step(s, w - (T - 1))
+
+    def tiles(width, body):
+        tile = tile_of(width)
+
+        def step(i, carry):
+            body(pl.ds(pl.multiple_of(i * tile, tile), tile), tile)
+            return carry
+
+        lax.fori_loop(0, width // tile, step, 0)
+
+    def rows_of(s):
+        return X[s].reshape(M, D)
+
+    def store_part(s, at, tile, value):
+        Pb[s, :, :, at] = value.astype(BF).reshape(T, rc, tile)
+
+    def tick(tau, carry):
+        n, s = tau // C, lax.rem(tau, C)
+
+        @pl.when((n >= 1) & (n <= 2))
+        def _():
+            rs_sent(s)
+
+        @pl.when(n == 1)
+        def _():
+            @pl.when(s == 0)
+            def _():
+                weight_wait(1)
+                weight_wait(2)
+
+            pair_start(0, s)
+
+            def gate_up(at, tile):
+                gate = dot_nn(rows_of(s), wg_v[:, at])
+                up = dot_nn(rows_of(s), wu_v[:, at])
+                inner = jnp.tanh(0.7978845608028654 * (gate + 0.044715 * gate * gate * gate))
+                half = 0.5 * (1.0 + inner)
+                gelu = gate * half
+                slope = half + 0.5 * gate * (1.0 - inner * inner) * (
+                    0.7978845608028654 * (1.0 + 0.134145 * gate * gate)
+                )
+                hid[s, :, at] = (gelu * up).astype(BF)
+                Ab[s, :, at] = (up * slope).astype(BF)
+                Bb[s, :, at] = gelu.astype(BF)
+
+            tiles(F, gate_up)
+            pair_start(1, s)
+
+        @pl.when(n == 2)
+        def _():
+            pair_start(2, s)
+
+            def gate_up_delta(at, tile):
+                delta = dot_nt(rows_of(s), wd_v[at, :])
+                Ab[s, :, at] = (delta * Ab[s, :, at].astype(F32)).astype(BF)
+                Bb[s, :, at] = (delta * Bb[s, :, at].astype(F32)).astype(BF)
+
+            tiles(F, gate_up_delta)
+            pair_start(3, s)
+            pair_start(4, s)
+
+        for a in range(1, T):
+            comm(tau, 2 * a - 1, a)
+
+        @pl.when(n == 0)
+        def _():
+            pair_start(6, s)
+            heads = heads_ref[:, s].reshape(M, heads_ref.shape[3])
+            tiles(D, lambda at, tile: store_part(s, at, tile, dot_nn(heads, wo_v[:, at])))
+
+        @pl.when(n == 1)
+        def _():
+            @pl.when(s == 0)
+            def _():
+                weight_wait(3)
+
+            tiles(D, lambda at, tile: store_part(s, at, tile, dot_nn(hid[s], wd_v[:, at])))
+            pair_sent(0, s)
+            ag_sent(s)
+
+        @pl.when(n == 2)
+        def _():
+            tiles(
+                D,
+                lambda at, tile: store_part(
+                    s, at, tile, dot_nt(Ab[s], wg_v[at, :]) + dot_nt(Bb[s], wu_v[at, :])
+                ),
+            )
+            pair_sent(2, s)
+            ag_sent(s)
+
+        @pl.when(n <= 2)
+        def _():
+            rs_start(s)
+
+        @pl.when(n == 3)
+        def _():
+            pair_start(5, s)
+            hdelta_ref[:, s] = (
+                dot_nt(rows_of(s), wo_v[...]).astype(BF).reshape(T, rc, heads_ref.shape[3])
+            )
+
+        for a in range(1, T):
+            comm(tau, 2 * a, a)
+        return carry
+
+    gsum_ref[...] = jnp.zeros_like(gsum_ref)
+    weight_wait(0)
+    lax.fori_loop(0, 4 * C, tick, 0)
+
+    for i in range(4):
+        for copy in weight_copies(i)[1:]:
+            copy.wait_send()
+
+    def close(s, carry):
+        for kind in (1, 3, 4, 5, 6):
+            pair_sent(kind, s)
+        for kind in range(7):
+            pair_received(kind, s)
+        rs_sent(s)
+        ag_sent(s)
+        return carry
+
+    lax.fori_loop(0, C, close, 0)
+
+
+def core_call(layer_in, cotangent, norm_gains, head_flat, w_out, w_gate, w_up, w_down):
+    T, NDP = lax.axis_size("tp"), lax.axis_size("dp")
+    C = T
+    Lr, D = layer_in.shape
+    rc = Lr // C
+    Hq = w_out.shape[0]
+    Dh = D // NDP
+    F = w_gate.shape[1]
+    M = T * rc
+    any_spec = pl.BlockSpec(memory_space=pl.ANY)
+    vm = pl.BlockSpec(memory_space=pltpu.VMEM)
+    sds = jax.ShapeDtypeStruct
+    outs = pl.pallas_call(
+        functools.partial(core_kernel, T, C, NDP),
+        out_shape=(
+            sds((Lr, D), BF), sds((Lr, D), F32), sds((3, D), F32), sds((T, C, rc, Hq), BF),
+            sds((NDP, C, T, rc, Dh), BF), sds((NDP, C, M, F), BF), sds((NDP, C, T, rc, Dh), BF),
+            sds((NDP, C, M, F), BF), sds((NDP, C, M, F), BF), sds((NDP, C, T, rc, Dh), BF),
+            sds((NDP, C, T, rc, Hq), BF),
+        ),
+        in_specs=[vm, vm, vm, vm] + [any_spec] * 4,
+        out_specs=[vm, vm, vm, vm] + [any_spec] * 7,
+        scratch_shapes=[
+            pltpu.VMEM((Hq, D), BF), pltpu.VMEM((D, F), BF), pltpu.VMEM((D, F), BF), pltpu.VMEM((F, D), BF),
+            pltpu.VMEM((C, T, rc, D), BF), pltpu.VMEM((C, T, rc, D), BF), pltpu.VMEM((C, T + 1, rc, D), BF),
+            pltpu.VMEM((C, M, F), BF), pltpu.VMEM((C, M, F), BF), pltpu.VMEM((C, M, F), BF),
+            pltpu.VMEM((C, rc, D), F32), pltpu.VMEM((C, rc, D), F32), pltpu.VMEM((rc, D), F32),
+            pltpu.SemaphoreType.DMA((2 * NDP - 1, 4)),
+            pltpu.SemaphoreType.DMA((C, 2, T - 1)), pltpu.SemaphoreType.DMA((C, 2, T - 1)),
+            pltpu.SemaphoreType.DMA((C, 2, T - 1)), pltpu.SemaphoreType.DMA((C, 2, T - 1)),
+            pltpu.SemaphoreType.DMA((2 * NDP - 1, 7, C)),
+        ],
+        compiler_params=pltpu.CompilerParams(
+            collective_id=0, has_side_effects=True, vmem_limit_bytes=66_000_000
+        ),
+        name="core",
+    )(layer_in, cotangent, norm_gains, head_flat.reshape(T, C, rc, Hq), w_out, w_gate, w_up, w_down)
+    out, mdelta, gsum, hdelta, rows, hidden, branch, gate, up, attn, heads = outs
+    flat = lambda a: a.reshape(NDP * T * Lr, a.shape[-1])
+    return (
+        out, mdelta, gsum, hdelta.reshape(T * Lr, Hq),
+        flat(rows), flat(hidden), flat(branch), flat(gate), flat(up), flat(attn), flat(heads),
+    )
 
 
 def rms_scale(values, gain_row):
     return values * lax.rsqrt(jnp.mean(values * values, axis=-1, keepdims=True) + EPS) * gain_row
-
-
-def glu_product(gate_proj, up_proj):
-    return jax.nn.gelu(gate_proj, approximate=True) * up_proj
 
 
 def rope_tables(positions, head_width):
@@ -46,23 +500,15 @@
     )
 
 
-def fetch_weights(query_part, key_part, value_part, out_part, gate_part, up_part, down_part):
+def fetch_weights(query_part, key_part, value_part):
     return (
         lax.all_gather(query_part, "dp", axis=0, tiled=True),
         lax.all_gather(key_part, "dp", axis=0, tiled=True),
         lax.all_gather(value_part, "dp", axis=0, tiled=True),
-        lax.all_gather(out_part, "dp", axis=1, tiled=True),
-        lax.all_gather(gate_part, "dp", axis=0, tiled=True),
-        lax.all_gather(up_part, "dp", axis=0, tiled=True),
-        lax.all_gather(down_part, "dp", axis=1, tiled=True),
     )
 
 
 def spread_rows(rows_part):
-    return lax.all_gather(rows_part, "tp", axis=0, tiled=True)
-
-
-def spread_grads(rows_part):
     return lax.all_gather(rows_part, "tp", axis=0, tiled=True)
 
 
@@ -73,6 +519,10 @@
         scatter_dimension=0,
         tiled=True,
     ).astype(jnp.float32)
+
+
+def over_ctx(terms, dim):
+    return lax.psum_scatter(terms.astype(BF), "ctx", scatter_dimension=dim, tiled=True).astype(F32)
 
 
 def shards(layer_in, cotangent, norm_gains, w_query, w_key, w_value, w_out, w_gate, w_up, w_down):
@@ -85,8 +535,7 @@
     last_pos = positions[block_rows - 1]
     cosine, sine_table = rope_tables(positions, HEAD)
     score_scale = HEAD ** (-0.5)
-    fetched = fetch_weights(w_query, w_key, w_value, w_out, w_gate, w_up, w_down)
-    query_full, key_full, value_full, out_full, gate_full, up_full, down_full = fetched
+    query_full, key_full, value_full = fetch_weights(w_query, w_key, w_value)
     query_heads = query_full.shape[1] // HEAD
     key_heads = key_full.shape[1] // HEAD
     group_size = query_heads // key_heads
@@ -148,54 +597,10 @@
     log_totals = jnp.log(totals)
     head_flat = head_rows.reshape(block_rows, query_heads * HEAD)
 
-    def attention_term(row_start, row_count):
-        return jnp.dot(head_flat, out_full, preferred_element_type=jnp.float32)
-
-    attention = collect_rows(attention_term, local_rows)
-    middle = input_float + rms_scale(attention, norm_gains[1])
-    normed_two = rms_scale(middle, norm_gains[2]).astype(jnp.bfloat16)
-    rows_two = spread_rows(normed_two)
-    gate_proj = jnp.dot(rows_two, gate_full, preferred_element_type=jnp.float32)
-    up_proj = jnp.dot(rows_two, up_full, preferred_element_type=jnp.float32)
-    hidden = glu_product(gate_proj, up_proj).astype(jnp.bfloat16)
-
-    def branch_term(row_start, row_count):
-        return jnp.dot(hidden, down_full, preferred_element_type=jnp.float32)
-
-    branch_two = collect_rows(branch_term, local_rows)
-    layer_out = (middle + rms_scale(branch_two, norm_gains[3])).astype(jnp.bfloat16)
-    refetched = fetch_weights(w_query, w_key, w_value, w_out, w_gate, w_up, w_down)
-    query_full, key_full, value_full, out_full, gate_full, up_full, down_full = refetched
-    seed_rows = cotangent.astype(jnp.float32)
-    unused_three, back_three = jax.vjp(rms_scale, branch_two, norm_gains[3])
-    branch_delta, gain_three = back_three(seed_rows)
-    branch_rows = spread_grads(branch_delta.astype(jnp.bfloat16))
-    grad_down = inner_rows(hidden, branch_rows)
-    hidden_delta = times_transposed(branch_rows, down_full)
-    unused_glu, back_glu = jax.vjp(glu_product, gate_proj, up_proj)
-    gate_delta, up_delta = back_glu(hidden_delta)
-    gate_half = gate_delta.astype(jnp.bfloat16)
-    up_half = up_delta.astype(jnp.bfloat16)
-    grad_gate = inner_rows(rows_two, gate_half)
-    grad_up = inner_rows(rows_two, up_half)
-
-    def normed_two_term(row_start, row_count):
-        first_term = times_transposed(gate_half, gate_full)
-        return first_term + times_transposed(up_half, up_full)
-
-    normed_delta_two = collect_rows(normed_two_term, local_rows)
-    unused_two, back_two = jax.vjp(rms_scale, middle, norm_gains[2])
-    middle_part_delta, gain_two = back_two(normed_delta_two)
-    middle_delta = seed_rows + middle_part_delta
-    unused_one, back_one = jax.vjp(rms_scale, attention, norm_gains[1])
-    attention_delta, gain_one = back_one(middle_delta)
-    attention_rows = spread_grads(attention_delta.astype(jnp.bfloat16))
-    grad_out = inner_rows(head_flat, attention_rows)
-    heads_delta = (
-        times_transposed(attention_rows, out_full)
-        .astype(jnp.bfloat16)
-        .reshape(block_rows, key_heads, group_size, HEAD)
-    )
+    core = core_call(layer_in, cotangent, norm_gains, head_flat, w_out, w_gate, w_up, w_down)
+    layer_out, middle_delta, gain_sums, heads_delta, *pairs = core
+    rows_pair, hid_pair, branch_pair, gate_pair, up_pair, attn_pair, head_pair = pairs
+    heads_delta = heads_delta.reshape(block_rows, key_heads, group_size, HEAD)
     row_delta = jnp.einsum(
         "bkgh,bkgh->kgb", heads_delta, head_rows, preferred_element_type=jnp.float32
     )
@@ -269,7 +674,7 @@
     unused_zero, back_zero = jax.vjp(rms_scale, input_float, norm_gains[0])
     input_delta, gain_zero = back_zero(normed_delta_one)
     input_grad = middle_delta + input_delta
-    gain_terms = jnp.stack([gain_zero, gain_one, gain_two, gain_three])
+    gain_terms = jnp.concatenate([gain_zero[None], gain_sums])
     gain_grads = lax.psum_scatter(gain_terms, ("dp", "ctx", "tp"), scatter_dimension=1, tiled=True)
     summed = (
         lax.psum_scatter(
@@ -281,18 +686,10 @@
         lax.psum_scatter(
             grad_value.astype(jnp.bfloat16), ("dp", "ctx"), scatter_dimension=0, tiled=True
         ).astype(jnp.float32),
-        lax.psum_scatter(
-            grad_out.astype(jnp.bfloat16), ("dp", "ctx"), scatter_dimension=1, tiled=True
-        ).astype(jnp.float32),
-        lax.psum_scatter(
-            grad_gate.astype(jnp.bfloat16), ("dp", "ctx"), scatter_dimension=0, tiled=True
-        ).astype(jnp.float32),
-        lax.psum_scatter(
-            grad_up.astype(jnp.bfloat16), ("dp", "ctx"), scatter_dimension=0, tiled=True
-        ).astype(jnp.float32),
-        lax.psum_scatter(
-            grad_down.astype(jnp.bfloat16), ("dp", "ctx"), scatter_dimension=1, tiled=True
-        ).astype(jnp.float32),
+        over_ctx(inner_rows(head_pair, attn_pair), 1),
+        over_ctx(inner_rows(rows_pair, gate_pair), 0),
+        over_ctx(inner_rows(rows_pair, up_pair), 0),
+        over_ctx(inner_rows(hid_pair, branch_pair), 1),
     )
     grad_query, grad_key, grad_value, grad_out, grad_gate, grad_up, grad_down = summed
     return (

time: 1190 us -> 880 us (0.74)
  waiting for transfers between devices: 885 us -> 468 us
  Pallas kernels: 0 us -> 191 us
  matrix products: 164 us -> 91.8 us
  other arithmetic: 53.4 us -> 40 us
    pallas_call x0 -> x1, Pallas kernels: none -> 191 us  [core_call(): pl.pallas_call(functools.partial(core_kernel, T, C, NDP), out_shape=(sds(...]
    reduce_scatter x4 -> x1, waiting for transfers between devices: 193 us -> 49 us  [collect_rows(): lax.psum_scatter(term_fn(jnp.int32(0), row_total * lax.axis_size('tp')).a...]
    all_gather x6 -> x0, waiting for transfers between devices: 140 us -> none  [the longest x2 98.5 us: spread_grads(): return lax.all_gather(rows_part, 'tp', axis=0, tiled=True)]
    reduce_scatter x4, waiting for transfers between devices: 210 us -> 143 us  [over_ctx(): lax.psum_scatter(terms.astype(BF), 'ctx', scatter_dimension=dim, tiled=True)]
    all_gather x2 -> x1, waiting for transfers between devices: 107 us -> 53.3 us  [spread_rows(): return lax.all_gather(rows_part, 'tp', axis=0, tiled=True)]
    dot_general x4 -> x0, matrix products: 40.5 us -> none  [the longest x1 13 us: shards(): up_proj = jnp.dot(rows_two, up_full, preferred_element_type=jnp.float32)]
    dot_general x7 -> x3, matrix products: 44.9 us -> 5.91 us  [times_transposed(): lax.dot_general(former, latter, (((1,), (1,)), ((), ())), preferred_eleme...]
  transfers between devices with their start and end apart: 26 -> 16, of which waited for: 26 -> 15; matrix products, arithmetic and copies ran while one was open for 12% -> 11% of each run, Pallas kernels for 0% -> 0%
where the time goes in v1:
time: 880 us; the launch traced here: 871 us
  waiting for transfers between devices  468 us (53%)
  Pallas kernels  191 us (22%)
  matrix products  91.8 us (10%)
  blocking collectives  40.7 us (5%)
  other arithmetic  40 us (5%)
  local copies, waits for them, and re-layouts  23.1 us (3%)
  between operations  15.2 us (2%)
    pallas_call x1, Pallas kernels, core_call(): pl.pallas_call(functools.partial(core_kernel, T, C, NDP), out_shape=(sds(...  191 us
    reduce_scatter x4, waiting for transfers between devices, over_ctx(): lax.psum_scatter(terms.astype(BF), 'ctx', scatter_dimension=dim, tiled=True)  143 us
    all_gather x1, waiting for transfers between devices, spread_rows(): return lax.all_gather(rows_part, 'tp', axis=0, tiled=True)  53.3 us
    reduce_scatter x1, waiting for transfers between devices, collect_rows(): lax.psum_scatter(term_fn(jnp.int32(0), row_total * lax.axis_size('tp')).a...  49 us
    dot_general x7, matrix products, inner_rows(): lax.dot_general(former, latter, (((0,), (0,)), ((), ())), preferred_eleme...  41.2 us
    unnamed x1, blocking collectives  40.7 us
    reduce_scatter x1, waiting for transfers between devices, shards(): lax.psum_scatter(grad_value.astype(jnp.bfloat16), ('dp', 'ctx'), scatter_...  38.7 us
    reduce_scatter x1, waiting for transfers between devices, shards(): lax.psum_scatter(grad_key.astype(jnp.bfloat16), ('dp', 'ctx'), scatter_di...  38.7 us
  transfers between devices with their start and end apart: 16, of which 15 were waited for; matrix products, arithmetic and copies ran while one was open for 11% of the time, Pallas kernels for 0%

profile of v1, /device:TPU:0, one launch (start us, length us, event | category | flops | bytes accessed | tf_op | source)
XLA Modules:
  0.0 871.1 jit_solution(11528262340177354856)
XLA Ops:
  8.8 1.3 fusion.66
  10.0 2.1 fusion.63
  13.5 1.8 fusion.81
  15.3 6.2 all-gather.11.cloned.1.call-done
  21.5 53.3 %all-gather.9.cloned.1.call-done = bf16[512,2304]{1,0:T(8,128)(2,1)} async-done(((bf16[128,2304]{1,0:T(8,128)(2,1)}), bf16[512,2304]{1,0:T(8,128)(2,1)}) %all-gather.9.cloned.1.call-update) | async-done | bytes 2359312 | tf_op jit(solution)/shard_map/all_gather | solution.py:512
  74.8 2.8 fusion.85
  77.7 1.1 broadcast_multiply_fusion
  78.9 5.5 all-gather.15.cloned.1.call-done
  84.4 3.5 convolution_convert_fusion.6
  91.2 6.8 all-gather.13.cloned.1.call-done
  98.0 3.8 fusion.86
  105.3 2.4 fusion.69
  107.6 20.2 %all-gather.17.cloned.1.call-done = bf16[2048,256]{0,1:T(8,128)(2,1)} async-done(((bf16[512,256]{0,1:T(8,128)(2,1)}), bf16[2048,256]{0,1:T(8,128)(2,1)}) %all-gather.17.cloned.1.call-update) | async-done | bytes 1048592 | tf_op jit(solution)/shard_map/all_gather | solution.py:578
  127.8 28.8 %all-gather.19.cloned.1.call-done = bf16[2048,256]{1,0:T(8,128)(2,1)} async-done(((bf16[512,256]{1,0:T(8,128)(2,1)}), bf16[2048,256]{1,0:T(8,128)(2,1)}) %all-gather.19.cloned.1.call-update) | async-done | bytes 1048592 | tf_op jit(solution)/shard_map/all_gather | solution.py:579
  156.6 9.9 %conditional.2 = (f32[512,1,2,256]{3,0,2,1:T(8,128)S(1)}, f32[1,2,512]{2,1,0:T(2,128)}, f32[1,2,512]{2,1,0:T(2,128)S(1)}) conditional(s32[]{:T(128)} %bitcast.39, () %tuple.26, (s32[512]{0:T(512)S(1)}, bf16[2048,1,256]{0,2,1:T(8,128)(2,1)}, bf16[512,1,2,256]{3,0,2,1:T(8,128)(2,1)}, bf16[2048,1,256]{2,0,1:T(8,128)(2,1)}) %tuple.95), branch_computations={%region_1.0_spmd, %region_2.4_spmd} | conditional | flops 2165308416 | bytes 27801652 | solution.py:593
  157.4 5.5 fusion
  162.9 2.9 fusion.6
  166.5 1.9 bitcast_convert_fusion
  168.9 1.1 reshape_reshape.5.heads_ref
  170.1 190.9 %core.1 = (bf16[128,2304]{1,0:T(8,128)(2,1)}, f32[128,2304]{1,0:T(8,128)}, f32[3,2304]{1,0:T(4,128)}, bf16[4,4,32,512]{3,2,1,0:T(8,128)(2,1)}, bf16[2,4,4,32,115...) custom-call(bf16[128,2304]{1,0:T(8,128)(2,1)} %x_ref.1, ...), custom_call_target="tpu_custom_call" | custom-call | tf_op jit(solution)/shard_map/core/pallas_call | solution.py:439
  360.9 2.0 reshape.346
  363.0 1.4 bitcast_convert_fusion.1
  364.4 33.1 %conditional.3 = (bf16[2048,1,256]{2,0,1:T(8,128)(2,1)S(1)}, bf16[2048,1,256]{2,0,1:T(8,128)(2,1)}, f32[512,1,2,256]{0,3,2,1:T(8,128)S(1)}) conditional(s32[]{:T(128)} %bitcast.39, () %tuple.28, (s32[512]{0:T(512)S(1)}, bf16[2048,1,256]{0,2,1:T(8,128)(2,1)}, bf16[512,1,2,256]{3,0,2,1:T(8,128)(2,1)}, f32[1,2,512]{2,1,0:T(2,128)S(1)}, ...), branch_computations={%region_4.5_spmd, %region_5.6_spmd.clone} | conditional | flops 5403048960 | bytes 81807488 | solution.py:642
  364.8 5.9 fusion.48
  370.8 1.8 iota_compare_fusion.1
  372.6 2.0 reshape.376
  374.7 8.5 fusion.16
  383.2 2.0 copy-done.21
  385.2 1.3 fusion.44
  386.9 3.7 fusion.38
  390.6 6.9 fusion.29
  397.5 1.4 copy.64
  399.7 4.5 fusion.60
  404.5 1.3 maximum_multiply_fusion.1
  407.0 2.9 convolution_convert_fusion.3
  410.0 15.4 %reduce-scatter.12.cloned.1.call-done = bf16[512,1,256]{0,2,1:T(8,128)(2,1)} async-done(((bf16[2048,1,256]{0,2,1:T(8,128)(2,1)}), bf16[512,1,256]{0,2,1:T(8,128)(2,1)}) %reduce-scatter.12.cloned.1.call-update) | async-done | bytes 262160 | tf_op jit(solution)/shard_map/reduce_scatter | solution.py:646
  429.2 1.8 convolution_convert_fusion.5
  431.1 25.7 %reduce-scatter.14.cloned.1.call-done = bf16[512,1,256]{2,0,1:T(8,128)(2,1)} async-done(((bf16[2048,1,256]{2,0,1:T(8,128)(2,1)}), bf16[512,1,256]{2,0,1:T(8,128)(2,1)}) %reduce-scatter.14.cloned.1.call-update) | async-done | bytes 262160 | tf_op jit(solution)/shard_map/reduce_scatter | solution.py:649
  456.8 2.8 convolution_convert_fusion.4
  459.7 2.2 fusion.79
  462.0 1.4 convolution_add_fusion
  463.5 2.2 fusion.59
  465.8 1.7 copy-done.19
  467.4 9.8 %convolution_convert_fusion = bf16[2304,1152]{0,1:T(8,128)(2,1)} fusion(bf16[1024,2304]{1,0:T(8,128)(2,1)} %bitcast.251, bf16[1024,1152]{1,0:T(8,128)(2,1)S(1)} %bitcast.254), kind=kOutput, calls=%fused_computation.51 | convolution fusion | flops 5438472192 | bytes 12386304 | tf_op jit(solution)/shard_map/dot_general | solution.py:492
  477.3 1.6 copy-done.18
  478.8 9.7 %convolution_convert_fusion.1 = bf16[1152,2304]{1,0:T(8,128)(2,1)} fusion(bf16[1024,1152]{1,0:T(8,128)(2,1)S(1)} %bitcast.252, bf16[1024,2304]{1,0:T(8,128)(2,1)} %bitcast.250), kind=kOutput, calls=%fused_computation.52 | convolution fusion | flops 5438472192 | bytes 12386304 | tf_op jit(solution)/shard_map/dot_general | solution.py:492
  488.8 9.7 %convolution_convert_fusion.2 = bf16[1152,2304]{1,0:T(8,128)(2,1)} fusion(bf16[1024,1152]{1,0:T(8,128)(2,1)S(1)} %bitcast.253, bf16[1024,2304]{1,0:T(8,128)(2,1)} %bitcast.249), kind=kOutput, calls=%fused_computation.53 | convolution fusion | flops 5438472192 | bytes 12386304 | tf_op jit(solution)/shard_map/dot_general | solution.py:492
  498.7 2.0 convert_element_type.141
  500.7 33.9 %reduce-scatter.18.cloned.1.call-done = bf16[288,512]{1,0:T(8,128)(2,1)} async-done(((bf16[2304,512]{1,0:T(8,128)(2,1)}), bf16[288,512]{1,0:T(8,128)(2,1)}) %reduce-scatter.18.cloned.1.call-update) | async-done | bytes 294928 | tf_op jit(solution)/shard_map/reduce_scatter | solution.py:680
  534.6 1.8 convert_element_type.135
  536.5 38.7 %reduce-scatter.20.cloned.1.call-done = bf16[288,256]{1,0:T(8,128)(2,1)} async-done(((bf16[2304,256]{1,0:T(8,128)(2,1)}), bf16[288,256]{1,0:T(8,128)(2,1)}) %reduce-scatter.20.cloned.1.call-update) | async-done | bytes 147472 | tf_op jit(solution)/shard_map/reduce_scatter | solution.py:683
  575.1 1.6 convert_element_type.137
  576.8 38.7 %reduce-scatter.22.cloned.1.call-done = bf16[288,256]{1,0:T(8,128)(2,1)} async-done(((bf16[2304,256]{1,0:T(8,128)(2,1)}), bf16[288,256]{1,0:T(8,128)(2,1)}) %reduce-scatter.22.cloned.1.call-update) | async-done | bytes 147472 | tf_op jit(solution)/shard_map/reduce_scatter | solution.py:686
  615.5 1.6 convert_element_type.139
  617.1 49.0 %reduce-scatter.16.cloned.1.call-done = bf16[128,2304]{1,0:T(8,128)(2,1)} async-done(((bf16[512,2304]{1,0:T(8,128)(2,1)}), bf16[128,2304]{1,0:T(8,128)(2,1)}) %reduce-scatter.16.cloned.1.call-update) | async-done | bytes 589840 | tf_op jit(solution)/shard_map/reduce_scatter | solution.py:516
  666.1 1.7 fusion.64
  667.9 40.7 %all-reduce = f32[4,2304]{1,0:T(4,128)S(1)} all-reduce(f32[4,2304]{1,0:T(4,128)S(1)} %pad_maximum_fusion.2), channel_id=7, replica_groups=mesh['dp'=2,'ctx'=4,'tp'=4] {'dp','ctx','tp'}, use_global_device_ids=true, to_apply=%region_11.12.clone | all-reduce | flops 9216 | bytes 73728
  709.3 2.4 fusion.65
  711.7 19.3 %reduce-scatter.30.cloned.1.call-done = bf16[2304,288]{0,1:T(8,128)(2,1)} async-done(((bf16[2304,1152]{0,1:T(8,128)(2,1)}), bf16[2304,288]{0,1:T(8,128)(2,1)}) %reduce-scatter.30.cloned.1.call-update) | async-done | bytes 1327120 | tf_op jit(solution)/shard_map/reduce_scatter | solution.py:525
  731.1 3.0 convert_element_type.147
  734.1 61.7 %reduce-scatter.28.cloned.1.call-done = bf16[288,2304]{1,0:T(8,128)(2,1)} async-done(((bf16[1152,2304]{1,0:T(8,128)(2,1)}), bf16[288,2304]{1,0:T(8,128)(2,1)}) %reduce-scatter.28.cloned.1.call-update) | async-done | bytes 1327120 | tf_op jit(solution)/shard_map/reduce_scatter | solution.py:525
  795.8 3.0 convert_element_type.145
  798.8 61.8 %reduce-scatter.26.cloned.1.call-done = bf16[288,2304]{1,0:T(8,128)(2,1)} async-done(((bf16[1152,2304]{1,0:T(8,128)(2,1)}), bf16[288,2304]{1,0:T(8,128)(2,1)}) %reduce-scatter.26.cloned.1.call-update) | async-done | bytes 1327120 | tf_op jit(solution)/shard_map/reduce_scatter | solution.py:525
  860.6 3.0 convert_element_type.143
  (104 shorter events, 19.9 us)
Async XLA Ops:
  7.2 14.3 %all-gather.11.cloned.1.call-start = ((), (), s32[]{:S(2)}) async-start(), calls=%async_computation.11 | async-start | bytes 1769472 | tf_op jit(solution)/shard_map/all_gather | solution.py:506
  7.9 66.9 %all-gather.9.cloned.1.call-start = ((), (), s32[]{:S(2)}) async-start(), calls=%async_computation.10 | async-start | bytes 2949120 | tf_op jit(solution)/shard_map/all_gather | solution.py:512
  12.1 72.3 %all-gather.15.cloned.1.call-start = ((), (), s32[]{:S(2)}) async-start(), calls=%async_computation.13 | async-start | bytes 1769472 | tf_op jit(solution)/shard_map/all_gather | solution.py:507
  12.9 85.1 %all-gather.13.cloned.1.call-start = ((), (), s32[]{:S(2)}) async-start(), calls=%async_computation.12 | async-start | bytes 3538944 | tf_op jit(solution)/shard_map/all_gather | solution.py:505
  13.5 114.3 %all-gather.17.cloned.1.call-start = ((), (), s32[]{:S(2)}) async-start(), calls=%async_computation.24 | async-start | bytes 1310720 | tf_op jit(solution)/shard_map/all_gather | solution.py:578
  78.8 77.8 %all-gather.19.cloned.1.call-start = ((), (), s32[]{:S(2)}) async-start(), calls=%async_computation.25 | async-start | bytes 1310720 | tf_op jit(solution)/shard_map/all_gather | solution.py:579
  87.9 337.5 %reduce-scatter.12.cloned.1.call-start = ((), (), s32[]{:S(2)}) async-start(), calls=%async_computation.14 | async-start | bytes 1310720 | tf_op jit(solution)/shard_map/reduce_scatter | solution.py:646
  157.4 5.5 copy-start.20
  360.9 3.5 copy-start.1
  374.7 10.5 %copy-start.9 = (bf16[2048,1,256]{0,2,1:T(8,128)(2,1)S(1)}, bf16[2048,1,256]{0,2,1:T(8,128)(2,1)}, u32[]{:S(2)}) copy-start(bf16[2048,1,256]{0,2,1:T(8,128)(2,1)} %get-tuple-element.120) | copy-start | bytes 3145732 | tf_op jit(solution)/shard_map/cond
  383.2 2.0 copy-start.21
  386.9 3.7 copy-start.10
  386.9 3.7 copy-start.13
  398.9 57.9 %reduce-scatter.14.cloned.1.call-start = ((), (), s32[]{:S(2)}) async-start(), calls=%async_computation.15 | async-start | bytes 1310720 | tf_op jit(solution)/shard_map/reduce_scatter | solution.py:649
  399.7 99.0 %reduce-scatter.24.cloned.1.call-start = ((), (), s32[]{:S(2)}) async-start(), calls=%async_computation.20 | async-start | bytes 1474560 | tf_op jit(solution)/shard_map/reduce_scatter | solution.py:525
  404.2 130.4 %reduce-scatter.18.cloned.1.call-start = ((), (), s32[]{:S(2)}) async-start(), calls=%async_computation.17 | async-start | bytes 2654208 | tf_op jit(solution)/shard_map/reduce_scatter | solution.py:680
  404.5 2.5 copy-start.16
  406.2 0.8 copy-start.2
  409.9 17.5 %copy-start.11 = (f32[512,1,128]{0,2,1:T(8,128)S(1)}, f32[512,1,128]{0,2,1:T(8,128)}, u32[]{:S(2)}) copy-start(f32[512,1,128]{0,2,1:T(8,128)} %get-tuple-element.151) | copy-start | bytes 786436
  409.9 19.3 %copy-start.17 = (bf16[512,2304]{1,0:T(8,128)(2,1)S(1)}, bf16[512,2304]{1,0:T(8,128)(2,1)}, u32[]{:S(2)}) copy-start(bf16[512,2304]{1,0:T(8,128)(2,1)} %all-gather.9.cloned.1.call-done) | copy-start | bytes 7077892
  409.9 165.2 %reduce-scatter.20.cloned.1.call-start = ((), (), s32[]{:S(2)}) async-start(), calls=%async_computation.18 | async-start | bytes 1327104 | tf_op jit(solution)/shard_map/reduce_scatter | solution.py:683
  428.5 0.7 copy-start.5
  431.0 28.7 %copy-start.6 = (bf16[512,1,256]{0,2,1:T(8,128)(2,1)S(1)}, bf16[512,1,256]{0,2,1:T(8,128)(2,1)}, u32[]{:S(2)}) copy-start(bf16[512,1,256]{0,2,1:T(8,128)(2,1)} %copy-done.5) | copy-start | bytes 786436
  431.0 184.5 %reduce-scatter.22.cloned.1.call-start = ((), (), s32[]{:S(2)}) async-start(), calls=%async_computation.19 | async-start | bytes 1327104 | tf_op jit(solution)/shard_map/reduce_scatter | solution.py:686
  459.6 2.3 copy-start.3
  459.6 2.3 copy-start.4
  459.6 206.5 %reduce-scatter.16.cloned.1.call-start = ((), (), s32[]{:S(2)}) async-start(), calls=%async_computation.16 | async-start | bytes 2949120 | tf_op jit(solution)/shard_map/reduce_scatter | solution.py:516
  462.0 1.5 copy-start.8
  462.0 1.5 copy-start.14
  465.7 1.7 copy-start.19
  465.7 265.4 %reduce-scatter.30.cloned.1.call-start = ((), (), s32[]{:S(2)}) async-start(), calls=%async_computation.23 | async-start | bytes 6635520 | tf_op jit(solution)/shard_map/reduce_scatter | solution.py:525
  477.2 1.7 copy-start.18
  477.2 318.6 %reduce-scatter.28.cloned.1.call-start = ((), (), s32[]{:S(2)}) async-start(), calls=%async_computation.22 | async-start | bytes 6635520 | tf_op jit(solution)/shard_map/reduce_scatter | solution.py:525
  488.6 372.0 %reduce-scatter.26.cloned.1.call-start = ((), (), s32[]{:S(2)}) async-start(), calls=%async_computation.21 | async-start | bytes 6635520 | tf_op jit(solution)/shard_map/reduce_scatter | solution.py:525
  498.6 167.5 %copy-start = (bf16[128,2304]{1,0:T(8,128)(2,1)S(1)}, bf16[128,2304]{1,0:T(8,128)(2,1)}, u32[]{:S(2)}) copy-start(bf16[128,2304]{1,0:T(8,128)(2,1)} %x_ref.1) | copy-start | bytes 1769476
  498.6 169.2 %copy-start.15 = (f32[3,2304]{1,0:T(4,128)S(1)}, f32[3,2304]{1,0:T(4,128)}, u32[]{:S(2)}) copy-start(f32[3,2304]{1,0:T(4,128)} %get-tuple-element.72) | copy-start | bytes 82948
  498.6 210.7 %copy-start.7 = (f32[128,2304]{1,0:T(8,128)S(1)}, f32[128,2304]{1,0:T(8,128)}, u32[]{:S(2)}) copy-start(f32[128,2304]{1,0:T(8,128)} %get-tuple-element.66) | copy-start | bytes 3538948
  798.8 64.8 %copy-start.12 = (bf16[128,2304]{1,0:T(8,128)(2,1)S(1)}, bf16[128,2304]{1,0:T(8,128)(2,1)}, u32[]{:S(2)}) copy-start(bf16[128,2304]{1,0:T(8,128)(2,1)} %get-tuple-element.176) | copy-start | bytes 1769476
Sparse Core Ops, SparseCore 0:
  9.5 11.9 all-gather.10
  23.6 51.1 all-gather.8
  76.4 7.9 all-gather.14
  85.8 12.1 all-gather.12
  100.2 27.5 all-gather.16
  130.1 26.4 all-gather.18
  399.0 26.2 reduce-scatter.11
  428.8 27.9 reduce-scatter.13
  459.7 28.6 reduce-scatter.23
  492.2 42.3 reduce-scatter.17
  538.4 36.6 reduce-scatter.19
  578.8 36.6 reduce-scatter.21
  618.4 47.6 reduce-scatter.15
  669.0 62.0 reduce-scatter.29
  733.9 61.8 reduce-scatter.27
  798.7 61.8 reduce-scatter.25

commit v2 on v1

--- a/solution.py
+++ b/solution.py
@@ -469,6 +469,597 @@
     )
 
 
+def flip(index, bit):
+    return index + bit * (1 - 2 * lax.rem(index // bit, 2))
+
+
+def flips(index, mask):
+    bit = 1
+    while bit <= mask:
+        if mask & bit:
+            index = flip(index, bit)
+        bit *= 2
+    return index
+
+
+def dot_tn(former, latter):
+    return lax.dot_general(former, latter, (((0,), (0,)), ((), ())), preferred_element_type=F32)
+
+
+def sub_sums(bits):
+    sums = [0]
+    for bit in bits:
+        sums = sums + [s + bit for s in sums]
+    return sums
+
+
+def bits_below(count):
+    return [1 << i for i in range(count.bit_length() - 1)]
+
+
+def tail_kernel(
+    T, NC, NDP, KH, NS,
+    x_ref, mdelta_ref, gain_ref, gsum_ref, q_ref, hd_ref, logt_ref, rdelta_ref, cos_ref, sin_ref,
+    k_ref, v_ref, rows1_ref, wq_ref, wk_ref, wv_ref,
+    rows_ref, branch_ref, attn_ref, head_ref, gate_ref, up_ref, hid_ref,
+    igrad_ref, gains_ref, gate_o, up_o, down_o, out_o, q_o, k_o, v_o,
+    L, Rc, Hd, RQ, RKV, WQ, WK, WV, Pe, *rest,
+):
+    m = NC.bit_length() - 1
+    Rv, rest = rest[:m], rest[m:]
+    (
+        st, dq, kvb, kvs, kvr, Pb, Rb, acc, G, GR,
+        l_sem, r_sem, w_sem, pair_sem, e_send, e_recv, st_sem, kv_send, kv_recv,
+        rs_send, rs_recv, g_send, g_recv, kvb_sem,
+    ) = rest
+    t, c, dp = lax.axis_index("tp"), lax.axis_index("ctx"), lax.axis_index("dp")
+    Lr, D = x_ref.shape
+    R, Hq = q_ref.shape
+    KVd = KH * HEAD
+    GS = Hq // KVd
+    Dh, RB = D // NDP, D // NDP // NC
+    F = gate_ref.shape[1]
+    W = Rc.shape[2] // 2
+    NF = F // (2 * W)
+    wide_units, units = 3 * NF, 3 * NF + 3
+    narrow = Hq // 2
+    scale = HEAD**-0.5
+
+    def along(axis, index):
+        return {axis: index}
+
+    others = [along("tp", lax.rem(t + o, T)) for o in range(1, T)]
+    others += [along("ctx", lax.rem(c + o, NC)) for o in range(1, NC)]
+    partners = [along("dp", lax.rem(dp + o, NDP)) for o in range(1, NDP)]
+    sem = pltpu.get_barrier_semaphore()
+    for peer in others + partners:
+        pl.semaphore_signal(sem, inc=1, device_id=peer, device_id_type=MESH)
+    pl.semaphore_wait(sem, len(others + partners))
+
+    def remote(src, dst, send, recv, peer):
+        return pltpu.make_async_remote_copy(src, dst, send, recv, device_id=peer, device_id_type=MESH)
+
+    firsts = [rows_ref, branch_ref, attn_ref]
+
+    def first_copy(i):
+        return pltpu.make_async_copy(firsts[i], L.at[i % 2], l_sem.at[i])
+
+    def half_of(ref, owner):
+        return ref.at[:, pl.ds(pl.multiple_of(owner * Dh, 128), Dh)]
+
+    rows_at = pl.ds(pl.multiple_of(dp * Dh, 128), Dh)
+    token_at = pl.ds(pl.multiple_of(dp * R, 128), R)
+    spread = [
+        (lambda owner: half_of(rows1_ref, owner), L.at[2, token_at]),
+        (lambda owner: wq_ref, WQ.at[rows_at]),
+        (lambda owner: wk_ref, WK.at[rows_at]),
+        (lambda owner: wv_ref, WV.at[rows_at]),
+    ]
+
+    def spread_local(i):
+        return pltpu.make_async_copy(spread[i][0](dp), spread[i][1], w_sem.at[0, i])
+
+    def spread_remote(i, o):
+        return remote(
+            spread[i][0](partners[o]["dp"]), spread[i][1],
+            w_sem.at[1 + 2 * o, i], w_sem.at[2 + 2 * o, i], partners[o],
+        )
+
+    kinds = [gate_ref, up_ref, hid_ref]
+
+    def chunk_copy(u, kind):
+        at = pl.ds(pl.multiple_of((u - kind * NF) * 2 * W, 128), 2 * W)
+        return pltpu.make_async_copy(kinds[kind].at[:, at], Rc.at[lax.rem(u, 2)], r_sem.at[lax.rem(u, 2)])
+
+    def chunk_start(u):
+        for kind in range(3):
+
+            @pl.when((u >= kind * NF) & (u < (kind + 1) * NF))
+            def _():
+                chunk_copy(u, kind).start()
+
+    first_copy(0).start()
+    chunk_start(0)
+    first_copy(1).start()
+    for i in range(4):
+        spread_local(i).start()
+        for o in range(NDP - 1):
+            spread_remote(i, o).start()
+    head_copy = pltpu.make_async_copy(head_ref, Hd, l_sem.at[3])
+    head_copy.start()
+
+    orders = [bits_below(NC), bits_below(NC)[::-1]]
+    first_of = [sum(NC >> (i + 1) for i in range(k)) for k in range(m)]
+
+    def e_copy(u, par, k, n, w):
+        order = orders[par]
+        kept = sub_sums(order[k + 1:])[n]
+        slot = lax.rem(u, NS)
+        at = first_of[k] + n
+        return remote(
+            Pe.at[slot, par, flips(c, kept + order[k]), :, pl.ds(0, w)],
+            Rv[k].at[slot, par, n, :, pl.ds(0, w)],
+            e_send.at[slot, par, at], e_recv.at[slot, par, at],
+            along("ctx", flip(c, order[k])),
+        )
+
+    def e_sent(u, w):
+        for par in (0, 1):
+            for k in range(m):
+                for n in range(NC >> (k + 1)):
+                    e_copy(u, par, k, n, w).wait_send()
+
+    def e_product(u, w):
+        slot = lax.rem(u, NS)
+
+        def store(par, first, second):
+            Pe[slot, par, :, :, :w] = dot_tn(first, second).reshape(NC, RB, w).astype(BF)
+
+        if w == W:
+            for kind in range(3):
+
+                @pl.when((u >= kind * NF) & (u < (kind + 1) * NF))
+                def _():
+                    chunk_copy(u, kind).wait()
+
+            @pl.when(u == 0)
+            def _():
+                first_copy(0).wait()
+
+            @pl.when(u == 2 * NF)
+            def _():
+                first_copy(1).wait()
+                first_copy(2).start()
+
+            chunk_start(u + 1)
+            at = jnp.where(u >= 2 * NF, 1, 0)
+            for par in (0, 1):
+                store(par, L[at], Rc[lax.rem(u, 2), :, par * W:(par + 1) * W])
+        else:
+
+            @pl.when(u == wide_units)
+            def _():
+                first_copy(2).wait()
+                head_copy.wait()
+                for par in (0, 1):
+                    store(par, L[0], Hd[:, par * w:(par + 1) * w])
+
+            @pl.when(u == wide_units + 1)
+            def _():
+                for par in (0, 1):
+                    store(par, L[2], RQ[:, :, par * w:(par + 1) * w].reshape(NDP * R, w))
+
+            @pl.when(u == wide_units + 2)
+            def _():
+                for par in (0, 1):
+                    store(par, L[2], RKV[:, par].reshape(NDP * R, w))
+
+    def e_send_step(u, k, w):
+        for par in (0, 1):
+            for n in range(NC >> (k + 1)):
+                e_copy(u, par, k, n, w).start()
+
+    def e_add(u, k, w):
+        slot = lax.rem(u, NS)
+        for par in (0, 1):
+            for n in range(NC >> (k + 1)):
+                e_copy(u, par, k, n, w).wait_recv()
+                if k < m - 1:
+                    kept = flips(c, sub_sums(orders[par][k + 1:])[n])
+                    Pe[slot, par, kept, :, :w] = (
+                        Pe[slot, par, kept, :, :w].astype(F32) + Rv[k][slot, par, n, :, :w].astype(F32)
+                    ).astype(BF)
+
+    def out_copies(u, w):
+        two = lax.rem(u, 2)
+
+        def copy(par, dst):
+            return pltpu.make_async_copy(st.at[two, par, :, pl.ds(0, w)], dst, st_sem.at[two, par])
+
+        if w == W:
+            pairs = []
+            for kind, dst in enumerate([gate_o, up_o, down_o]):
+                base = (u - kind * NF) * 2 * W
+                pairs.append((
+                    (u >= kind * NF) & (u < (kind + 1) * NF),
+                    [copy(p, dst.at[:, pl.ds(pl.multiple_of(base + p * W, 128), W)]) for p in (0, 1)],
+                ))
+            return pairs
+        return [
+            (u == wide_units, [copy(p, out_o.at[:, pl.ds(p * w, w)]) for p in (0, 1)]),
+            (u == wide_units + 1, [copy(p, q_o.at[:, pl.ds(p * w, w)]) for p in (0, 1)]),
+            (u == wide_units + 2, [copy(0, k_o), copy(1, v_o)]),
+        ]
+
+    def out_wait(u):
+        for w in (W, narrow):
+            for here, copies in out_copies(u, w):
+
+                @pl.when(here)
+                def _():
+                    for copy in copies:
+                        copy.wait()
+
+    def e_finish(u, w):
+        slot, two = lax.rem(u, NS), lax.rem(u, 2)
+        e_add(u, m - 1, w)
+        out_wait(u - 2)
+        for par in (0, 1):
+            st[two, par, :, :w] = Pe[slot, par, c, :, :w].astype(F32) + Rv[m - 1][slot, par, 0, :, :w].astype(F32)
+        for here, copies in out_copies(u, w):
+
+            @pl.when(here)
+            def _():
+                for copy in copies:
+                    copy.start()
+
+    def by_width(u, body):
+        @pl.when((u >= 0) & (u < wide_units))
+        def _():
+            body(W)
+
+        @pl.when((u >= wide_units) & (u < units))
+        def _():
+            body(narrow)
+
+    key_tile = min(256, R)
+
+    def kv_copy(d):
+        return remote(
+            kvs.at[lax.rem(d, kvs.shape[0])], kvr.at[d - 1], kv_send.at[d - 1], kv_recv.at[d - 1],
+            along("ctx", jnp.maximum(c - d, 0)),
+        )
+
+    def block_copies(block):
+        at = pl.ds(pl.multiple_of(block * R, 128), R)
+        two = lax.rem(block, 2)
+        return [
+            pltpu.make_async_copy(ref.at[at], kvb.at[two, i], kvb_sem.at[two, i])
+            for i, ref in enumerate((k_ref, v_ref))
+        ]
+
+    def block_start(block):
+        for copy in block_copies(block):
+            copy.start()
+
+    def block_wait(block):
+        for copy in block_copies(block):
+            copy.wait()
+
+    def attend(two, masked, dst):
+        for kh in range(KH):
+            cols = slice(kh * HEAD, (kh + 1) * HEAD)
+
+            def key_step(i, carry):
+                start = pl.multiple_of(i * key_tile, key_tile)
+                at = pl.ds(start, key_tile)
+                keys, values = kvb[two, 0, at, cols], kvb[two, 1, at, cols]
+                key_sum = jnp.zeros((key_tile, HEAD), F32)
+                value_sum = jnp.zeros((key_tile, HEAD), F32)
+                for g in range(GS):
+                    h = kh * GS + g
+                    head = slice(h * HEAD, (h + 1) * HEAD)
+                    query, delta = q_ref[:, head], hd_ref[:, head]
+                    bent = jnp.tanh(dot_nt(keys, query) * (scale / CAP))
+                    prob = jnp.exp(CAP * bent - logt_ref[h:h + 1, :])
+                    if masked:
+                        key_pos = start + lax.broadcasted_iota(jnp.int32, prob.shape, 0)
+                        prob = jnp.where(key_pos <= lax.broadcasted_iota(jnp.int32, prob.shape, 1), prob, 0.0)
+                    grad = prob * (dot_nt(values, delta) - rdelta_ref[h:h + 1, :]) * (1.0 - bent * bent)
+                    grad = grad.astype(BF)
+                    value_sum += dot_nn(prob.astype(BF), delta)
+                    key_sum += dot_nn(grad, query)
+                    dq[:, head] += dot_tn(grad, keys)
+                rows = pl.ds(start, key_tile)
+                kvs[dst, 0, rows, cols] = (key_sum * scale).astype(BF)
+                kvs[dst, 1, rows, cols] = value_sum.astype(BF)
+                return carry
+
+            lax.fori_loop(0, R // key_tile, key_step, 0)
+
+    def attention():
+        dq[...] = jnp.zeros_like(dq)
+        block_start(0)
+
+        def far(block, carry):
+            d = c - block
+
+            @pl.when(block < c)
+            def _():
+                slot = lax.rem(d, kvs.shape[0])
+                block_wait(block)
+                block_start(block + 1)
+
+                @pl.when(d + kvs.shape[0] <= c)
+                def _():
+                    kv_copy(d + kvs.shape[0]).wait_send()
+
+                attend(lax.rem(block, 2), False, slot)
+                kv_copy(d).start()
+
+            return carry
+
+        lax.fori_loop(0, NC - 1, far, 0)
+
+        @pl.when(c >= kvs.shape[0])
+        def _():
+            kv_copy(kvs.shape[0]).wait_send()
+
+        block_wait(c)
+        attend(lax.rem(c, 2), True, 0)
+
+    def turned(values, h):
+        a, b = values[:, h * HEAD:h * HEAD + HEAD // 2], values[:, h * HEAD + HEAD // 2:(h + 1) * HEAD]
+        cosine, sine = cos_ref[...], sin_ref[...]
+        return jnp.concatenate([a * cosine + b * sine, b * cosine - a * sine], axis=1).astype(BF)
+
+    def pair_remote(i, o):
+        ref = [RQ, RKV][i]
+        return remote(ref.at[dp], ref.at[dp], pair_sem.at[2 * o, i], pair_sem.at[2 * o + 1, i], partners[o])
+
+    has_left, has_right = t > 0, t < T - 1
+
+    def rs_copy(side, k, j):
+        if side == 0:
+            slot, peer = j, jnp.minimum(t + 1, T - 1)
+        else:
+            slot, peer = jnp.where(j == t - 1, T, j), jnp.maximum(t - 1, 0)
+        return remote(Pb.at[j], Rb.at[slot], rs_send.at[side, k], rs_recv.at[side, k], along("tp", peer))
+
+    def rs_block(side, k):
+        return (T - 1 - k + t) if side == 0 else (k - (T - 1 - t))
+
+    def rs_sends(side, k):
+        return (t <= k) & has_right if side == 0 else (T - 1 - t <= k) & has_left
+
+    def rs_step(k):
+        for side in (0, 1):
+            j = rs_block(side, k)
+
+            @pl.when(rs_sends(side, k))
+            def _():
+                if k:
+
+                    @pl.when(has_left if side == 0 else has_right)
+                    def _():
+                        rs_copy(side, k - 1, j).wait_recv()
+                        Pb[j] = (Pb[j].astype(F32) + Rb[j].astype(F32)).astype(BF)
+
+                rs_copy(side, k, j).start()
+
+    def own_keys():
+        for which in range(2):
+            dst = []
+            for kh in range(KH):
+                dst.append(kvs[0, which, :, kh * HEAD:(kh + 1) * HEAD].astype(F32))
+            acc[which] = jnp.concatenate(dst, axis=1) if KH > 1 else dst[0]
+
+        def come(i, carry):
+            d = i + 1
+
+            @pl.when(c + d <= NC - 1)
+            def _():
+                kv_copy(d).wait_recv()
+                for which in range(2):
+                    acc[which] += kvr[d - 1, which].astype(F32)
+
+            return carry
+
+        lax.fori_loop(0, NC - 1, come, 0)
+        for kh in range(KH):
+            cols = slice(kh * HEAD, (kh + 1) * HEAD)
+            RKV[dp, 0, :, cols] = turned(acc[0], kh)
+        RKV[dp, 1] = acc[1].astype(BF)
+        for h in range(Hq // HEAD):
+            RQ[dp, :, h * HEAD:(h + 1) * HEAD] = turned(dq[...] * scale, h)
+        for i in range(2):
+            for o in range(NDP - 1):
+                pair_remote(i, o).start()
+        for i in range(4):
+            spread_local(i).wait()
+            for o in range(NDP - 1):
+                spread_remote(i, o).wait_recv()
+        tile = tile_of(D)
+
+        def part(i, carry):
+            at = pl.ds(pl.multiple_of(i * tile, tile), tile)
+            terms = dot_nt(RQ[dp], WQ[at, :]) + dot_nt(RKV[dp, 0], WK[at, :]) + dot_nt(RKV[dp, 1], WV[at, :])
+            Pb[:, :, at] = terms.astype(BF).reshape(T, Lr, tile)
+            return carry
+
+        lax.fori_loop(0, D // tile, part, 0)
+        rs_step(0)
+
+    def rs_finish():
+        igrad_ref[...] = Pb[t].astype(F32)
+
+        @pl.when(has_left)
+        def _():
+            rs_copy(0, T - 2, t).wait_recv()
+            igrad_ref[...] += Rb[t].astype(F32)
+
+        @pl.when(has_right)
+        def _():
+            rs_copy(1, T - 2, t).wait_recv()
+            igrad_ref[...] += Rb[T].astype(F32)
+
+        rows = x_ref[...].astype(F32)
+        grad, terms = rms_back(rows, inverse_rms(rows), gain_ref[0:1], igrad_ref[...])
+        igrad_ref[...] = mdelta_ref[...] + grad
+        G[0, 0:1] = terms
+        G[0, 1:4] = gsum_ref[...]
+
+    meets = [("tp", t, b) for b in bits_below(T)] + [("ctx", c, b) for b in bits_below(NC)]
+    meets += [("dp", dp, b) for b in bits_below(NDP)]
+
+    def g_copy(k):
+        axis, index, bit = meets[k]
+        return remote(G.at[k], GR.at[k], g_send.at[k], g_recv.at[k], along(axis, flip(index, bit)))
+
+    def tick(i, carry):
+        def start(w):
+            @pl.when(i >= NS)
+            def _():
+                by_width(i - NS, lambda before: e_sent(i - NS, before))
+
+            e_product(i, w)
+            e_send_step(i, 0, w)
+
+        by_width(i, start)
+
+        @pl.when(i == 1)
+        def _():
+            attention()
+
+        @pl.when(i == 2)
+        def _():
+            own_keys()
+
+        for k in range(1, T - 1):
+
+            @pl.when(i == 2 + k)
+            def _():
+                rs_step(k)
+
+        @pl.when(i == 1 + T)
+        def _():
+            rs_finish()
+            g_copy(0).start()
+
+        for k in range(len(meets)):
+
+            @pl.when(i == 2 + T + k)
+            def _():
+                g_copy(k).wait_recv()
+                G[k + 1] = G[k] + GR[k]
+                if k + 1 < len(meets):
+                    g_copy(k + 1).start()
+
+        @pl.when(i == wide_units)
+        def _():
+            for p in range(2):
+                for o in range(NDP - 1):
+                    pair_remote(p, o).wait_recv()
+
+        for k in range(1, m):
+
+            def middle(w):
+                e_add(i - k, k - 1, w)
+                e_send_step(i - k, k, w)
+
+            by_width(i - k, middle)
+        by_width(i - m, lambda w: e_finish(i - m, w))
+        return carry
+
+    lax.fori_loop(0, units + m, tick, 0)
+    gains_ref[...] = G[len(meets)]
+
+    for u in (units - 2, units - 1):
+        out_wait(jnp.int32(u))
+    for u in range(units - NS, units):
+        by_width(jnp.int32(u), lambda w: e_sent(jnp.int32(u), w))
+    for side in (0, 1):
+        for k in range(T - 1):
+
+            @pl.when(rs_sends(side, k))
+            def _():
+                rs_copy(side, k, rs_block(side, k)).wait_send()
+
+    for k in range(len(meets)):
+        g_copy(k).wait_send()
+    for o in range(NDP - 1):
+        for i in range(4):
+            spread_remote(i, o).wait_send()
+        for i in range(2):
+            pair_remote(i, o).wait_send()
+
+    def kv_close(i, carry):
+        d = i + 1
+
+        @pl.when((d <= c) & (d < kvs.shape[0]))
+        def _():
+            kv_copy(d).wait_send()
+
+        return carry
+
+    lax.fori_loop(0, min(NC - 1, kvs.shape[0] - 1), kv_close, 0)
+
+
+def tail_call(
+    layer_in, middle_delta, norm_gains, gain_sums, query, heads_delta, log_totals, row_delta, cosine, sine,
+    keys, values, rows_one, w_query, w_key, w_value, rows, branch, attn, heads, gate, up, hidden,
+):
+    T, NC, NDP = lax.axis_size("tp"), lax.axis_size("ctx"), lax.axis_size("dp")
+    Lr, D = layer_in.shape
+    R, Hq = query.shape
+    KVd = w_key.shape[1]
+    KH = KVd // HEAD
+    Dh = D // NDP
+    RB = Dh // NC
+    F = gate.shape[1]
+    W = tile_of(F) // 2
+    m = NC.bit_length() - 1
+    NS = max(4, m + 1)
+    tokens = NDP * R
+    kv_slots = min(NC, 4)
+    meets = sum(n.bit_length() - 1 for n in (T, NC, NDP))
+    any_spec = pl.BlockSpec(memory_space=pl.ANY)
+    vm = pl.BlockSpec(memory_space=pltpu.VMEM)
+    sds = jax.ShapeDtypeStruct
+    dma = pltpu.SemaphoreType.DMA
+    return pl.pallas_call(
+        functools.partial(tail_kernel, T, NC, NDP, KH, NS),
+        out_shape=(
+            sds((Lr, D), F32), sds((4, D), F32),
+            sds((RB, F), F32), sds((RB, F), F32), sds((RB, F), F32), sds((RB, Hq), F32),
+            sds((RB, Hq), F32), sds((RB, KVd), F32), sds((RB, KVd), F32),
+        ),
+        in_specs=[vm] * 10 + [any_spec] * 13,
+        out_specs=[vm] * 2 + [any_spec] * 7,
+        scratch_shapes=[
+            pltpu.VMEM((3, tokens, Dh), BF), pltpu.VMEM((2, tokens, 2 * W), BF), pltpu.VMEM((tokens, Hq), BF),
+            pltpu.VMEM((NDP, R, Hq), BF), pltpu.VMEM((NDP, 2, R, KVd), BF),
+            pltpu.VMEM((D, Hq), BF), pltpu.VMEM((D, KVd), BF), pltpu.VMEM((D, KVd), BF),
+            pltpu.VMEM((NS, 2, NC, RB, W), BF),
+            *[pltpu.VMEM((NS, 2, NC >> (k + 1), RB, W), BF) for k in range(m)],
+            pltpu.VMEM((2, 2, RB, W), F32), pltpu.VMEM((R, Hq), F32), pltpu.VMEM((2, 2, R, KVd), BF),
+            pltpu.VMEM((kv_slots, 2, R, KVd), BF), pltpu.VMEM((NC - 1, 2, R, KVd), BF),
+            pltpu.VMEM((T, Lr, D), BF), pltpu.VMEM((T + 1, Lr, D), BF), pltpu.VMEM((2, R, KVd), F32),
+            pltpu.VMEM((meets + 1, 4, D), F32), pltpu.VMEM((meets, 4, D), F32),
+            dma((4,)), dma((2,)), dma((2 * NDP - 1, 4)), dma((2 * (NDP - 1), 2)),
+            dma((NS, 2, NC - 1)), dma((NS, 2, NC - 1)), dma((2, 2)), dma((NC - 1,)), dma((NC - 1,)),
+            dma((2, T - 1)), dma((2, T - 1)), dma((meets,)), dma((meets,)), dma((2, 2)),
+        ],
+        compiler_params=pltpu.CompilerParams(
+            collective_id=1, has_side_effects=True, vmem_limit_bytes=66_000_000
+        ),
+        name="tail",
+    )(
+        layer_in, middle_delta, norm_gains, gain_sums, query, heads_delta, log_totals, row_delta, cosine, sine,
+        keys, values, rows_one, w_query, w_key, w_value, rows, branch, attn, heads, gate, up, hidden,
+    )
+
+
 def rms_scale(values, gain_row):
     return values * lax.rsqrt(jnp.mean(values * values, axis=-1, keepdims=True) + EPS) * gain_row
 
@@ -488,18 +1079,6 @@
     return values * cosine[:, None, :] + turned * (sine_sign * sine_table)[:, None, :]
 
 
-def inner_rows(former, latter):
-    return lax.dot_general(
-        former, latter, (((0,), (0,)), ((), ())), preferred_element_type=jnp.float32
-    )
-
-
-def times_transposed(former, latter):
-    return lax.dot_general(
-        former, latter, (((1,), (1,)), ((), ())), preferred_element_type=jnp.float32
-    )
-
-
 def fetch_weights(query_part, key_part, value_part):
     return (
         lax.all_gather(query_part, "dp", axis=0, tiled=True),
@@ -510,19 +1089,6 @@
 
 def spread_rows(rows_part):
     return lax.all_gather(rows_part, "tp", axis=0, tiled=True)
-
-
-def collect_rows(term_fn, row_total):
-    return lax.psum_scatter(
-        term_fn(jnp.int32(0), row_total * lax.axis_size("tp")).astype(jnp.bfloat16),
-        "tp",
-        scatter_dimension=0,
-        tiled=True,
-    ).astype(jnp.float32)
-
-
-def over_ctx(terms, dim):
-    return lax.psum_scatter(terms.astype(BF), "ctx", scatter_dimension=dim, tiled=True).astype(F32)
 
 
 def shards(layer_in, cotangent, norm_gains, w_query, w_key, w_value, w_out, w_gate, w_up, w_down):
@@ -604,94 +1170,36 @@
     row_delta = jnp.einsum(
         "bkgh,bkgh->kgb", heads_delta, head_rows, preferred_element_type=jnp.float32
     )
-    buffer_zero = jnp.zeros((seq_rows, key_heads, HEAD), jnp.float32)
-    key_buffer = buffer_zero
-    value_buffer = buffer_zero
-    back_key_block = lax.all_gather(key_rot, "ctx", axis=0, tiled=True)
-    back_value_block = lax.all_gather(value_rows, "ctx", axis=0, tiled=True)
-
-    def back_compute_piece():
-        capped, allowed = scores_for(back_key_block)
-        prob_rows = jnp.where(allowed, jnp.exp(capped - log_totals[..., None]), 0.0)
-        value_part = jnp.einsum(
-            "kgbl,bkgh->lkh",
-            prob_rows.astype(jnp.bfloat16),
-            heads_delta,
-            preferred_element_type=jnp.float32,
-        )
-        prob_delta = jnp.einsum(
-            "bkgh,lkh->kgbl", heads_delta, back_value_block, preferred_element_type=jnp.float32
-        )
-        score_grad = prob_rows * (prob_delta - row_delta[..., None]) * (1.0 - (capped / CAP) ** 2)
-        score_half = score_grad.astype(jnp.bfloat16)
-        query_part = (
-            jnp.einsum(
-                "kgbl,lkh->bkgh", score_half, back_key_block, preferred_element_type=jnp.float32
-            )
-            * score_scale
-        )
-        key_part = (
-            jnp.einsum("kgbl,bkgh->lkh", score_half, query_rot, preferred_element_type=jnp.float32)
-            * score_scale
-        )
-        return (query_part, key_part, value_part)
-
-    def back_keep_piece():
-        return (accum_zero, key_buffer, value_buffer)
-
-    query_grad, key_buffer, value_buffer = lax.cond(
-        jnp.int32(0) <= last_pos, back_compute_piece, back_keep_piece
+    heads_here = query_heads
+    input_grad, gain_total, grad_gate, grad_up, down_turned, out_turned, grad_query, grad_key, grad_value = tail_call(
+        layer_in,
+        middle_delta,
+        norm_gains,
+        gain_sums,
+        query_rot.reshape(block_rows, query_heads * HEAD),
+        heads_delta.reshape(block_rows, query_heads * HEAD),
+        log_totals.reshape(heads_here, block_rows),
+        row_delta.reshape(heads_here, block_rows),
+        cosine[:, : HEAD // 2],
+        sine_table[:, : HEAD // 2],
+        key_block.reshape(seq_rows, key_heads * HEAD),
+        value_block.reshape(seq_rows, key_heads * HEAD),
+        rows_one,
+        w_query,
+        w_key,
+        w_value,
+        rows_pair,
+        branch_pair,
+        attn_pair,
+        head_pair,
+        gate_pair,
+        up_pair,
+        hid_pair,
     )
-    key_grad, value_grad = (
-        lax.psum_scatter(
-            key_buffer.astype(jnp.bfloat16), "ctx", scatter_dimension=0, tiled=True
-        ).astype(jnp.float32),
-        lax.psum_scatter(
-            value_buffer.astype(jnp.bfloat16), "ctx", scatter_dimension=0, tiled=True
-        ).astype(jnp.float32),
-    )
-    query_delta = (
-        rotate(query_grad.reshape(block_rows, query_heads, HEAD), cosine, sine_table, -1.0)
-        .astype(jnp.bfloat16)
-        .reshape(block_rows, query_heads * HEAD)
-    )
-    key_delta = (
-        rotate(key_grad, cosine, sine_table, -1.0)
-        .astype(jnp.bfloat16)
-        .reshape(block_rows, key_heads * HEAD)
-    )
-    value_delta = value_grad.astype(jnp.bfloat16).reshape(block_rows, key_heads * HEAD)
-    grad_query = inner_rows(rows_one, query_delta)
-    grad_key = inner_rows(rows_one, key_delta)
-    grad_value = inner_rows(rows_one, value_delta)
-
-    def normed_one_term(row_start, row_count):
-        first_term = times_transposed(query_delta, query_full)
-        second_term = times_transposed(key_delta, key_full)
-        return first_term + second_term + times_transposed(value_delta, value_full)
-
-    normed_delta_one = collect_rows(normed_one_term, local_rows)
-    unused_zero, back_zero = jax.vjp(rms_scale, input_float, norm_gains[0])
-    input_delta, gain_zero = back_zero(normed_delta_one)
-    input_grad = middle_delta + input_delta
-    gain_terms = jnp.concatenate([gain_zero[None], gain_sums])
-    gain_grads = lax.psum_scatter(gain_terms, ("dp", "ctx", "tp"), scatter_dimension=1, tiled=True)
-    summed = (
-        lax.psum_scatter(
-            grad_query.astype(jnp.bfloat16), ("dp", "ctx"), scatter_dimension=0, tiled=True
-        ).astype(jnp.float32),
-        lax.psum_scatter(
-            grad_key.astype(jnp.bfloat16), ("dp", "ctx"), scatter_dimension=0, tiled=True
-        ).astype(jnp.float32),
-        lax.psum_scatter(
-            grad_value.astype(jnp.bfloat16), ("dp", "ctx"), scatter_dimension=0, tiled=True
-        ).astype(jnp.float32),
-        over_ctx(inner_rows(head_pair, attn_pair), 1),
-        over_ctx(inner_rows(rows_pair, gate_pair), 0),
-        over_ctx(inner_rows(rows_pair, up_pair), 0),
-        over_ctx(inner_rows(hid_pair, branch_pair), 1),
-    )
-    grad_query, grad_key, grad_value, grad_out, grad_gate, grad_up, grad_down = summed
+    grad_down, grad_out = down_turned.T, out_turned.T
+    ranks = (lax.axis_index("dp") * ctx_count + lax.axis_index("ctx")) * tp_count + lax.axis_index("tp")
+    gain_width = gain_total.shape[1] // (lax.axis_size("dp") * ctx_count * tp_count)
+    gain_grads = lax.dynamic_slice_in_dim(gain_total, ranks * gain_width, gain_width, 1)
     return (
         layer_out,
         input_grad,

time: 880 us -> 581 us (0.66)
  waiting for transfers between devices: 468 us -> 122 us
  Pallas kernels: 191 us -> 385 us
  matrix products: 91.8 us -> 17.9 us
  blocking collectives: 40.7 us -> 0 us
  other arithmetic: 40 us -> 10.5 us
    reduce_scatter x10 -> x0, waiting for transfers between devices: 344 us -> none  [the longest x4 143 us: over_ctx(): lax.psum_scatter(terms.astype(BF), 'ctx', scatter_dimension=dim, tiled=True)]
    pallas_call x0 -> x1, Pallas kernels: none -> 194 us  [tail_call(): pl.pallas_call(functools.partial(tail_kernel, T, NC, NDP, KH, NS), out_sh...]
    dot_general x14 -> x0, matrix products: 67.4 us -> none  [the longest x7 41.2 us: inner_rows(): lax.dot_general(former, latter, (((0,), (0,)), ((), ())), preferred_eleme...]
    unnamed x1 -> x0, blocking collectives: 40.7 us -> none
    convert_element_type x10 -> x1, other arithmetic: 18.5 us -> 0.89 us  [shards(): (accumulated / jnp.transpose(totals, (2, 0, 1))[..., None]).astype(jnp.bf...]
    all_gather x1, waiting for transfers between devices: 28.8 us -> 16.7 us  [shards(): value_block = lax.all_gather(value_rows, 'ctx', axis=0, tiled=True)]
    unnamed x38 -> x40, local copies, waits for them, and re-layouts: 8.27 us -> 18 us
  transfers between devices with their start and end apart: 16 -> 6, of which waited for: 15 -> 6; matrix products, arithmetic and copies ran while one was open for 11% -> 4% of each run, Pallas kernels for 0% -> 0%
where the time goes in v2:
time: 581 us; the launch traced here: 580 us
  Pallas kernels  385 us (66%)
  waiting for transfers between devices  122 us (21%)
  local copies, waits for them, and re-layouts  28.6 us (5%)
  matrix products  17.9 us (3%)
  between operations  15 us (3%)
  other arithmetic  10.5 us (2%)
    pallas_call x1, Pallas kernels, tail_call(): pl.pallas_call(functools.partial(tail_kernel, T, NC, NDP, KH, NS), out_sh...  194 us
    pallas_call x1, Pallas kernels, core_call(): pl.pallas_call(functools.partial(core_kernel, T, C, NDP), out_shape=(sds(...  191 us
    all_gather x1, waiting for transfers between devices, spread_rows(): return lax.all_gather(rows_part, 'tp', axis=0, tiled=True)  53.3 us
    all_gather x1, waiting for transfers between devices, shards(): key_block = lax.all_gather(key_rot, 'ctx', axis=0, tiled=True)  28.8 us
    unnamed x40, local copies, waits for them, and re-layouts  18 us
    all_gather x1, waiting for transfers between devices, shards(): value_block = lax.all_gather(value_rows, 'ctx', axis=0, tiled=True)  16.7 us
  transfers between devices with their start and end apart: 6, of which 6 were waited for; matrix products, arithmetic and copies ran while one was open for 4% of the time, Pallas kernels for 0%

profile of v2, /device:TPU:0, one launch (start us, length us, event | category | flops | bytes accessed | tf_op | source)
XLA Modules:
  0.0 579.9 jit_solution(13460462164374031044)
XLA Ops:
  7.2 0.0 all-gather.15.cloned.1.call-start
  7.2 0.7 all-gather.15.cloned.1.call-update
  7.9 0.0 all-gather.9.cloned.1.call-start
  8.0 0.8 slice_reduce_fusion
  8.8 1.3 fusion.16
  10.0 2.1 fusion.18
  12.1 0.0 all-gather.11.cloned.1.call-start
  12.2 0.7 all-gather.11.cloned.1.call-update
  12.9 0.0 all-gather.13.cloned.1.call-start
  12.9 0.5 all-gather.13.cloned.1.call-update
  13.5 0.0 all-gather.19.cloned.1.call-start
  13.5 8.0 %all-gather.15.cloned.1.call-done = bf16[2304,256]{1,0:T(8,128)(2,1)} async-done(((bf16[1152,256]{1,0:T(8,128)(2,1)}), bf16[2304,256]{1,0:T(8,128)(2,1)}) %all-gather.15.cloned.1.call-update) | async-done | bytes 1179664 | tf_op jit(solution)/shard_map/all_gather | solution.py:1086
  21.5 53.3 %all-gather.9.cloned.1.call-done.rows1_ref = bf16[512,2304]{1,0:T(8,128)(2,1)} async-done(((bf16[128,2304]{1,0:T(8,128)(2,1)}), bf16[512,2304]{1,0:T(8,128)(2,1)}) %all-gather.9.cloned.1.call-update) | async-done | bytes 2359312 | tf_op jit(solution)/shard_map/all_gather | solution.py:1091
  74.8 3.5 convolution_convert_fusion
  78.3 0.0 all-gather.17.cloned.1.call-start
  78.4 0.6 slice.18
  79.7 1.0 multiply_cosine_fusion
  80.7 3.7 all-gather.11.cloned.1.call-done
  84.4 2.8 fusion.28
  87.2 0.9 pad_maximum_fusion
  88.1 9.8 %all-gather.13.cloned.1.call-done = bf16[2304,512]{1,0:T(8,128)(2,1)} async-done(((bf16[1152,512]{1,0:T(8,128)(2,1)}), bf16[2304,512]{1,0:T(8,128)(2,1)}) %all-gather.13.cloned.1.call-update) | async-done | bytes 2359312 | tf_op jit(solution)/shard_map/all_gather | solution.py:1084
  98.0 3.8 fusion.29
  101.8 0.4 mul.135
  102.1 0.1 copy.40
  102.2 1.3 copy.27
  103.5 1.3 copy.23
  104.8 1.0 fusion.26
  105.9 1.2 copy.37
  107.1 1.3 copy.38
  108.4 0.1 fusion.27
  108.5 0.1 fusion.21
  108.6 0.1 copy.39
  108.7 1.0 copy-done.3
  109.7 0.2 fusion.20
  109.9 0.2 copy-done.2
  110.1 1.1 add_convert_fusion.q_ref
  111.2 16.7 %all-gather.19.cloned.1.call-done.v_ref = bf16[2048,256]{1,0:T(8,128)(2,1)} async-done(((bf16[512,256]{1,0:T(8,128)(2,1)}), bf16[2048,256]{1,0:T(8,128)(2,1)}) %all-gather.19.cloned.1.call-update) | async-done | bytes 1048592 | tf_op jit(solution)/shard_map/all_gather | solution.py:1145
  127.9 28.8 %all-gather.17.cloned.1.call-done.k_ref = bf16[2048,256]{1,0:T(8,128)(2,1)} async-done(((bf16[512,256]{1,0:T(8,128)(2,1)}), bf16[2048,256]{1,0:T(8,128)(2,1)}) %all-gather.17.cloned.1.call-update) | async-done | bytes 1048592 | tf_op jit(solution)/shard_map/all_gather | solution.py:1144
  156.7 9.4 %conditional.1 = (f32[512,1,2,256]{3,0,2,1:T(8,128)S(1)}, f32[1,2,512]{2,1,0:T(2,128)}, f32[2,512]{1,0:T(2,128)S(1)}) conditional(s32[]{:T(128)} %bitcast.14, () %tuple.18, (s32[512]{0:T(512)S(1)}, bf16[2048,1,256]{2,0,1:T(8,128)(2,1)}, bf16[512,1,2,256]{3,0,2,1:T(8,128)(2,1)S(1)}, bf16[2048,1,256]{2,0,1:T(8,128)(2,1)}) %tuple.45), branch_computations={%region_1.0_spmd, %region_2.4_spmd} | conditional | flops 2165308416 | bytes 27801652 | solution.py:1159
  156.7 0.8 iota_compare_fusion
  157.6 4.9 fusion
  162.5 2.9 fusion.6
  165.4 0.7 log.8
  166.1 1.0 copy-done
  167.1 0.9 divide_convert_fusion
  168.0 0.5 copy.26
  168.5 1.1 reshape_reshape.2.heads_ref
  169.7 190.8 %core.1 = (bf16[128,2304]{1,0:T(8,128)(2,1)}, f32[128,2304]{1,0:T(8,128)}, f32[3,2304]{1,0:T(4,128)}, bf16[4,4,32,512]{3,2,1,0:T(8,128)(2,1)}, bf16[2,4,4,32,115...) custom-call(bf16[128,2304]{1,0:T(8,128)(2,1)} %x_ref.3, ...), custom_call_target="tpu_custom_call" | custom-call | tf_op jit(solution)/shard_map/core/pallas_call | solution.py:439
  360.5 1.3 reshape.183
  361.7 0.4 bitcast_convert_fusion
  362.1 1.6 multiply_reduce_fusion.rdelta_ref
  363.8 194.5 %tail.1 = (f32[128,2304]{1,0:T(8,128)}, f32[4,2304]{1,0:T(4,128)}, f32[288,2304]{1,0:T(8,128)}, f32[288,2304]{1,0:T(8,128)}, f32[288,2304]{1,0:T(8,128)}, /*inde...) custom-call(bf16[128,2304]{1,0:T(8,128)(2,1)} %x_ref.3, ...), custom_call_target="tpu_custom_call" | custom-call | tf_op jit(solution)/shard_map/tail/pallas_call | solution.py:1030
  558.3 1.4 constant_dynamic-slice_fusion
  559.7 0.8 copy.57
  560.5 2.5 copy.58
  563.0 0.8 copy.59
  563.8 0.7 copy.60
  564.6 0.7 copy.61
  565.3 0.8 copy.62
  566.1 1.5 copy.63
  567.6 1.2 copy-done.5
  568.8 1.5 copy.64
  570.3 1.2 copy-done.4
  571.5 1.5 copy.65
  (33 shorter events, 0.2 us)
Async XLA Ops:
  7.2 14.3 %all-gather.15.cloned.1.call-start = ((), (), s32[]{:S(2)}) async-start(), calls=%async_computation.3 | async-start | bytes 1769472 | tf_op jit(solution)/shard_map/all_gather | solution.py:1086
  7.9 66.9 %all-gather.9.cloned.1.call-start = ((), (), s32[]{:S(2)}) async-start(), calls=%async_computation | async-start | bytes 2949120 | tf_op jit(solution)/shard_map/all_gather | solution.py:1091
  12.1 72.3 %all-gather.11.cloned.1.call-start = ((), (), s32[]{:S(2)}) async-start(), calls=%async_computation.1 | async-start | bytes 1769472 | tf_op jit(solution)/shard_map/all_gather | solution.py:1085
  12.9 85.1 %all-gather.13.cloned.1.call-start = ((), (), s32[]{:S(2)}) async-start(), calls=%async_computation.2 | async-start | bytes 3538944 | tf_op jit(solution)/shard_map/all_gather | solution.py:1084
  13.5 114.5 %all-gather.19.cloned.1.call-start = ((), (), s32[]{:S(2)}) async-start(), calls=%async_computation.5 | async-start | bytes 1310720 | tf_op jit(solution)/shard_map/all_gather | solution.py:1145
  78.3 78.4 %all-gather.17.cloned.1.call-start = ((), (), s32[]{:S(2)}) async-start(), calls=%async_computation.4 | async-start | bytes 1310720 | tf_op jit(solution)/shard_map/all_gather | solution.py:1144
  80.6 6.6 %copy-start.7 = (f32[512,128]{1,0:T(8,128)}, f32[512,128]{1,0:T(8,128)S(1)}, u32[]{:S(2)}) copy-start(f32[512,128]{1,0:T(8,128)S(1)} %get-tuple-element.80.cos_ref) | copy-start | bytes 786436
  80.7 6.6 %copy-start.8 = (f32[512,128]{1,0:T(8,128)}, f32[512,128]{1,0:T(8,128)S(1)}, u32[]{:S(2)}) copy-start(f32[512,128]{1,0:T(8,128)S(1)} %get-tuple-element.81.sin_ref) | copy-start | bytes 786436
  108.5 1.2 copy-start.3
  108.7 1.4 copy-start.2
  157.6 5.0 copy-start.9
  166.1 1.0 copy-start
  360.5 1.6 copy-start.1
  363.8 195.9 %copy-start.10 = (bf16[128,2304]{1,0:T(8,128)(2,1)S(1)}, bf16[128,2304]{1,0:T(8,128)(2,1)}, u32[]{:S(2)}) copy-start(bf16[128,2304]{1,0:T(8,128)(2,1)} %get-tuple-element.98) | copy-start | bytes 1769476
  558.3 4.7 copy-start.12
  559.7 4.2 copy-start.14
  559.7 4.9 copy-start.13
  560.5 4.8 copy-start.11
  560.5 5.6 copy-start.6
  566.1 2.7 copy-start.5
  568.8 2.7 copy-start.4
Sparse Core Ops, SparseCore 0:
  9.5 11.9 all-gather.14
  23.6 51.1 all-gather.8
  76.4 7.9 all-gather.10
  85.8 12.1 all-gather.12
  100.2 27.6 all-gather.18
  130.2 26.4 all-gather.16

commit v3 on v2

--- a/solution.py
+++ b/solution.py
@@ -469,6 +469,281 @@
     )
 
 
+def front_kernel(
+    T, NC, NDP, KH, C,
+    x_ref, gain_ref, freq_ref, wq_ref, wk_ref, wv_ref,
+    q_o, heads_o, logt_o, cos_o, sin_o, kv_o, rows1_o,
+    X, WQ, WK, WV, KV, turned_sum, totals,
+    w_sem, ag_send, ag_recv, pair_sem, kv_send, kv_recv, out_sem,
+):
+    t, c, dp = lax.axis_index("tp"), lax.axis_index("ctx"), lax.axis_index("dp")
+    Lr, D = x_ref.shape
+    R, Hq = q_o.shape
+    rc = Lr // C
+    KVd = KH * HEAD
+    GS = Hq // KVd
+    Dh = D // NDP
+    scale = HEAD**-0.5
+    has_left, has_right = t > 0, t < T - 1
+
+    def remote(src, dst, send, recv, axis, index):
+        return pltpu.make_async_remote_copy(
+            src, dst, send, recv, device_id={axis: index}, device_id_type=MESH
+        )
+
+    partners = [lax.rem(dp + o, NDP) for o in range(1, NDP)]
+    peers = [("tp", lax.rem(t + o, T)) for o in range(1, T)]
+    peers += [("ctx", lax.rem(c + o, NC)) for o in range(1, NC)]
+    peers += [("dp", p) for p in partners]
+    sem = pltpu.get_barrier_semaphore()
+    for axis, index in peers:
+        pl.semaphore_signal(sem, inc=1, device_id={axis: index}, device_id_type=MESH)
+    pl.semaphore_wait(sem, len(peers))
+
+    rows_at = pl.ds(pl.multiple_of(dp * Dh, 128), Dh)
+    weights = [(wq_ref, WQ), (wk_ref, WK), (wv_ref, WV)]
+
+    def weight_local(i):
+        return pltpu.make_async_copy(weights[i][0], weights[i][1].at[rows_at], w_sem.at[0, i])
+
+    def weight_remote(i, o):
+        return remote(
+            weights[i][0], weights[i][1].at[rows_at], w_sem.at[1 + 2 * o, i], w_sem.at[2 + 2 * o, i],
+            "dp", partners[o],
+        )
+
+    for i in range(3):
+        weight_local(i).start()
+        for o in range(NDP - 1):
+            weight_remote(i, o).start()
+
+    def ag_copy(s, side, k, j):
+        at = pl.ds(s * rc, rc)
+        peer = jnp.minimum(t + 1, T - 1) if side == 0 else jnp.maximum(t - 1, 0)
+        return remote(X.at[j, at], X.at[j, at], ag_send.at[s, side, k], ag_recv.at[s, side, k], "tp", peer)
+
+    def ag_block(side, k):
+        return (t - k) if side == 0 else (t + k)
+
+    def ag_there(side, k):
+        return (t >= k) if side == 0 else (t + k <= T - 1)
+
+    def onward(side):
+        return has_right if side == 0 else has_left
+
+    rows = x_ref[...].astype(F32)
+    X[t] = (rows * inverse_rms(rows) * gain_ref[0:1]).astype(BF)
+    for s in range(C):
+        for side in (0, 1):
+
+            @pl.when(onward(side))
+            def _():
+                ag_copy(s, side, 0, t).start()
+
+    position = (c * R + lax.broadcasted_iota(jnp.int32, (R, HEAD // 2), 0)).astype(F32)
+    angles = position * freq_ref[...]
+    cos_o[...] = jnp.cos(angles)
+    sin_o[...] = jnp.sin(angles)
+    for i in range(3):
+        weight_local(i).wait()
+        for o in range(NDP - 1):
+            weight_remote(i, o).wait_recv()
+
+    def kv_copy(d, j):
+        return remote(
+            KV.at[c, j], KV.at[c, j], kv_send.at[d - 1, j], kv_recv.at[d - 1, j],
+            "ctx", jnp.minimum(c + d, NC - 1),
+        )
+
+    def kv_from(b, j):
+        d = c - b
+        return remote(KV.at[b, j], KV.at[b, j], kv_send.at[d - 1, j], kv_recv.at[d - 1, j], "ctx", c)
+
+    def pair_copies(j):
+        def half(owner):
+            return X.at[j, :, pl.ds(pl.multiple_of(owner * Dh, 128), Dh)]
+
+        copies = [pltpu.make_async_copy(half(dp), rows1_o.at[dp, j], pair_sem.at[0, j])]
+        for o, partner in enumerate(partners):
+            copies.append(
+                remote(
+                    half(partner), rows1_o.at[dp, j], pair_sem.at[1 + 2 * o, j], pair_sem.at[2 + 2 * o, j],
+                    "dp", partner,
+                )
+            )
+        return copies
+
+    def turned(values, h, at):
+        a, b = values[:, h * HEAD:h * HEAD + HEAD // 2], values[:, h * HEAD + HEAD // 2:(h + 1) * HEAD]
+        cosine, sine = cos_o[at], sin_o[at]
+        return jnp.concatenate([a * cosine - b * sine, b * cosine + a * sine], axis=1).astype(BF)
+
+    def project(j):
+        for copy in pair_copies(j):
+            copy.start()
+        at = pl.ds(pl.multiple_of(j * Lr, Lr), Lr)
+        values = dot_nn(X[j], WK[...])
+        for kh in range(KH):
+            KV[c, j, 0, :, kh * HEAD:(kh + 1) * HEAD] = turned(values, kh, at)
+        KV[c, j, 1] = dot_nn(X[j], WV[...]).astype(BF)
+
+        def push(i, carry):
+            @pl.when(c + 1 + i <= NC - 1)
+            def _():
+                kv_copy(i + 1, j).start()
+
+            return carry
+
+        lax.fori_loop(0, NC - 1, push, 0)
+        values = dot_nn(X[j], WQ[...])
+        for h in range(Hq // HEAD):
+            q_o[at, h * HEAD:(h + 1) * HEAD] = turned(values, h, at)
+
+    def gather(k, carry):
+        for side in (0, 1):
+
+            @pl.when(ag_there(side, k) & (k > 0))
+            def _():
+                for s in range(C):
+                    ag_copy(s, side, k - 1, ag_block(side, k)).wait_recv()
+
+                    @pl.when(onward(side) & (k <= T - 2))
+                    def _():
+                        ag_copy(s, side, k, ag_block(side, k)).start()
+
+        for side in (0, 1):
+
+            @pl.when(ag_there(side, k) & ((k > 0) | (side == 0)))
+            def _():
+                project(ag_block(side, k))
+
+        return carry
+
+    lax.fori_loop(0, T, gather, 0)
+
+    per = max(1, 256 // Lr)
+    tile = per * Lr
+    turned_sum[...] = jnp.zeros_like(turned_sum)
+    totals[...] = jnp.zeros_like(totals)
+
+    def out_copy(b):
+        return pltpu.make_async_copy(KV.at[b], kv_o.at[b], out_sem.at[b])
+
+    def key_step(b, p, masked):
+        for kh in range(KH):
+            cols = slice(kh * HEAD, (kh + 1) * HEAD)
+            keys = KV[b, pl.ds(p * per, per), 0, :, cols].reshape(tile, HEAD)
+            values = KV[b, pl.ds(p * per, per), 1, :, cols].reshape(tile, HEAD)
+            for g in range(GS):
+                h = kh * GS + g
+                scores = dot_nt(keys, q_o[:, h * HEAD:(h + 1) * HEAD])
+                weights = jnp.exp(CAP * jnp.tanh(scores * (scale / CAP)))
+                if masked:
+                    key_pos = p * tile + lax.broadcasted_iota(jnp.int32, weights.shape, 0)
+                    allowed = key_pos <= lax.broadcasted_iota(jnp.int32, weights.shape, 1)
+                    weights = jnp.where(allowed, weights, 0.0)
+                totals[h:h + 1] += jnp.sum(weights, axis=0, keepdims=True)
+                turned_sum[h] += dot_tn(values, weights.astype(BF))
+
+    def own_step(p, carry):
+        key_step(c, p, True)
+        return carry
+
+    out_copy(c).start()
+    lax.fori_loop(0, T // per, own_step, 0)
+
+    def far_block(i, carry):
+        @pl.when(i < c)
+        def _():
+            b = c - 1 - i
+            for j in range(T):
+                kv_from(b, j).wait_recv()
+            out_copy(b).start()
+
+            def far_step(p, carry):
+                key_step(b, p, False)
+                return carry
+
+            lax.fori_loop(0, T // per, far_step, 0)
+
+        return carry
+
+    lax.fori_loop(0, NC - 1, far_block, 0)
+    for h in range(Hq // HEAD):
+        heads_o[:, h * HEAD:(h + 1) * HEAD] = (turned_sum[h] / totals[h:h + 1]).T.astype(BF)
+    logt_o[...] = jnp.log(totals[...])
+
+    for i in range(3):
+        for o in range(NDP - 1):
+            weight_remote(i, o).wait_send()
+    for s in range(C):
+        for side in (0, 1):
+            for k in range(T - 1):
+
+                @pl.when(ag_there(side, k) & onward(side))
+                def _():
+                    ag_copy(s, side, k, ag_block(side, k)).wait_send()
+
+    for j in range(T):
+        copies = pair_copies(j)
+        copies[0].wait()
+        for copy in copies[1:]:
+            copy.wait()
+
+    def close(i, carry):
+        @pl.when(c + 1 + i <= NC - 1)
+        def _():
+            for j in range(T):
+                kv_copy(i + 1, j).wait_send()
+
+        return carry
+
+    lax.fori_loop(0, NC - 1, close, 0)
+
+    def close_out(b, carry):
+        @pl.when(b <= c)
+        def _():
+            out_copy(b).wait()
+
+        return carry
+
+    lax.fori_loop(0, NC, close_out, 0)
+
+
+def front_call(layer_in, norm_gains, frequency, w_query, w_key, w_value):
+    T, NC, NDP = lax.axis_size("tp"), lax.axis_size("ctx"), lax.axis_size("dp")
+    C = T
+    Lr, D = layer_in.shape
+    R = T * Lr
+    Hq, KVd = w_query.shape[1], w_key.shape[1]
+    Dh = D // NDP
+    H = Hq // HEAD
+    any_spec = pl.BlockSpec(memory_space=pl.ANY)
+    vm = pl.BlockSpec(memory_space=pltpu.VMEM)
+    sds = jax.ShapeDtypeStruct
+    dma = pltpu.SemaphoreType.DMA
+    return pl.pallas_call(
+        functools.partial(front_kernel, T, NC, NDP, KVd // HEAD, C),
+        out_shape=(
+            sds((R, Hq), BF), sds((R, Hq), BF), sds((H, R), F32),
+            sds((R, HEAD // 2), F32), sds((R, HEAD // 2), F32),
+            sds((NC, T, 2, Lr, KVd), BF), sds((NDP, T, Lr, Dh), BF),
+        ),
+        in_specs=[vm] * 3 + [any_spec] * 3,
+        out_specs=[vm] * 5 + [any_spec] * 2,
+        scratch_shapes=[
+            pltpu.VMEM((T, Lr, D), BF), pltpu.VMEM((D, Hq), BF), pltpu.VMEM((D, KVd), BF), pltpu.VMEM((D, KVd), BF),
+            pltpu.VMEM((NC, T, 2, Lr, KVd), BF), pltpu.VMEM((H, HEAD, R), F32), pltpu.VMEM((H, R), F32),
+            dma((2 * NDP - 1, 3)), dma((C, 2, T - 1)), dma((C, 2, T - 1)), dma((2 * NDP - 1, T)),
+            dma((NC - 1, T)), dma((NC - 1, T)), dma((NC,)),
+        ],
+        compiler_params=pltpu.CompilerParams(
+            collective_id=2, has_side_effects=True, vmem_limit_bytes=66_000_000
+        ),
+        name="front",
+    )(layer_in, norm_gains, frequency, w_query, w_key, w_value)
+
+
 def flip(index, bit):
     return index + bit * (1 - 2 * lax.rem(index // bit, 2))
 
@@ -499,8 +774,8 @@
 
 def tail_kernel(
     T, NC, NDP, KH, NS,
-    x_ref, mdelta_ref, gain_ref, gsum_ref, q_ref, hd_ref, logt_ref, rdelta_ref, cos_ref, sin_ref,
-    k_ref, v_ref, rows1_ref, wq_ref, wk_ref, wv_ref,
+    x_ref, mdelta_ref, gain_ref, gsum_ref, q_ref, hd_ref, heads_ref, logt_ref, cos_ref, sin_ref,
+    kv_ref, rows1_ref, wq_ref, wk_ref, wv_ref,
     rows_ref, branch_ref, attn_ref, head_ref, gate_ref, up_ref, hid_ref,
     igrad_ref, gains_ref, gate_o, up_o, down_o, out_o, q_o, k_o, v_o,
     L, Rc, Hd, RQ, RKV, WQ, WK, WV, Pe, *rest,
@@ -508,7 +783,7 @@
     m = NC.bit_length() - 1
     Rv, rest = rest[:m], rest[m:]
     (
-        st, dq, kvb, kvs, kvr, Pb, Rb, acc, G, GR,
+        st, dq, rdelta, kvb, kvs, kvr, Pb, Rb, acc, G, GR,
         l_sem, r_sem, w_sem, pair_sem, e_send, e_recv, st_sem, kv_send, kv_recv,
         rs_send, rs_recv, g_send, g_recv, kvb_sem,
     ) = rest
@@ -542,15 +817,10 @@
     firsts = [rows_ref, branch_ref, attn_ref]
 
     def first_copy(i):
-        return pltpu.make_async_copy(firsts[i], L.at[i % 2], l_sem.at[i])
-
-    def half_of(ref, owner):
-        return ref.at[:, pl.ds(pl.multiple_of(owner * Dh, 128), Dh)]
+        return pltpu.make_async_copy(firsts[i], L.at[i % 2], l_sem.at[i % 2])
 
     rows_at = pl.ds(pl.multiple_of(dp * Dh, 128), Dh)
-    token_at = pl.ds(pl.multiple_of(dp * R, 128), R)
     spread = [
-        (lambda owner: half_of(rows1_ref, owner), L.at[2, token_at]),
         (lambda owner: wq_ref, WQ.at[rows_at]),
         (lambda owner: wk_ref, WK.at[rows_at]),
         (lambda owner: wv_ref, WV.at[rows_at]),
@@ -581,12 +851,14 @@
     first_copy(0).start()
     chunk_start(0)
     first_copy(1).start()
-    for i in range(4):
+    for i in range(3):
         spread_local(i).start()
         for o in range(NDP - 1):
             spread_remote(i, o).start()
     head_copy = pltpu.make_async_copy(head_ref, Hd, l_sem.at[3])
     head_copy.start()
+    rows1_copy = pltpu.make_async_copy(rows1_ref, L.at[2], l_sem.at[2])
+    rows1_copy.start()
 
     orders = [bits_below(NC), bits_below(NC)[::-1]]
     first_of = [sum(NC >> (i + 1) for i in range(k)) for k in range(m)]
@@ -646,6 +918,7 @@
 
             @pl.when(u == wide_units + 1)
             def _():
+                rows1_copy.wait()
                 for par in (0, 1):
                     store(par, L[2], RQ[:, :, par * w:(par + 1) * w].reshape(NDP * R, w))
 
@@ -722,7 +995,8 @@
         def _():
             body(narrow)
 
-    key_tile = min(256, R)
+    per = max(1, 256 // Lr)
+    key_tile = per * Lr
 
     def kv_copy(d):
         return remote(
@@ -730,21 +1004,9 @@
             along("ctx", jnp.maximum(c - d, 0)),
         )
 
-    def block_copies(block):
-        at = pl.ds(pl.multiple_of(block * R, 128), R)
+    def block_copy(block):
         two = lax.rem(block, 2)
-        return [
-            pltpu.make_async_copy(ref.at[at], kvb.at[two, i], kvb_sem.at[two, i])
-            for i, ref in enumerate((k_ref, v_ref))
-        ]
-
-    def block_start(block):
-        for copy in block_copies(block):
-            copy.start()
-
-    def block_wait(block):
-        for copy in block_copies(block):
-            copy.wait()
+        return pltpu.make_async_copy(kv_ref.at[block], kvb.at[two], kvb_sem.at[two])
 
     def attend(two, masked, dst):
         for kh in range(KH):
@@ -752,8 +1014,9 @@
 
             def key_step(i, carry):
                 start = pl.multiple_of(i * key_tile, key_tile)
-                at = pl.ds(start, key_tile)
-                keys, values = kvb[two, 0, at, cols], kvb[two, 1, at, cols]
+                at = pl.ds(i * per, per)
+                keys = kvb[two, at, 0, :, cols].reshape(key_tile, HEAD)
+                values = kvb[two, at, 1, :, cols].reshape(key_tile, HEAD)
                 key_sum = jnp.zeros((key_tile, HEAD), F32)
                 value_sum = jnp.zeros((key_tile, HEAD), F32)
                 for g in range(GS):
@@ -765,7 +1028,7 @@
                     if masked:
                         key_pos = start + lax.broadcasted_iota(jnp.int32, prob.shape, 0)
                         prob = jnp.where(key_pos <= lax.broadcasted_iota(jnp.int32, prob.shape, 1), prob, 0.0)
-                    grad = prob * (dot_nt(values, delta) - rdelta_ref[h:h + 1, :]) * (1.0 - bent * bent)
+                    grad = prob * (dot_nt(values, delta) - rdelta[h:h + 1, :]) * (1.0 - bent * bent)
                     grad = grad.astype(BF)
                     value_sum += dot_nn(prob.astype(BF), delta)
                     key_sum += dot_nn(grad, query)
@@ -779,7 +1042,11 @@
 
     def attention():
         dq[...] = jnp.zeros_like(dq)
-        block_start(0)
+        for h in range(Hq // HEAD):
+            head = slice(h * HEAD, (h + 1) * HEAD)
+            product = hd_ref[:, head].astype(F32) * heads_ref[:, head].astype(F32)
+            rdelta[h:h + 1] = jnp.sum(product.T, axis=0, keepdims=True)
+        block_copy(0).start()
 
         def far(block, carry):
             d = c - block
@@ -787,8 +1054,8 @@
             @pl.when(block < c)
             def _():
                 slot = lax.rem(d, kvs.shape[0])
-                block_wait(block)
-                block_start(block + 1)
+                block_copy(block).wait()
+                block_copy(block + 1).start()
 
                 @pl.when(d + kvs.shape[0] <= c)
                 def _():
@@ -805,7 +1072,7 @@
         def _():
             kv_copy(kvs.shape[0]).wait_send()
 
-        block_wait(c)
+        block_copy(c).wait()
         attend(lax.rem(c, 2), True, 0)
 
     def turned(values, h):
@@ -875,7 +1142,7 @@
         for i in range(2):
             for o in range(NDP - 1):
                 pair_remote(i, o).start()
-        for i in range(4):
+        for i in range(3):
             spread_local(i).wait()
             for o in range(NDP - 1):
                 spread_remote(i, o).wait_recv()
@@ -988,7 +1255,7 @@
     for k in range(len(meets)):
         g_copy(k).wait_send()
     for o in range(NDP - 1):
-        for i in range(4):
+        for i in range(3):
             spread_remote(i, o).wait_send()
         for i in range(2):
             pair_remote(i, o).wait_send()
@@ -1006,8 +1273,8 @@
 
 
 def tail_call(
-    layer_in, middle_delta, norm_gains, gain_sums, query, heads_delta, log_totals, row_delta, cosine, sine,
-    keys, values, rows_one, w_query, w_key, w_value, rows, branch, attn, heads, gate, up, hidden,
+    layer_in, middle_delta, norm_gains, gain_sums, query, heads_delta, head_rows, log_totals, cosine, sine,
+    keys_values, rows_one, w_query, w_key, w_value, rows, branch, attn, heads, gate, up, hidden,
 ):
     T, NC, NDP = lax.axis_size("tp"), lax.axis_size("ctx"), lax.axis_size("dp")
     Lr, D = layer_in.shape
@@ -1034,7 +1301,7 @@
             sds((RB, F), F32), sds((RB, F), F32), sds((RB, F), F32), sds((RB, Hq), F32),
             sds((RB, Hq), F32), sds((RB, KVd), F32), sds((RB, KVd), F32),
         ),
-        in_specs=[vm] * 10 + [any_spec] * 13,
+        in_specs=[vm] * 10 + [any_spec] * 12,
         out_specs=[vm] * 2 + [any_spec] * 7,
         scratch_shapes=[
             pltpu.VMEM((3, tokens, Dh), BF), pltpu.VMEM((2, tokens, 2 * W), BF), pltpu.VMEM((tokens, Hq), BF),
@@ -1042,175 +1309,44 @@
             pltpu.VMEM((D, Hq), BF), pltpu.VMEM((D, KVd), BF), pltpu.VMEM((D, KVd), BF),
             pltpu.VMEM((NS, 2, NC, RB, W), BF),
             *[pltpu.VMEM((NS, 2, NC >> (k + 1), RB, W), BF) for k in range(m)],
-            pltpu.VMEM((2, 2, RB, W), F32), pltpu.VMEM((R, Hq), F32), pltpu.VMEM((2, 2, R, KVd), BF),
+            pltpu.VMEM((2, 2, RB, W), F32), pltpu.VMEM((R, Hq), F32), pltpu.VMEM((Hq // HEAD, R), F32), pltpu.VMEM((2, T, 2, Lr, KVd), BF),
             pltpu.VMEM((kv_slots, 2, R, KVd), BF), pltpu.VMEM((NC - 1, 2, R, KVd), BF),
             pltpu.VMEM((T, Lr, D), BF), pltpu.VMEM((T + 1, Lr, D), BF), pltpu.VMEM((2, R, KVd), F32),
             pltpu.VMEM((meets + 1, 4, D), F32), pltpu.VMEM((meets, 4, D), F32),
-            dma((4,)), dma((2,)), dma((2 * NDP - 1, 4)), dma((2 * (NDP - 1), 2)),
+            dma((4,)), dma((2,)), dma((2 * NDP - 1, 3)), dma((2 * (NDP - 1), 2)),
             dma((NS, 2, NC - 1)), dma((NS, 2, NC - 1)), dma((2, 2)), dma((NC - 1,)), dma((NC - 1,)),
-            dma((2, T - 1)), dma((2, T - 1)), dma((meets,)), dma((meets,)), dma((2, 2)),
+            dma((2, T - 1)), dma((2, T - 1)), dma((meets,)), dma((meets,)), dma((2,)),
         ],
         compiler_params=pltpu.CompilerParams(
             collective_id=1, has_side_effects=True, vmem_limit_bytes=66_000_000
         ),
         name="tail",
     )(
-        layer_in, middle_delta, norm_gains, gain_sums, query, heads_delta, log_totals, row_delta, cosine, sine,
-        keys, values, rows_one, w_query, w_key, w_value, rows, branch, attn, heads, gate, up, hidden,
+        layer_in, middle_delta, norm_gains, gain_sums, query, heads_delta, head_rows, log_totals, cosine, sine,
+        keys_values, rows_one, w_query, w_key, w_value, rows, branch, attn, heads, gate, up, hidden,
     )
 
 
-def rms_scale(values, gain_row):
-    return values * lax.rsqrt(jnp.mean(values * values, axis=-1, keepdims=True) + EPS) * gain_row
-
-
-def rope_tables(positions, head_width):
-    half_width = head_width // 2
-    frequency = THETA ** (-(jnp.arange(half_width, dtype=jnp.float32) * 2.0) / head_width)
-    angles = positions.astype(jnp.float32)[:, None] * frequency[None, :]
-    cosine = jnp.concatenate([jnp.cos(angles), jnp.cos(angles)], axis=1)
-    sine_table = jnp.concatenate([jnp.sin(angles), jnp.sin(angles)], axis=1)
-    return (cosine, sine_table)
-
-
-def rotate(values, cosine, sine_table, sine_sign):
-    half_width = values.shape[-1] // 2
-    turned = jnp.concatenate([-values[..., half_width:], values[..., :half_width]], axis=-1)
-    return values * cosine[:, None, :] + turned * (sine_sign * sine_table)[:, None, :]
-
-
-def fetch_weights(query_part, key_part, value_part):
+def shards(layer_in, cotangent, norm_gains, w_query, w_key, w_value, w_out, w_gate, w_up, w_down):
+    tp_count, ctx_count, dp_count = lax.axis_size("tp"), lax.axis_size("ctx"), lax.axis_size("dp")
+    half_width = HEAD // 2
+    frequency = THETA ** (-(jnp.arange(half_width, dtype=F32) * 2.0) / HEAD)
+    query, head_rows, log_totals, cosine, sine, keys_values, rows_one = front_call(
+        layer_in, norm_gains, frequency[None, :], w_query, w_key, w_value
+    )
+    core = core_call(layer_in, cotangent, norm_gains, head_rows, w_out, w_gate, w_up, w_down)
+    layer_out, middle_delta, gain_sums, heads_delta, rows, hidden, branch, gate, up, attn, heads = core
+    input_grad, gains, grad_gate, grad_up, down_turned, out_turned, grad_query, grad_key, grad_value = tail_call(
+        layer_in, middle_delta, norm_gains, gain_sums, query, heads_delta, head_rows, log_totals, cosine, sine,
+        keys_values, rows_one.reshape(-1, rows_one.shape[-1]), w_query, w_key, w_value,
+        rows, branch, attn, heads, gate, up, hidden,
+    )
+    rank = (lax.axis_index("dp") * ctx_count + lax.axis_index("ctx")) * tp_count + lax.axis_index("tp")
+    width = gains.shape[1] // (dp_count * ctx_count * tp_count)
+    gain_grads = lax.dynamic_slice_in_dim(gains, rank * width, width, 1)
     return (
-        lax.all_gather(query_part, "dp", axis=0, tiled=True),
-        lax.all_gather(key_part, "dp", axis=0, tiled=True),
-        lax.all_gather(value_part, "dp", axis=0, tiled=True),
-    )
-
-
-def spread_rows(rows_part):
-    return lax.all_gather(rows_part, "tp", axis=0, tiled=True)
-
-
-def shards(layer_in, cotangent, norm_gains, w_query, w_key, w_value, w_out, w_gate, w_up, w_down):
-    tp_count = lax.axis_size("tp")
-    ctx_count = lax.axis_size("ctx")
-    local_rows = layer_in.shape[0]
-    block_rows = local_rows * tp_count
-    seq_rows = block_rows * ctx_count
-    positions = lax.axis_index("ctx") * block_rows + jnp.arange(block_rows, dtype=jnp.int32)
-    last_pos = positions[block_rows - 1]
-    cosine, sine_table = rope_tables(positions, HEAD)
-    score_scale = HEAD ** (-0.5)
-    query_full, key_full, value_full = fetch_weights(w_query, w_key, w_value)
-    query_heads = query_full.shape[1] // HEAD
-    key_heads = key_full.shape[1] // HEAD
-    group_size = query_heads // key_heads
-    input_float = layer_in.astype(jnp.float32)
-    normed_one = rms_scale(input_float, norm_gains[0]).astype(jnp.bfloat16)
-    rows_one = spread_rows(normed_one)
-    query_proj = jnp.dot(rows_one, query_full, preferred_element_type=jnp.float32).reshape(
-        block_rows, query_heads, HEAD
-    )
-    query_rot = (
-        rotate(query_proj, cosine, sine_table, 1.0)
-        .astype(jnp.bfloat16)
-        .reshape(block_rows, key_heads, group_size, HEAD)
-    )
-    key_proj = jnp.dot(rows_one, key_full, preferred_element_type=jnp.float32).reshape(
-        block_rows, key_heads, HEAD
-    )
-    key_rot = rotate(key_proj, cosine, sine_table, 1.0).astype(jnp.bfloat16)
-    value_rows = (
-        jnp.dot(rows_one, value_full, preferred_element_type=jnp.float32)
-        .astype(jnp.bfloat16)
-        .reshape(block_rows, key_heads, HEAD)
-    )
-
-    def scores_for(key_block):
-        piece_len = key_block.shape[0]
-        raw_scores = (
-            jnp.einsum("bkgh,lkh->kgbl", query_rot, key_block, preferred_element_type=jnp.float32)
-            * score_scale
-        )
-        capped = CAP * jnp.tanh(raw_scores / CAP)
-        key_pos = jnp.arange(piece_len, dtype=jnp.int32)
-        allowed = key_pos[None, :] <= positions[:, None]
-        return (capped, allowed)
-
-    accum_zero = jnp.zeros((block_rows, key_heads, group_size, HEAD), jnp.float32)
-    totals_zero = jnp.zeros((key_heads, group_size, block_rows), jnp.float32)
-    accumulated = accum_zero
-    totals = totals_zero
-    key_block = lax.all_gather(key_rot, "ctx", axis=0, tiled=True)
-    value_block = lax.all_gather(value_rows, "ctx", axis=0, tiled=True)
-
-    def attend_compute_piece():
-        capped, allowed = scores_for(key_block)
-        exp_scores = jnp.where(allowed, jnp.exp(capped), 0.0)
-        weights = exp_scores.astype(jnp.bfloat16)
-        summed = jnp.einsum(
-            "kgbl,lkh->bkgh", weights, value_block, preferred_element_type=jnp.float32
-        )
-        return (summed, jnp.sum(exp_scores, axis=-1))
-
-    def attend_keep_piece():
-        return (accumulated, totals)
-
-    accumulated, totals = lax.cond(
-        jnp.int32(0) <= last_pos, attend_compute_piece, attend_keep_piece
-    )
-    head_rows = (accumulated / jnp.transpose(totals, (2, 0, 1))[..., None]).astype(jnp.bfloat16)
-    log_totals = jnp.log(totals)
-    head_flat = head_rows.reshape(block_rows, query_heads * HEAD)
-
-    core = core_call(layer_in, cotangent, norm_gains, head_flat, w_out, w_gate, w_up, w_down)
-    layer_out, middle_delta, gain_sums, heads_delta, *pairs = core
-    rows_pair, hid_pair, branch_pair, gate_pair, up_pair, attn_pair, head_pair = pairs
-    heads_delta = heads_delta.reshape(block_rows, key_heads, group_size, HEAD)
-    row_delta = jnp.einsum(
-        "bkgh,bkgh->kgb", heads_delta, head_rows, preferred_element_type=jnp.float32
-    )
-    heads_here = query_heads
-    input_grad, gain_total, grad_gate, grad_up, down_turned, out_turned, grad_query, grad_key, grad_value = tail_call(
-        layer_in,
-        middle_delta,
-        norm_gains,
-        gain_sums,
-        query_rot.reshape(block_rows, query_heads * HEAD),
-        heads_delta.reshape(block_rows, query_heads * HEAD),
-        log_totals.reshape(heads_here, block_rows),
-        row_delta.reshape(heads_here, block_rows),
-        cosine[:, : HEAD // 2],
-        sine_table[:, : HEAD // 2],
-        key_block.reshape(seq_rows, key_heads * HEAD),
-        value_block.reshape(seq_rows, key_heads * HEAD),
-        rows_one,
-        w_query,
-        w_key,
-        w_value,
-        rows_pair,
-        branch_pair,
-        attn_pair,
-        head_pair,
-        gate_pair,
-        up_pair,
-        hid_pair,
-    )
-    grad_down, grad_out = down_turned.T, out_turned.T
-    ranks = (lax.axis_index("dp") * ctx_count + lax.axis_index("ctx")) * tp_count + lax.axis_index("tp")
-    gain_width = gain_total.shape[1] // (lax.axis_size("dp") * ctx_count * tp_count)
-    gain_grads = lax.dynamic_slice_in_dim(gain_total, ranks * gain_width, gain_width, 1)
-    return (
-        layer_out,
-        input_grad,
-        gain_grads,
-        grad_query,
-        grad_key,
-        grad_value,
-        grad_out,
-        grad_gate,
-        grad_up,
-        grad_down,
+        layer_out, input_grad, gain_grads, grad_query, grad_key, grad_value,
+        out_turned.T, grad_gate, grad_up, down_turned.T,
     )
 
 

time: 581 us -> 456 us (0.78)
  waiting for transfers between devices: 122 us -> 0 us
  Pallas kernels: 385 us -> 439 us
  matrix products: 17.9 us -> 0 us
  between operations: 15 us -> 0.71 us
  local copies, waits for them, and re-layouts: 28.6 us -> 14.7 us
  other arithmetic: 10.5 us -> 0.53 us
    all_gather x6 -> x0, waiting for transfers between devices: 120 us -> none  [the longest x1 53.3 us: spread_rows(): return lax.all_gather(rows_part, 'tp', axis=0, tiled=True)]
    pallas_call x0 -> x1, Pallas kernels: none -> 53.6 us  [front_call(): pl.pallas_call(functools.partial(front_kernel, T, NC, NDP, KVd // HEAD, C...]
    dot_general x5 -> x0, matrix products: 17.9 us -> none  [the longest x1 4.94 us: scores_for(): jnp.einsum('bkgh,lkh->kgbl', query_rot, key_block, preferred_element_type...]
    unnamed x40 -> x25, local copies, waits for them, and re-layouts: 18 us -> 13.3 us
  transfers between devices with their start and end apart: 6 -> 0, of which waited for: 6 -> 0; matrix products, arithmetic and copies ran while one was open for 4% -> 0% of each run, Pallas kernels for 0% -> 0%
where the time goes in v3:
time: 456 us; the launch traced here: 455 us
  Pallas kernels  439 us (96%)
  local copies, waits for them, and re-layouts  14.7 us (3%)
    pallas_call x1, Pallas kernels, tail_call(): pl.pallas_call(functools.partial(tail_kernel, T, NC, NDP, KH, NS), out_sh...  198 us
    pallas_call x1, Pallas kernels, core_call(): pl.pallas_call(functools.partial(core_kernel, T, C, NDP), out_shape=(sds(...  188 us
    pallas_call x1, Pallas kernels, front_call(): pl.pallas_call(functools.partial(front_kernel, T, NC, NDP, KVd // HEAD, C...  53.6 us
    unnamed x25, local copies, waits for them, and re-layouts  13.3 us

profile of v3, /device:TPU:0, one launch (start us, length us, event | category | flops | bytes accessed | tf_op | source)
XLA Modules:
  0.0 455.3 jit_solution(13848523858607266682)
XLA Ops:
  0.6 0.5 multiply_power_fusion.freq_ref
  1.2 53.6 %front.1 = (bf16[512,512]{1,0:T(8,128)(2,1)}, bf16[512,512]{1,0:T(8,128)(2,1)}, f32[2,512]{1,0:T(2,128)}, f32[512,128]{1,0:T(8,128)}, f32[512,128]{1,0:T(8,128)}...) custom-call(bf16[128,2304]{1,0:T(8,128)(2,1)} %x_ref.5, f32[4,2304]{1,0:T(4,128)} %gain_ref.5, ...), custom_call_target="tpu_custom_call" | custom-call | tf_op jit(solution)/shard_map/front/pallas_call | solution.py:725
  54.8 187.5 %core.1 = (bf16[128,2304]{1,0:T(8,128)(2,1)}, f32[128,2304]{1,0:T(8,128)}, f32[3,2304]{1,0:T(4,128)}, bf16[4,4,32,512]{3,2,1,0:T(8,128)(2,1)}, bf16[2,4,4,32,115...) custom-call(bf16[128,2304]{1,0:T(8,128)(2,1)} %x_ref.5, ...), custom_call_target="tpu_custom_call" | custom-call | tf_op jit(solution)/shard_map/core/pallas_call | solution.py:439
  242.3 0.0 copy-start.4
  242.3 198.2 %tail.1 = (f32[128,2304]{1,0:T(8,128)}, f32[4,2304]{1,0:T(4,128)}, f32[288,2304]{1,0:T(8,128)}, f32[288,2304]{1,0:T(8,128)}, f32[288,2304]{1,0:T(8,128)}, /*inde...) custom-call(bf16[128,2304]{1,0:T(8,128)(2,1)} %x_ref.5, ...), custom_call_target="tpu_custom_call" | custom-call | tf_op jit(solution)/shard_map/tail/pallas_call | solution.py:1297
  440.5 0.0 copy-start.5
  440.5 0.0 copy-start.7
  440.6 1.4 constant_dynamic-slice_fusion
  442.0 0.0 copy-done.4
  442.0 0.0 copy-start.6
  442.0 0.0 copy-start.3
  442.0 0.8 copy.29
  442.8 0.0 copy-start.2
  442.8 2.5 copy.30
  445.3 0.0 copy-done.5
  445.3 0.8 copy.31
  446.1 0.0 copy-done.7
  446.1 0.7 copy.32
  446.8 0.0 copy-done.6
  446.8 0.7 copy.33
  447.6 0.0 copy-done.3
  447.6 0.8 copy.34
  448.4 0.0 copy-done.2
  448.4 0.0 copy-start.1
  448.4 1.5 copy.35
  449.9 1.2 copy-done.1
  451.1 0.0 copy-start
  451.1 1.5 copy.36
  452.6 1.2 copy-done
  453.8 1.5 copy.37
Async XLA Ops:
  242.3 199.7 %copy-start.4 = (bf16[128,2304]{1,0:T(8,128)(2,1)S(1)}, bf16[128,2304]{1,0:T(8,128)(2,1)}, u32[]{:S(2)}) copy-start(bf16[128,2304]{1,0:T(8,128)(2,1)} %get-tuple-element.74) | copy-start | bytes 1769476
  440.5 4.8 %copy-start.5 = (f32[288,512]{1,0:T(8,128)S(1)}, f32[288,512]{1,0:T(8,128)}, u32[]{:S(2)}) copy-start(f32[288,512]{1,0:T(8,128)} %get-tuple-element.77) | copy-start | bytes 1769476
  440.5 5.6 %copy-start.7 = (f32[288,256]{1,0:T(8,128)S(1)}, f32[288,256]{1,0:T(8,128)}, u32[]{:S(2)}) copy-start(f32[288,256]{1,0:T(8,128)} %get-tuple-element.78) | copy-start | bytes 884740
  442.0 4.9 %copy-start.6 = (f32[288,256]{1,0:T(8,128)S(1)}, f32[288,256]{1,0:T(8,128)}, u32[]{:S(2)}) copy-start(f32[288,256]{1,0:T(8,128)} %get-tuple-element.79) | copy-start | bytes 884740
  442.0 5.6 %copy-start.3 = (f32[288,512]{1,0:T(8,128)S(1)}, f32[288,512]{1,0:T(8,128)}, u32[]{:S(2)}) copy-start(f32[288,512]{1,0:T(8,128)} %get-tuple-element.60) | copy-start | bytes 1769476
  442.8 5.6 %copy-start.2 = (f32[288,2304]{1,0:T(8,128)S(1)}, f32[288,2304]{1,0:T(8,128)}, u32[]{:S(2)}) copy-start(f32[288,2304]{1,0:T(8,128)} %get-tuple-element.81) | copy-start | bytes 7962628
  448.4 2.7 copy-start.1
  451.1 2.7 copy-start

commit v4 on v3

--- a/solution.py
+++ b/solution.py
@@ -53,16 +53,45 @@
     pl.semaphore_wait(sem, count_of)
 
 
+def flip(index, bit):
+    return index + bit * (1 - 2 * lax.rem(index // bit, 2))
+
+
+def flips(index, mask):
+    bit = 1
+    while bit <= mask:
+        if mask & bit:
+            index = flip(index, bit)
+        bit *= 2
+    return index
+
+
+def dot_tn(former, latter):
+    return lax.dot_general(former, latter, (((0,), (0,)), ((), ())), preferred_element_type=F32)
+
+
+def sub_sums(bits):
+    sums = [0]
+    for bit in bits:
+        sums = sums + [s + bit for s in sums]
+    return sums
+
+
+def bits_below(count):
+    return [1 << i for i in range(count.bit_length() - 1)]
+
+
 def core_kernel(
-    T, C, NDP,
+    T, C, NC, NDP,
     x_ref, ct_ref, gain_ref, heads_ref, wo_ref, wg_ref, wu_ref, wd_ref,
     out_ref, mdelta_ref, gsum_ref, hdelta_ref,
-    rows_pair, hid_pair, branch_pair, gate_pair, up_pair, attn_pair, head_pair,
+    rows_pair, hid_pair, branch_pair, gate_pair, up_pair, attn_pair, head_pair, down_o,
     wo_v, wg_v, wu_v, wd_v, X, Pb, Rb, hid, Ab, Bb, att, mid, acc,
-    w_sem, rs_send, rs_recv, ag_send, ag_recv, pair_sem,
+    L, Rc, st, w_sem, rs_send, rs_recv, ag_send, ag_recv, pair_sem, l_sem, e_send, e_recv, st_sem, free_sem,
 ):
     t = lax.axis_index("tp")
     dp = lax.axis_index("dp")
+    c = lax.axis_index("ctx")
     D = x_ref.shape[1]
     rc = x_ref.shape[0] // C
     Dh = D // NDP
@@ -71,10 +100,11 @@
     has_left, has_right = t > 0, t < T - 1
     left, right = {"tp": jnp.maximum(t - 1, 0)}, {"tp": jnp.minimum(t + 1, T - 1)}
     partners = [{"dp": lax.rem(dp + o, NDP)} for o in range(1, NDP)]
+    meets = [{"ctx": flip(c, bit)} for bit in bits_below(NC)]
 
     barrier(
-        has_left.astype(jnp.int32) + has_right.astype(jnp.int32) + (NDP - 1),
-        [(has_left, left), (has_right, right)] + [(t >= 0, p) for p in partners],
+        has_left.astype(jnp.int32) + has_right.astype(jnp.int32) + len(partners + meets),
+        [(has_left, left), (has_right, right)] + [(t >= 0, p) for p in partners + meets],
     )
 
     rows_at = pl.ds(pl.multiple_of(dp * Dh, 128), Dh)
@@ -144,12 +174,12 @@
         for copy in pair_of(kind, s):
             copy.start()
 
-    def pair_sent(kind, s):
-        for o, copy in enumerate(pair_of(kind, s)):
-            if o == 0:
-                copy.wait()
-            else:
-                copy.wait_send()
+    def pair_kept(kind, s):
+        pair_of(kind, s)[0].wait()
+
+    def pair_away(kind, s):
+        for copy in pair_of(kind, s)[1:]:
+            copy.wait_send()
 
     def pair_received(kind, s):
         for copy in pair_of(kind, s)[1:]:
@@ -313,6 +343,117 @@
 
     def store_part(s, at, tile, value):
         Pb[s, :, :, at] = value.astype(BF).reshape(T, rc, tile)
+
+    m = NC.bit_length() - 1
+    RB = Dh // NC
+    W = Rc.shape[-1] // 2
+    units = F // (2 * W)
+    begin = 3 * C - 1
+    pitch = -(-RB // 16) * 16
+    orders = [bits_below(NC), bits_below(NC)[::-1]]
+    first_of = [sum(NC >> (i + 1) for i in range(k)) for k in range(m)]
+
+    def block_of(ref, i):
+        down = ref.shape[0] // pitch
+        row = pl.multiple_of(lax.rem(i, down) * pitch, 16)
+        return ref.at[pl.ds(row, RB), pl.ds(pl.multiple_of((i // down) * W, 128), W)]
+
+    def part_of(u, par, owner):
+        return block_of(wd_v, (u * 2 + par) * NC + owner)
+
+    def came_of(u, par, at):
+        return block_of(wu_v, (u * 2 + par) * (NC - 1) + at)
+
+    def e_copy(u, par, k, n):
+        order = orders[par]
+        at = first_of[k] + n
+        return pltpu.make_async_remote_copy(
+            part_of(u, par, flips(c, sub_sums(order[k + 1:])[n] + order[k])), came_of(u, par, at),
+            e_send.at[u, par, at], e_recv.at[u, par, at],
+            device_id={"ctx": flip(c, order[k])}, device_id_type=MESH,
+        )
+
+    def e_each(u, k, act):
+        for par in (0, 1):
+            for n in range(NC >> (k + 1)):
+                act(par, n)
+
+    def e_add(u, k):
+        def one(par, n):
+            e_copy(u, par, k, n).wait_recv()
+            if k < m - 1:
+                ref = part_of(u, par, flips(c, sub_sums(orders[par][k + 1:])[n]))
+                ref[...] = (ref[...].astype(F32) + came_of(u, par, first_of[k] + n)[...].astype(F32)).astype(BF)
+
+        e_each(u, k, one)
+
+    def chunk_load(u):
+        at = pl.ds(pl.multiple_of(u * 2 * W, 128), 2 * W)
+        return pltpu.make_async_copy(hid_pair.at[:, :, :, at], Rc, l_sem.at[1])
+
+    def first_all():
+        return pltpu.make_async_copy(branch_pair, L, l_sem.at[0])
+
+    def out_copy(u, par):
+        at = pl.ds(pl.multiple_of((2 * u + par) * W, 128), W)
+        return pltpu.make_async_copy(st.at[par], down_o.at[:, at], st_sem.at[par])
+
+    def engine(tau):
+        u = tau - begin
+
+        @pl.when((u >= 0) & (u < units))
+        def _():
+            @pl.when(u == 0)
+            def _():
+                first_all().wait()
+                pl.semaphore_wait(free_sem, len(meets))
+
+            chunk_load(u).wait()
+            rows = NDP * C * M
+            for par in (0, 1):
+                product = dot_tn(L[...].reshape(rows, Dh), Rc[:, :, :, par * W:(par + 1) * W].reshape(rows, W))
+                for owner in range(NC):
+                    part_of(u, par, owner)[...] = product[owner * RB:(owner + 1) * RB].astype(BF)
+
+            @pl.when(u + 1 < units)
+            def _():
+                chunk_load(u + 1).start()
+
+            e_each(u, 0, lambda par, n: e_copy(u, par, 0, n).start())
+
+        for k in range(1, m):
+
+            @pl.when((u - k >= 0) & (u - k < units))
+            def _():
+                e_add(u - k, k - 1)
+                e_each(u - k, k, lambda par, n: e_copy(u - k, par, k, n).start())
+
+        @pl.when((u - m >= 0) & (u - m < units))
+        def _():
+            e_add(u - m, m - 1)
+            for par in (0, 1):
+
+                @pl.when(u - m > 0)
+                def _():
+                    out_copy(u - m - 1, par).wait()
+
+                st[par] = (
+                    part_of(u - m, par, c)[...].astype(F32) + came_of(u - m, par, first_of[m - 1])[...].astype(F32)
+                )
+                out_copy(u - m, par).start()
+
+    def engine_open():
+        pair_kept(2, C - 1)
+
+        def each(s, carry):
+            pair_kept(1, s)
+            pair_received(1, s)
+            pair_received(2, s)
+            return carry
+
+        lax.fori_loop(0, C, each, 0)
+        first_all().start()
+        chunk_load(0).start()
 
     def tick(tau, carry):
         n, s = tau // C, lax.rem(tau, C)
@@ -359,6 +500,10 @@
             pair_start(3, s)
             pair_start(4, s)
 
+            @pl.when(s == C - 1)
+            def _():
+                engine_open()
+
         for a in range(1, T):
             comm(tau, 2 * a - 1, a)
 
@@ -375,7 +520,8 @@
                 weight_wait(3)
 
             tiles(D, lambda at, tile: store_part(s, at, tile, dot_nn(hid[s], wd_v[:, at])))
-            pair_sent(0, s)
+            pair_kept(0, s)
+            pair_away(0, s)
             ag_sent(s)
 
         @pl.when(n == 2)
@@ -386,12 +532,24 @@
                     s, at, tile, dot_nt(Ab[s], wg_v[at, :]) + dot_nt(Bb[s], wu_v[at, :])
                 ),
             )
-            pair_sent(2, s)
+            pair_away(2, s)
+
+            @pl.when(s < C - 1)
+            def _():
+                pair_kept(2, s)
+
             ag_sent(s)
 
+            @pl.when(s == C - 1)
+            def _():
+                for meet in meets:
+                    pl.semaphore_signal(free_sem, inc=1, device_id=meet, device_id_type=MESH)
+
         @pl.when(n <= 2)
         def _():
             rs_start(s)
+
+        engine(tau)
 
         @pl.when(n == 3)
         def _():
@@ -406,66 +564,83 @@
 
     gsum_ref[...] = jnp.zeros_like(gsum_ref)
     weight_wait(0)
-    lax.fori_loop(0, 4 * C, tick, 0)
+    lax.fori_loop(0, max(4 * C, begin + units + m), tick, 0)
 
     for i in range(4):
         for copy in weight_copies(i)[1:]:
             copy.wait_send()
 
     def close(s, carry):
-        for kind in (1, 3, 4, 5, 6):
-            pair_sent(kind, s)
-        for kind in range(7):
+        for kind in (3, 4, 5, 6):
+            pair_kept(kind, s)
             pair_received(kind, s)
+            pair_away(kind, s)
+        pair_received(0, s)
+        pair_away(1, s)
         rs_sent(s)
         ag_sent(s)
         return carry
 
     lax.fori_loop(0, C, close, 0)
 
+    def close_engine(u, carry):
+        for k in range(m):
+            e_each(u, k, lambda par, n: e_copy(u, par, k, n).wait_send())
+        return carry
+
+    lax.fori_loop(0, units, close_engine, 0)
+    for par in (0, 1):
+        out_copy(units - 1, par).wait()
+
 
 def core_call(layer_in, cotangent, norm_gains, head_flat, w_out, w_gate, w_up, w_down):
-    T, NDP = lax.axis_size("tp"), lax.axis_size("dp")
+    T, NC, NDP = lax.axis_size("tp"), lax.axis_size("ctx"), lax.axis_size("dp")
     C = T
     Lr, D = layer_in.shape
     rc = Lr // C
     Hq = w_out.shape[0]
+    RB = D // NDP // NC
     Dh = D // NDP
     F = w_gate.shape[1]
     M = T * rc
+    W = tile_of(F) // 2
     any_spec = pl.BlockSpec(memory_space=pl.ANY)
     vm = pl.BlockSpec(memory_space=pltpu.VMEM)
     sds = jax.ShapeDtypeStruct
     outs = pl.pallas_call(
-        functools.partial(core_kernel, T, C, NDP),
+        functools.partial(core_kernel, T, C, NC, NDP),
         out_shape=(
             sds((Lr, D), BF), sds((Lr, D), F32), sds((3, D), F32), sds((T, C, rc, Hq), BF),
             sds((NDP, C, T, rc, Dh), BF), sds((NDP, C, M, F), BF), sds((NDP, C, T, rc, Dh), BF),
             sds((NDP, C, M, F), BF), sds((NDP, C, M, F), BF), sds((NDP, C, T, rc, Dh), BF),
-            sds((NDP, C, T, rc, Hq), BF),
+            sds((NDP, C, T, rc, Hq), BF), sds((RB, F), F32),
         ),
         in_specs=[vm, vm, vm, vm] + [any_spec] * 4,
-        out_specs=[vm, vm, vm, vm] + [any_spec] * 7,
+        out_specs=[vm, vm, vm, vm] + [any_spec] * 8,
         scratch_shapes=[
             pltpu.VMEM((Hq, D), BF), pltpu.VMEM((D, F), BF), pltpu.VMEM((D, F), BF), pltpu.VMEM((F, D), BF),
             pltpu.VMEM((C, T, rc, D), BF), pltpu.VMEM((C, T, rc, D), BF), pltpu.VMEM((C, T + 1, rc, D), BF),
             pltpu.VMEM((C, M, F), BF), pltpu.VMEM((C, M, F), BF), pltpu.VMEM((C, M, F), BF),
             pltpu.VMEM((C, rc, D), F32), pltpu.VMEM((C, rc, D), F32), pltpu.VMEM((rc, D), F32),
+            pltpu.VMEM((NDP, C, T, rc, Dh), BF), pltpu.VMEM((NDP, C, M, 2 * W), BF), pltpu.VMEM((2, RB, W), F32),
             pltpu.SemaphoreType.DMA((2 * NDP - 1, 4)),
             pltpu.SemaphoreType.DMA((C, 2, T - 1)), pltpu.SemaphoreType.DMA((C, 2, T - 1)),
             pltpu.SemaphoreType.DMA((C, 2, T - 1)), pltpu.SemaphoreType.DMA((C, 2, T - 1)),
             pltpu.SemaphoreType.DMA((2 * NDP - 1, 7, C)),
+            pltpu.SemaphoreType.DMA((2,)), pltpu.SemaphoreType.DMA((F // (2 * W), 2, NC - 1)),
+            pltpu.SemaphoreType.DMA((F // (2 * W), 2, NC - 1)), pltpu.SemaphoreType.DMA((2,)),
+            pltpu.SemaphoreType.REGULAR,
         ],
         compiler_params=pltpu.CompilerParams(
-            collective_id=0, has_side_effects=True, vmem_limit_bytes=66_000_000
+            collective_id=0, has_side_effects=True, vmem_limit_bytes=67_043_328
         ),
         name="core",
     )(layer_in, cotangent, norm_gains, head_flat.reshape(T, C, rc, Hq), w_out, w_gate, w_up, w_down)
-    out, mdelta, gsum, hdelta, rows, hidden, branch, gate, up, attn, heads = outs
+    out, mdelta, gsum, hdelta, rows, hidden, branch, gate, up, attn, heads, down = outs
     flat = lambda a: a.reshape(NDP * T * Lr, a.shape[-1])
     return (
         out, mdelta, gsum, hdelta.reshape(T * Lr, Hq),
-        flat(rows), flat(hidden), flat(branch), flat(gate), flat(up), flat(attn), flat(heads),
+        flat(rows), flat(gate), flat(up), flat(attn), flat(heads), down,
     )
 
 
@@ -744,40 +919,12 @@
     )(layer_in, norm_gains, frequency, w_query, w_key, w_value)
 
 
-def flip(index, bit):
-    return index + bit * (1 - 2 * lax.rem(index // bit, 2))
-
-
-def flips(index, mask):
-    bit = 1
-    while bit <= mask:
-        if mask & bit:
-            index = flip(index, bit)
-        bit *= 2
-    return index
-
-
-def dot_tn(former, latter):
-    return lax.dot_general(former, latter, (((0,), (0,)), ((), ())), preferred_element_type=F32)
-
-
-def sub_sums(bits):
-    sums = [0]
-    for bit in bits:
-        sums = sums + [s + bit for s in sums]
-    return sums
-
-
-def bits_below(count):
-    return [1 << i for i in range(count.bit_length() - 1)]
-
-
 def tail_kernel(
     T, NC, NDP, KH, NS,
     x_ref, mdelta_ref, gain_ref, gsum_ref, q_ref, hd_ref, heads_ref, logt_ref, cos_ref, sin_ref,
     kv_ref, rows1_ref, wq_ref, wk_ref, wv_ref,
-    rows_ref, branch_ref, attn_ref, head_ref, gate_ref, up_ref, hid_ref,
-    igrad_ref, gains_ref, gate_o, up_o, down_o, out_o, q_o, k_o, v_o,
+    rows_ref, attn_ref, head_ref, gate_ref, up_ref,
+    igrad_ref, gains_ref, gate_o, up_o, out_o, q_o, k_o, v_o,
     L, Rc, Hd, RQ, RKV, WQ, WK, WV, Pe, *rest,
 ):
     m = NC.bit_length() - 1
@@ -794,9 +941,9 @@
     GS = Hq // KVd
     Dh, RB = D // NDP, D // NDP // NC
     F = gate_ref.shape[1]
-    W = Rc.shape[2] // 2
+    W = Rc.shape[-1] // 2
     NF = F // (2 * W)
-    wide_units, units = 3 * NF, 3 * NF + 3
+    wide_units, units = 2 * NF, 2 * NF + 3
     narrow = Hq // 2
     scale = HEAD**-0.5
 
@@ -814,10 +961,10 @@
     def remote(src, dst, send, recv, peer):
         return pltpu.make_async_remote_copy(src, dst, send, recv, device_id=peer, device_id_type=MESH)
 
-    firsts = [rows_ref, branch_ref, attn_ref]
+    firsts = [rows_ref, attn_ref, rows1_ref]
 
     def first_copy(i):
-        return pltpu.make_async_copy(firsts[i], L.at[i % 2], l_sem.at[i % 2])
+        return pltpu.make_async_copy(firsts[i], L.at[i], l_sem.at[i])
 
     rows_at = pl.ds(pl.multiple_of(dp * Dh, 128), Dh)
     spread = [
@@ -835,14 +982,14 @@
             w_sem.at[1 + 2 * o, i], w_sem.at[2 + 2 * o, i], partners[o],
         )
 
-    kinds = [gate_ref, up_ref, hid_ref]
+    kinds = [gate_ref, up_ref]
 
     def chunk_copy(u, kind):
         at = pl.ds(pl.multiple_of((u - kind * NF) * 2 * W, 128), 2 * W)
         return pltpu.make_async_copy(kinds[kind].at[:, at], Rc.at[lax.rem(u, 2)], r_sem.at[lax.rem(u, 2)])
 
     def chunk_start(u):
-        for kind in range(3):
+        for kind in range(2):
 
             @pl.when((u >= kind * NF) & (u < (kind + 1) * NF))
             def _():
@@ -857,8 +1004,7 @@
             spread_remote(i, o).start()
     head_copy = pltpu.make_async_copy(head_ref, Hd, l_sem.at[3])
     head_copy.start()
-    rows1_copy = pltpu.make_async_copy(rows1_ref, L.at[2], l_sem.at[2])
-    rows1_copy.start()
+    first_copy(2).start()
 
     orders = [bits_below(NC), bits_below(NC)[::-1]]
     first_of = [sum(NC >> (i + 1) for i in range(k)) for k in range(m)]
@@ -888,7 +1034,7 @@
             Pe[slot, par, :, :, :w] = dot_tn(first, second).reshape(NC, RB, w).astype(BF)
 
         if w == W:
-            for kind in range(3):
+            for kind in range(2):
 
                 @pl.when((u >= kind * NF) & (u < (kind + 1) * NF))
                 def _():
@@ -898,27 +1044,21 @@
             def _():
                 first_copy(0).wait()
 
-            @pl.when(u == 2 * NF)
+            chunk_start(u + 1)
+            for par in (0, 1):
+                store(par, L[0], Rc[lax.rem(u, 2), :, par * W:(par + 1) * W])
+        else:
+
+            @pl.when(u == wide_units)
             def _():
                 first_copy(1).wait()
-                first_copy(2).start()
-
-            chunk_start(u + 1)
-            at = jnp.where(u >= 2 * NF, 1, 0)
-            for par in (0, 1):
-                store(par, L[at], Rc[lax.rem(u, 2), :, par * W:(par + 1) * W])
-        else:
-
-            @pl.when(u == wide_units)
-            def _():
-                first_copy(2).wait()
                 head_copy.wait()
                 for par in (0, 1):
-                    store(par, L[0], Hd[:, par * w:(par + 1) * w])
+                    store(par, L[1], Hd[:, par * w:(par + 1) * w])
 
             @pl.when(u == wide_units + 1)
             def _():
-                rows1_copy.wait()
+                first_copy(2).wait()
                 for par in (0, 1):
                     store(par, L[2], RQ[:, :, par * w:(par + 1) * w].reshape(NDP * R, w))
 
@@ -951,7 +1091,7 @@
 
         if w == W:
             pairs = []
-            for kind, dst in enumerate([gate_o, up_o, down_o]):
+            for kind, dst in enumerate([gate_o, up_o]):
                 base = (u - kind * NF) * 2 * W
                 pairs.append((
                     (u >= kind * NF) & (u < (kind + 1) * NF),
@@ -1274,7 +1414,7 @@
 
 def tail_call(
     layer_in, middle_delta, norm_gains, gain_sums, query, heads_delta, head_rows, log_totals, cosine, sine,
-    keys_values, rows_one, w_query, w_key, w_value, rows, branch, attn, heads, gate, up, hidden,
+    keys_values, rows_one, w_query, w_key, w_value, rows, attn, heads, gate, up,
 ):
     T, NC, NDP = lax.axis_size("tp"), lax.axis_size("ctx"), lax.axis_size("dp")
     Lr, D = layer_in.shape
@@ -1298,11 +1438,11 @@
         functools.partial(tail_kernel, T, NC, NDP, KH, NS),
         out_shape=(
             sds((Lr, D), F32), sds((4, D), F32),
-            sds((RB, F), F32), sds((RB, F), F32), sds((RB, F), F32), sds((RB, Hq), F32),
+            sds((RB, F), F32), sds((RB, F), F32), sds((RB, Hq), F32),
             sds((RB, Hq), F32), sds((RB, KVd), F32), sds((RB, KVd), F32),
         ),
-        in_specs=[vm] * 10 + [any_spec] * 12,
-        out_specs=[vm] * 2 + [any_spec] * 7,
+        in_specs=[vm] * 10 + [any_spec] * 10,
+        out_specs=[vm] * 2 + [any_spec] * 6,
         scratch_shapes=[
             pltpu.VMEM((3, tokens, Dh), BF), pltpu.VMEM((2, tokens, 2 * W), BF), pltpu.VMEM((tokens, Hq), BF),
             pltpu.VMEM((NDP, R, Hq), BF), pltpu.VMEM((NDP, 2, R, KVd), BF),
@@ -1323,7 +1463,7 @@
         name="tail",
     )(
         layer_in, middle_delta, norm_gains, gain_sums, query, heads_delta, head_rows, log_totals, cosine, sine,
-        keys_values, rows_one, w_query, w_key, w_value, rows, branch, attn, heads, gate, up, hidden,
+        keys_values, rows_one, w_query, w_key, w_value, rows, attn, heads, gate, up,
     )
 
 
@@ -1335,11 +1475,11 @@
         layer_in, norm_gains, frequency[None, :], w_query, w_key, w_value
     )
     core = core_call(layer_in, cotangent, norm_gains, head_rows, w_out, w_gate, w_up, w_down)
-    layer_out, middle_delta, gain_sums, heads_delta, rows, hidden, branch, gate, up, attn, heads = core
-    input_grad, gains, grad_gate, grad_up, down_turned, out_turned, grad_query, grad_key, grad_value = tail_call(
+    layer_out, middle_delta, gain_sums, heads_delta, rows, gate, up, attn, heads, down_turned = core
+    input_grad, gains, grad_gate, grad_up, out_turned, grad_query, grad_key, grad_value = tail_call(
         layer_in, middle_delta, norm_gains, gain_sums, query, heads_delta, head_rows, log_totals, cosine, sine,
         keys_values, rows_one.reshape(-1, rows_one.shape[-1]), w_query, w_key, w_value,
-        rows, branch, attn, heads, gate, up, hidden,
+        rows, attn, heads, gate, up,
     )
     rank = (lax.axis_index("dp") * ctx_count + lax.axis_index("ctx")) * tp_count + lax.axis_index("tp")
     width = gains.shape[1] // (dp_count * ctx_count * tp_count)

time: 456 us -> 429 us (0.941)
  Pallas kernels: 439 us -> 413 us
    pallas_call x1, Pallas kernels: 198 us -> 151 us  [tail_call(): pl.pallas_call(functools.partial(tail_kernel, T, NC, NDP, KH, NS), out_sh...]
    pallas_call x1, Pallas kernels: 188 us -> 208 us  [core_call(): pl.pallas_call(functools.partial(core_kernel, T, C, NC, NDP), out_shape=(...]
where the time goes in v4:
time: 429 us; the launch traced here: 428 us
  Pallas kernels  413 us (96%)
  local copies, waits for them, and re-layouts  14.7 us (3%)
    pallas_call x1, Pallas kernels, core_call(): pl.pallas_call(functools.partial(core_kernel, T, C, NC, NDP), out_shape=(...  208 us
    pallas_call x1, Pallas kernels, tail_call(): pl.pallas_call(functools.partial(tail_kernel, T, NC, NDP, KH, NS), out_sh...  151 us
    pallas_call x1, Pallas kernels, front_call(): pl.pallas_call(functools.partial(front_kernel, T, NC, NDP, KVd // HEAD, C...  53.6 us
    unnamed x25, local copies, waits for them, and re-layouts  13.3 us

profile of v4, /device:TPU:0, one launch (start us, length us, event | category | flops | bytes accessed | tf_op | source)
XLA Modules:
  0.0 428.5 jit_solution(9288818426281014937)
XLA Ops:
  0.6 0.5 multiply_power_fusion.freq_ref
  1.2 53.6 %front.1 = (bf16[512,512]{1,0:T(8,128)(2,1)}, bf16[512,512]{1,0:T(8,128)(2,1)}, f32[2,512]{1,0:T(2,128)}, f32[512,128]{1,0:T(8,128)}, f32[512,128]{1,0:T(8,128)}...) custom-call(bf16[128,2304]{1,0:T(8,128)(2,1)} %x_ref.5, f32[4,2304]{1,0:T(4,128)} %gain_ref.5, ...), custom_call_target="tpu_custom_call" | custom-call | tf_op jit(solution)/shard_map/front/pallas_call | solution.py:900
  54.8 207.9 %core.1 = (bf16[128,2304]{1,0:T(8,128)(2,1)}, f32[128,2304]{1,0:T(8,128)}, f32[3,2304]{1,0:T(4,128)}, bf16[4,4,32,512]{3,2,1,0:T(8,128)(2,1)}, bf16[2,4,4,32,115...) custom-call(bf16[128,2304]{1,0:T(8,128)(2,1)} %x_ref.5, ...), custom_call_target="tpu_custom_call" | custom-call | tf_op jit(solution)/shard_map/core/pallas_call | solution.py:610
  262.7 0.0 copy-start.3
  262.7 151.0 %tail.1 = (f32[128,2304]{1,0:T(8,128)}, f32[4,2304]{1,0:T(4,128)}, f32[288,2304]{1,0:T(8,128)}, f32[288,2304]{1,0:T(8,128)}, f32[288,512]{1,0:T(8,128)}, /*index...) custom-call(bf16[128,2304]{1,0:T(8,128)(2,1)} %x_ref.5, f32[128,2304]{1,0:T(8,128)} %get-tuple-element.37.mdelta_ref, ...), custom_call_target="tpu_custom_call" | custom-call | tf_op jit(solution)/shard_map/tail/pallas_call | solution.py:1437
  413.7 0.0 copy-start.5
  413.7 0.0 copy-start.7
  413.8 1.4 constant_dynamic-slice_fusion
  415.2 0.0 copy-done.3
  415.2 0.0 copy-start.6
  415.2 0.8 copy.29
  416.0 0.0 copy-start.4
  416.0 0.0 copy-start.2
  416.0 2.5 copy.30
  418.5 0.0 copy-done.5
  418.5 0.8 copy.31
  419.3 0.0 copy-done.7
  419.3 0.7 copy.32
  420.0 0.0 copy-done.6
  420.0 0.7 copy.33
  420.7 0.0 copy-done.4
  420.8 0.8 copy.34
  421.6 0.0 copy-done.2
  421.6 0.0 copy-start.1
  421.6 1.5 copy.35
  423.1 1.2 copy-done.1
  424.3 0.0 copy-start
  424.3 1.5 copy.36
  425.8 1.2 copy-done
  427.0 1.5 copy.37
Async XLA Ops:
  262.7 152.4 %copy-start.3 = (bf16[128,2304]{1,0:T(8,128)(2,1)S(1)}, bf16[128,2304]{1,0:T(8,128)(2,1)}, u32[]{:S(2)}) copy-start(bf16[128,2304]{1,0:T(8,128)(2,1)} %get-tuple-element.70) | copy-start | bytes 1769476
  413.7 4.8 %copy-start.5 = (f32[288,512]{1,0:T(8,128)S(1)}, f32[288,512]{1,0:T(8,128)}, u32[]{:S(2)}) copy-start(f32[288,512]{1,0:T(8,128)} %get-tuple-element.73) | copy-start | bytes 1769476
  413.7 5.6 %copy-start.7 = (f32[288,256]{1,0:T(8,128)S(1)}, f32[288,256]{1,0:T(8,128)}, u32[]{:S(2)}) copy-start(f32[288,256]{1,0:T(8,128)} %get-tuple-element.74) | copy-start | bytes 884740
  415.2 4.9 %copy-start.6 = (f32[288,256]{1,0:T(8,128)S(1)}, f32[288,256]{1,0:T(8,128)}, u32[]{:S(2)}) copy-start(f32[288,256]{1,0:T(8,128)} %get-tuple-element.75) | copy-start | bytes 884740
  416.0 4.8 %copy-start.4 = (f32[288,512]{1,0:T(8,128)S(1)}, f32[288,512]{1,0:T(8,128)}, u32[]{:S(2)}) copy-start(f32[288,512]{1,0:T(8,128)} %get-tuple-element.56) | copy-start | bytes 1769476
  416.0 5.6 %copy-start.2 = (f32[288,2304]{1,0:T(8,128)S(1)}, f32[288,2304]{1,0:T(8,128)}, u32[]{:S(2)}) copy-start(f32[288,2304]{1,0:T(8,128)} %get-tuple-element.77) | copy-start | bytes 7962628
  421.6 2.7 copy-start.1
  424.3 2.7 copy-start

commit v5 on v4

--- a/solution.py
+++ b/solution.py
@@ -83,7 +83,7 @@
 
 def core_kernel(
     T, C, NC, NDP,
-    x_ref, ct_ref, gain_ref, heads_ref, wo_ref, wg_ref, wu_ref, wd_ref,
+    x_ref, ct_ref, gain_ref, heads_ref, wo_ref, wg_ref, wo_other, wg_other, wut_ref, wdt_ref,
     out_ref, mdelta_ref, gsum_ref, hdelta_ref,
     rows_pair, hid_pair, branch_pair, gate_pair, up_pair, attn_pair, head_pair, down_o,
     wo_v, wg_v, wu_v, wd_v, X, Pb, Rb, hid, Ab, Bb, att, mid, acc,
@@ -102,42 +102,39 @@
     partners = [{"dp": lax.rem(dp + o, NDP)} for o in range(1, NDP)]
     meets = [{"ctx": flip(c, bit)} for bit in bits_below(NC)]
 
+    def columns_of(ref, owner):
+        return ref.at[:, pl.ds(pl.multiple_of(owner * Dh, 128), Dh)]
+
+    def rows_part(ref, owner):
+        return ref.at[pl.ds(pl.multiple_of(owner * Dh, 128), Dh)]
+
+    owners = [p["dp"] for p in partners]
+    loads = [
+        [pltpu.make_async_copy(wo_ref, columns_of(wo_v, dp), w_sem.at[0, 0])]
+        + [
+            pltpu.make_async_copy(columns_of(wo_other, p), columns_of(wo_v, p), w_sem.at[1 + o, 0])
+            for o, p in enumerate(owners)
+        ],
+        [pltpu.make_async_copy(wg_ref, rows_part(wg_v, dp), w_sem.at[0, 1])]
+        + [
+            pltpu.make_async_copy(rows_part(wg_other, p), rows_part(wg_v, p), w_sem.at[1 + o, 1])
+            for o, p in enumerate(owners)
+        ],
+        [pltpu.make_async_copy(wut_ref, wu_v, w_sem.at[0, 2])],
+        [pltpu.make_async_copy(wdt_ref, wd_v, w_sem.at[0, 3])],
+    ]
+    for load in loads:
+        for copy in load:
+            copy.start()
+
     barrier(
         has_left.astype(jnp.int32) + has_right.astype(jnp.int32) + len(partners + meets),
         [(has_left, left), (has_right, right)] + [(t >= 0, p) for p in partners + meets],
     )
 
-    rows_at = pl.ds(pl.multiple_of(dp * Dh, 128), Dh)
-    weights = [
-        (wo_ref, lambda: wo_v.at[:, rows_at]),
-        (wg_ref, lambda: wg_v.at[rows_at]),
-        (wu_ref, lambda: wu_v.at[rows_at]),
-        (wd_ref, lambda: wd_v.at[:, rows_at]),
-    ]
-
-    def weight_copies(i):
-        src, dst = weights[i]
-        copies = [pltpu.make_async_copy(src, dst(), w_sem.at[0, i])]
-        for o, partner in enumerate(partners):
-            copies.append(
-                pltpu.make_async_remote_copy(
-                    src, dst(), w_sem.at[1 + 2 * o, i], w_sem.at[2 + 2 * o, i],
-                    device_id=partner, device_id_type=MESH,
-                )
-            )
-        return copies
-
-    for i in range(4):
-        for copy in weight_copies(i):
-            copy.start()
-
     def weight_wait(i):
-        src, dst = weights[i]
-        for o, copy in enumerate(weight_copies(i)):
-            if o == 0:
-                copy.wait()
-            else:
-                copy.wait_recv()
+        for copy in loads[i]:
+            copy.wait()
 
     def pair_copies(kind, s, src, half, dst):
         def cut(owner):
@@ -361,8 +358,15 @@
     def part_of(u, par, owner):
         return block_of(wd_v, (u * 2 + par) * NC + owner)
 
+    early = units * 2 * (2 * NC - 1) <= (D // pitch) * (F // W)
+
     def came_of(u, par, at):
-        return block_of(wu_v, (u * 2 + par) * (NC - 1) + at)
+        i = (u * 2 + par) * (NC - 1) + at
+        return block_of(wd_v, units * 2 * NC + i) if early else block_of(wu_v, i)
+
+    def free():
+        for meet in meets:
+            pl.semaphore_signal(free_sem, inc=1, device_id=meet, device_id_type=MESH)
 
     def e_copy(u, par, k, n):
         order = orders[par]
@@ -439,7 +443,7 @@
 
                 st[par] = (
                     part_of(u - m, par, c)[...].astype(F32) + came_of(u - m, par, first_of[m - 1])[...].astype(F32)
-                )
+                ).astype(BF)
                 out_copy(u - m, par).start()
 
     def engine_open():
@@ -473,7 +477,7 @@
 
             def gate_up(at, tile):
                 gate = dot_nn(rows_of(s), wg_v[:, at])
-                up = dot_nn(rows_of(s), wu_v[:, at])
+                up = dot_nt(rows_of(s), wu_v[at, :])
                 inner = jnp.tanh(0.7978845608028654 * (gate + 0.044715 * gate * gate * gate))
                 half = 0.5 * (1.0 + inner)
                 gelu = gate * half
@@ -492,7 +496,7 @@
             pair_start(2, s)
 
             def gate_up_delta(at, tile):
-                delta = dot_nt(rows_of(s), wd_v[at, :])
+                delta = dot_nn(rows_of(s), wd_v[:, at])
                 Ab[s, :, at] = (delta * Ab[s, :, at].astype(F32)).astype(BF)
                 Bb[s, :, at] = (delta * Bb[s, :, at].astype(F32)).astype(BF)
 
@@ -502,7 +506,12 @@
 
             @pl.when(s == C - 1)
             def _():
+                if early:
+                    free()
                 engine_open()
+
+        if early:
+            engine(tau)
 
         for a in range(1, T):
             comm(tau, 2 * a - 1, a)
@@ -519,7 +528,7 @@
             def _():
                 weight_wait(3)
 
-            tiles(D, lambda at, tile: store_part(s, at, tile, dot_nn(hid[s], wd_v[:, at])))
+            tiles(D, lambda at, tile: store_part(s, at, tile, dot_nt(hid[s], wd_v[at, :])))
             pair_kept(0, s)
             pair_away(0, s)
             ag_sent(s)
@@ -529,7 +538,7 @@
             tiles(
                 D,
                 lambda at, tile: store_part(
-                    s, at, tile, dot_nt(Ab[s], wg_v[at, :]) + dot_nt(Bb[s], wu_v[at, :])
+                    s, at, tile, dot_nt(Ab[s], wg_v[at, :]) + dot_nn(Bb[s], wu_v[:, at])
                 ),
             )
             pair_away(2, s)
@@ -540,16 +549,15 @@
 
             ag_sent(s)
 
-            @pl.when(s == C - 1)
-            def _():
-                for meet in meets:
-                    pl.semaphore_signal(free_sem, inc=1, device_id=meet, device_id_type=MESH)
+            if not early:
+                pl.when(s == C - 1)(free)
 
         @pl.when(n <= 2)
         def _():
             rs_start(s)
 
-        engine(tau)
+        if not early:
+            engine(tau)
 
         @pl.when(n == 3)
         def _():
@@ -565,10 +573,6 @@
     gsum_ref[...] = jnp.zeros_like(gsum_ref)
     weight_wait(0)
     lax.fori_loop(0, max(4 * C, begin + units + m), tick, 0)
-
-    for i in range(4):
-        for copy in weight_copies(i)[1:]:
-            copy.wait_send()
 
     def close(s, carry):
         for kind in (3, 4, 5, 6):
@@ -593,7 +597,7 @@
         out_copy(units - 1, par).wait()
 
 
-def core_call(layer_in, cotangent, norm_gains, head_flat, w_out, w_gate, w_up, w_down):
+def core_call(layer_in, cotangent, norm_gains, head_flat, w_out, w_gate, *weights):
     T, NC, NDP = lax.axis_size("tp"), lax.axis_size("ctx"), lax.axis_size("dp")
     C = T
     Lr, D = layer_in.shape
@@ -613,17 +617,17 @@
             sds((Lr, D), BF), sds((Lr, D), F32), sds((3, D), F32), sds((T, C, rc, Hq), BF),
             sds((NDP, C, T, rc, Dh), BF), sds((NDP, C, M, F), BF), sds((NDP, C, T, rc, Dh), BF),
             sds((NDP, C, M, F), BF), sds((NDP, C, M, F), BF), sds((NDP, C, T, rc, Dh), BF),
-            sds((NDP, C, T, rc, Hq), BF), sds((RB, F), F32),
+            sds((NDP, C, T, rc, Hq), BF), sds((RB, F), BF),
         ),
-        in_specs=[vm, vm, vm, vm] + [any_spec] * 4,
+        in_specs=[vm, vm, vm, vm] + [any_spec] * 6,
         out_specs=[vm, vm, vm, vm] + [any_spec] * 8,
         scratch_shapes=[
             pltpu.VMEM((Hq, D), BF), pltpu.VMEM((D, F), BF), pltpu.VMEM((D, F), BF), pltpu.VMEM((F, D), BF),
             pltpu.VMEM((C, T, rc, D), BF), pltpu.VMEM((C, T, rc, D), BF), pltpu.VMEM((C, T + 1, rc, D), BF),
             pltpu.VMEM((C, M, F), BF), pltpu.VMEM((C, M, F), BF), pltpu.VMEM((C, M, F), BF),
             pltpu.VMEM((C, rc, D), F32), pltpu.VMEM((C, rc, D), F32), pltpu.VMEM((rc, D), F32),
-            pltpu.VMEM((NDP, C, T, rc, Dh), BF), pltpu.VMEM((NDP, C, M, 2 * W), BF), pltpu.VMEM((2, RB, W), F32),
-            pltpu.SemaphoreType.DMA((2 * NDP - 1, 4)),
+            pltpu.VMEM((NDP, C, T, rc, Dh), BF), pltpu.VMEM((NDP, C, M, 2 * W), BF), pltpu.VMEM((2, RB, W), BF),
+            pltpu.SemaphoreType.DMA((NDP, 4)),
             pltpu.SemaphoreType.DMA((C, 2, T - 1)), pltpu.SemaphoreType.DMA((C, 2, T - 1)),
             pltpu.SemaphoreType.DMA((C, 2, T - 1)), pltpu.SemaphoreType.DMA((C, 2, T - 1)),
             pltpu.SemaphoreType.DMA((2 * NDP - 1, 7, C)),
@@ -635,7 +639,7 @@
             collective_id=0, has_side_effects=True, vmem_limit_bytes=67_043_328
         ),
         name="core",
-    )(layer_in, cotangent, norm_gains, head_flat.reshape(T, C, rc, Hq), w_out, w_gate, w_up, w_down)
+    )(layer_in, cotangent, norm_gains, head_flat.reshape(T, C, rc, Hq), w_out, w_gate, *weights)
     out, mdelta, gsum, hdelta, rows, hidden, branch, gate, up, attn, heads, down = outs
     flat = lambda a: a.reshape(NDP * T * Lr, a.shape[-1])
     return (
@@ -646,10 +650,10 @@
 
 def front_kernel(
     T, NC, NDP, KH, C,
-    x_ref, gain_ref, freq_ref, wq_ref, wk_ref, wv_ref,
-    q_o, heads_o, logt_o, cos_o, sin_o, kv_o, rows1_o,
-    X, WQ, WK, WV, KV, turned_sum, totals,
-    w_sem, ag_send, ag_recv, pair_sem, kv_send, kv_recv, out_sem,
+    x_ref, gain_ref, freq_ref, wq_ref, wk_ref, wv_ref, wo_ref, wg_ref, wu_ref, wd_ref,
+    q_o, heads_o, logt_o, cos_o, sin_o, kv_o, rows1_o, wo_o, wg_o, wut_o, wdt_o,
+    X, WQ, WK, WV, KV, turned_sum, totals, up_v, upt_v, down_v, downt_v,
+    w_sem, ag_send, ag_recv, pair_sem, kv_send, kv_recv, out_sem, t_sem, p_sem,
 ):
     t, c, dp = lax.axis_index("tp"), lax.axis_index("ctx"), lax.axis_index("dp")
     Lr, D = x_ref.shape
@@ -673,7 +677,6 @@
     sem = pltpu.get_barrier_semaphore()
     for axis, index in peers:
         pl.semaphore_signal(sem, inc=1, device_id={axis: index}, device_id_type=MESH)
-    pl.semaphore_wait(sem, len(peers))
 
     rows_at = pl.ds(pl.multiple_of(dp * Dh, 128), Dh)
     weights = [(wq_ref, WQ), (wk_ref, WK), (wv_ref, WV)]
@@ -687,10 +690,17 @@
             "dp", partners[o],
         )
 
+    turns = [
+        pltpu.make_async_copy(wu_ref, up_v, t_sem.at[0]),
+        pltpu.make_async_copy(wd_ref, down_v, t_sem.at[1]),
+    ]
     for i in range(3):
         weight_local(i).start()
-        for o in range(NDP - 1):
-            weight_remote(i, o).start()
+    for copy in turns:
+        copy.start()
+    rows = x_ref[...].astype(F32)
+    X[t] = (rows * inverse_rms(rows) * gain_ref[0:1]).astype(BF)
+    pl.semaphore_wait(sem, len(peers))
 
     def ag_copy(s, side, k, j):
         at = pl.ds(s * rc, rc)
@@ -706,14 +716,61 @@
     def onward(side):
         return has_right if side == 0 else has_left
 
-    rows = x_ref[...].astype(F32)
-    X[t] = (rows * inverse_rms(rows) * gain_ref[0:1]).astype(BF)
     for s in range(C):
         for side in (0, 1):
 
             @pl.when(onward(side))
             def _():
                 ag_copy(s, side, 0, t).start()
+
+    for i in range(3):
+        for o in range(NDP - 1):
+            weight_remote(i, o).start()
+
+    def parts(ref, i):
+        height = ref.shape[0] // T
+        return pl.ds(pl.multiple_of(i * height, 16), height), height
+
+    def part_dst(dst, ref, i, columns):
+        at, height = parts(ref, i)
+        if columns:
+            return dst.at[at, rows_at]
+        return dst.at[pl.ds(pl.multiple_of(dp * Dh + i * height, 16), height)]
+
+    moved = [(wo_ref, wo_o, True, False), (wg_ref, wg_o, False, False)]
+    moved += [(upt_v, wut_o, True, True), (downt_v, wdt_o, False, True)]
+
+    def part_remote(w, i, o):
+        src, dst, columns, _ = moved[w]
+        return remote(
+            src.at[parts(src, i)[0]], part_dst(dst, src, i, columns),
+            p_sem.at[1 + 2 * o, w, i], p_sem.at[2 + 2 * o, w, i], "dp", partners[o],
+        )
+
+    def part_local(w, i):
+        src, dst, columns, _ = moved[w]
+        return pltpu.make_async_copy(src.at[parts(src, i)[0]], part_dst(dst, src, i, columns), p_sem.at[0, w, i])
+
+    def part_start(w, i):
+        for o in range(NDP - 1):
+            part_remote(w, i, o).start()
+        if moved[w][3]:
+            part_local(w, i).start()
+
+    def turn():
+        for copy, src, dst in zip(turns, (up_v, down_v), (upt_v, downt_v), strict=True):
+            copy.wait()
+            height = src.shape[0] // T
+
+            def some(i, carry):
+                at = pl.ds(pl.multiple_of(i * height, 128), height)
+                dst[:, at] = src[at, :].T
+                return carry
+
+            if height % 128 == 0:
+                lax.fori_loop(0, T, some, 0)
+            else:
+                dst[...] = src[...].T
 
     position = (c * R + lax.broadcasted_iota(jnp.int32, (R, HEAD // 2), 0)).astype(F32)
     angles = position * freq_ref[...]
@@ -792,6 +849,15 @@
             def _():
                 project(ag_block(side, k))
 
+        part_start(0, k)
+        part_start(1, k)
+
+        @pl.when(k == 0)
+        def _():
+            turn()
+
+        part_start(2, k)
+        part_start(3, k)
         return carry
 
     lax.fori_loop(0, T, gather, 0)
@@ -851,6 +917,16 @@
     for i in range(3):
         for o in range(NDP - 1):
             weight_remote(i, o).wait_send()
+
+    def close_parts(i, carry):
+        for w in range(4):
+            for o in range(NDP - 1):
+                part_remote(w, i, o).wait()
+            if moved[w][3]:
+                part_local(w, i).wait()
+        return carry
+
+    lax.fori_loop(0, T, close_parts, 0)
     for s in range(C):
         for side in (0, 1):
             for k in range(T - 1):
@@ -885,13 +961,14 @@
     lax.fori_loop(0, NC, close_out, 0)
 
 
-def front_call(layer_in, norm_gains, frequency, w_query, w_key, w_value):
+def front_call(layer_in, norm_gains, frequency, w_query, w_key, w_value, w_out, w_gate, w_up, w_down):
     T, NC, NDP = lax.axis_size("tp"), lax.axis_size("ctx"), lax.axis_size("dp")
     C = T
     Lr, D = layer_in.shape
     R = T * Lr
     Hq, KVd = w_query.shape[1], w_key.shape[1]
     Dh = D // NDP
+    F = w_gate.shape[1]
     H = Hq // HEAD
     any_spec = pl.BlockSpec(memory_space=pl.ANY)
     vm = pl.BlockSpec(memory_space=pltpu.VMEM)
@@ -903,20 +980,22 @@
             sds((R, Hq), BF), sds((R, Hq), BF), sds((H, R), F32),
             sds((R, HEAD // 2), F32), sds((R, HEAD // 2), F32),
             sds((NC, T, 2, Lr, KVd), BF), sds((NDP, T, Lr, Dh), BF),
+            sds((Hq, D), BF), sds((D, F), BF), sds((F, D), BF), sds((D, F), BF),
         ),
-        in_specs=[vm] * 3 + [any_spec] * 3,
-        out_specs=[vm] * 5 + [any_spec] * 2,
+        in_specs=[vm] * 3 + [any_spec] * 7,
+        out_specs=[vm] * 5 + [any_spec] * 6,
         scratch_shapes=[
             pltpu.VMEM((T, Lr, D), BF), pltpu.VMEM((D, Hq), BF), pltpu.VMEM((D, KVd), BF), pltpu.VMEM((D, KVd), BF),
             pltpu.VMEM((NC, T, 2, Lr, KVd), BF), pltpu.VMEM((H, HEAD, R), F32), pltpu.VMEM((H, R), F32),
+            pltpu.VMEM((Dh, F), BF), pltpu.VMEM((F, Dh), BF), pltpu.VMEM((F, Dh), BF), pltpu.VMEM((Dh, F), BF),
             dma((2 * NDP - 1, 3)), dma((C, 2, T - 1)), dma((C, 2, T - 1)), dma((2 * NDP - 1, T)),
-            dma((NC - 1, T)), dma((NC - 1, T)), dma((NC,)),
+            dma((NC - 1, T)), dma((NC - 1, T)), dma((NC,)), dma((2,)), dma((2 * NDP - 1, 4, T)),
         ],
         compiler_params=pltpu.CompilerParams(
             collective_id=2, has_side_effects=True, vmem_limit_bytes=66_000_000
         ),
         name="front",
-    )(layer_in, norm_gains, frequency, w_query, w_key, w_value)
+    )(layer_in, norm_gains, frequency, w_query, w_key, w_value, w_out, w_gate, w_up, w_down)
 
 
 def tail_kernel(
@@ -953,11 +1032,6 @@
     others = [along("tp", lax.rem(t + o, T)) for o in range(1, T)]
     others += [along("ctx", lax.rem(c + o, NC)) for o in range(1, NC)]
     partners = [along("dp", lax.rem(dp + o, NDP)) for o in range(1, NDP)]
-    sem = pltpu.get_barrier_semaphore()
-    for peer in others + partners:
-        pl.semaphore_signal(sem, inc=1, device_id=peer, device_id_type=MESH)
-    pl.semaphore_wait(sem, len(others + partners))
-
     def remote(src, dst, send, recv, peer):
         return pltpu.make_async_remote_copy(src, dst, send, recv, device_id=peer, device_id_type=MESH)
 
@@ -997,11 +1071,11 @@
 
     first_copy(0).start()
     chunk_start(0)
+    sem = pltpu.get_barrier_semaphore()
+    for peer in others + partners:
+        pl.semaphore_signal(sem, inc=1, device_id=peer, device_id_type=MESH)
+    pl.semaphore_wait(sem, len(others + partners))
     first_copy(1).start()
-    for i in range(3):
-        spread_local(i).start()
-        for o in range(NDP - 1):
-            spread_remote(i, o).start()
     head_copy = pltpu.make_async_copy(head_ref, Hd, l_sem.at[3])
     head_copy.start()
     first_copy(2).start()
@@ -1118,7 +1192,8 @@
         e_add(u, m - 1, w)
         out_wait(u - 2)
         for par in (0, 1):
-            st[two, par, :, :w] = Pe[slot, par, c, :, :w].astype(F32) + Rv[m - 1][slot, par, 0, :, :w].astype(F32)
+            total = Pe[slot, par, c, :, :w].astype(F32) + Rv[m - 1][slot, par, 0, :, :w].astype(F32)
+            st[two, par, :, :w] = total.astype(BF)
         for here, copies in out_copies(u, w):
 
             @pl.when(here)
@@ -1336,6 +1411,10 @@
 
         @pl.when(i == 1)
         def _():
+            for w in range(3):
+                spread_local(w).start()
+                for o in range(NDP - 1):
+                    spread_remote(w, o).start()
             attention()
 
         @pl.when(i == 2)
@@ -1438,8 +1517,8 @@
         functools.partial(tail_kernel, T, NC, NDP, KH, NS),
         out_shape=(
             sds((Lr, D), F32), sds((4, D), F32),
-            sds((RB, F), F32), sds((RB, F), F32), sds((RB, Hq), F32),
-            sds((RB, Hq), F32), sds((RB, KVd), F32), sds((RB, KVd), F32),
+            sds((RB, F), BF), sds((RB, F), BF), sds((RB, Hq), BF),
+            sds((RB, Hq), BF), sds((RB, KVd), BF), sds((RB, KVd), BF),
         ),
         in_specs=[vm] * 10 + [any_spec] * 10,
         out_specs=[vm] * 2 + [any_spec] * 6,
@@ -1449,7 +1528,7 @@
             pltpu.VMEM((D, Hq), BF), pltpu.VMEM((D, KVd), BF), pltpu.VMEM((D, KVd), BF),
             pltpu.VMEM((NS, 2, NC, RB, W), BF),
             *[pltpu.VMEM((NS, 2, NC >> (k + 1), RB, W), BF) for k in range(m)],
-            pltpu.VMEM((2, 2, RB, W), F32), pltpu.VMEM((R, Hq), F32), pltpu.VMEM((Hq // HEAD, R), F32), pltpu.VMEM((2, T, 2, Lr, KVd), BF),
+            pltpu.VMEM((2, 2, RB, W), BF), pltpu.VMEM((R, Hq), F32), pltpu.VMEM((Hq // HEAD, R), F32), pltpu.VMEM((2, T, 2, Lr, KVd), BF),
             pltpu.VMEM((kv_slots, 2, R, KVd), BF), pltpu.VMEM((NC - 1, 2, R, KVd), BF),
             pltpu.VMEM((T, Lr, D), BF), pltpu.VMEM((T + 1, Lr, D), BF), pltpu.VMEM((2, R, KVd), F32),
             pltpu.VMEM((meets + 1, 4, D), F32), pltpu.VMEM((meets, 4, D), F32),
@@ -1467,27 +1546,71 @@
     )
 
 
+def finish_kernel(width, count, gains_ref, *refs):
+    n = count
+    srcs, gain_o, dsts = refs[:n], refs[n], refs[n + 1:2 * n + 1]
+    held, wide, sems = refs[2 * n + 1:3 * n + 1], refs[3 * n + 1:-1], refs[-1]
+    for i in range(n):
+        pltpu.make_async_copy(srcs[i], held[i], sems.at[0, i]).start()
+    rank = lax.axis_index("dp")
+    for axis in ("ctx", "tp"):
+        rank = rank * lax.axis_size(axis) + lax.axis_index(axis)
+    gains = gains_ref[...]
+    total = gains.shape[1]
+    gain_o[...] = pltpu.roll(gains, lax.rem(total - rank * width, total), axis=1)[:4, :width]
+    buffers = []
+    for i in range(n):
+        pltpu.make_async_copy(srcs[i], held[i], sems.at[0, i]).wait()
+        buffer = held[i]
+        if held[i].dtype != dsts[i].dtype:
+            buffer = wide[len([b for b in buffers if b])]
+            buffer[...] = held[i][...].astype(buffer.dtype)
+        buffers.append(buffer is not held[i])
+        pltpu.make_async_copy(buffer, dsts[i], sems.at[1, i]).start()
+    used = 0
+    for i in range(n):
+        buffer = wide[used] if buffers[i] else held[i]
+        used += buffers[i]
+        pltpu.make_async_copy(buffer, dsts[i], sems.at[1, i]).wait()
+
+
+def finish_call(gains, arrays, dtypes):
+    width = gains.shape[1] // (lax.axis_size("tp") * lax.axis_size("ctx") * lax.axis_size("dp"))
+    any_spec = pl.BlockSpec(memory_space=pl.ANY)
+    vm = pl.BlockSpec(memory_space=pltpu.VMEM)
+    sds = jax.ShapeDtypeStruct
+    n = len(arrays)
+    return pl.pallas_call(
+        functools.partial(finish_kernel, width, n),
+        out_shape=[sds((4, width), F32)] + [sds(a.shape, d) for a, d in zip(arrays, dtypes, strict=True)],
+        in_specs=[vm] + [any_spec] * n,
+        out_specs=[vm] + [any_spec] * n,
+        scratch_shapes=[pltpu.VMEM(a.shape, a.dtype) for a in arrays]
+        + [pltpu.VMEM(a.shape, d) for a, d in zip(arrays, dtypes, strict=True) if a.dtype != d]
+        + [pltpu.SemaphoreType.DMA((2, n))],
+        compiler_params=pltpu.CompilerParams(vmem_limit_bytes=66_000_000),
+        name="finish",
+    )(gains, *arrays)
+
+
 def shards(layer_in, cotangent, norm_gains, w_query, w_key, w_value, w_out, w_gate, w_up, w_down):
-    tp_count, ctx_count, dp_count = lax.axis_size("tp"), lax.axis_size("ctx"), lax.axis_size("dp")
     half_width = HEAD // 2
     frequency = THETA ** (-(jnp.arange(half_width, dtype=F32) * 2.0) / HEAD)
-    query, head_rows, log_totals, cosine, sine, keys_values, rows_one = front_call(
-        layer_in, norm_gains, frequency[None, :], w_query, w_key, w_value
+    query, head_rows, log_totals, cosine, sine, keys_values, rows_one, *weights = front_call(
+        layer_in, norm_gains, frequency[None, :], w_query, w_key, w_value, w_out, w_gate, w_up, w_down
     )
-    core = core_call(layer_in, cotangent, norm_gains, head_rows, w_out, w_gate, w_up, w_down)
-    layer_out, middle_delta, gain_sums, heads_delta, rows, gate, up, attn, heads, down_turned = core
-    input_grad, gains, grad_gate, grad_up, out_turned, grad_query, grad_key, grad_value = tail_call(
+    core = core_call(layer_in, cotangent, norm_gains, head_rows, w_out, w_gate, *weights)
+    layer_out, middle_delta, gain_sums, heads_delta, rows, gate, up, attn, heads, down_sum = core
+    input_grad, gains, *sums = tail_call(
         layer_in, middle_delta, norm_gains, gain_sums, query, heads_delta, head_rows, log_totals, cosine, sine,
         keys_values, rows_one.reshape(-1, rows_one.shape[-1]), w_query, w_key, w_value,
         rows, attn, heads, gate, up,
     )
-    rank = (lax.axis_index("dp") * ctx_count + lax.axis_index("ctx")) * tp_count + lax.axis_index("tp")
-    width = gains.shape[1] // (dp_count * ctx_count * tp_count)
-    gain_grads = lax.dynamic_slice_in_dim(gains, rank * width, width, 1)
-    return (
-        layer_out, input_grad, gain_grads, grad_query, grad_key, grad_value,
-        out_turned.T, grad_gate, grad_up, down_turned.T,
+    arrays = [layer_out, input_grad, down_sum, *sums]
+    gain_grads, layer_out, input_grad, down_turned, grad_gate, grad_up, out_turned, *rest = finish_call(
+        gains, arrays, [BF] + [F32] * (len(arrays) - 1)
     )
+    return (layer_out, input_grad, gain_grads, *rest, out_turned.T, grad_gate, grad_up, down_turned.T)
 
 
 def solution(mesh):

time: 429 us -> 407 us (0.949)
  local copies, waits for them, and re-layouts: 14.7 us -> 0 us
  Pallas kernels: 413 us -> 405 us
    pallas_call x1, Pallas kernels: 208 us -> 191 us  [core_call(): pl.pallas_call(functools.partial(core_kernel, T, C, NC, NDP), out_shape=(...]
    unnamed x25 -> x0, local copies, waits for them, and re-layouts: 13.3 us -> none
    pallas_call x0 -> x1, Pallas kernels: none -> 7.68 us  [finish_call(): pl.pallas_call(functools.partial(finish_kernel, width, n), out_shape=[sds...]
where the time goes in v5:
time: 407 us; the launch traced here: 406 us
  Pallas kernels  405 us (100%)
    pallas_call x1, Pallas kernels, core_call(): pl.pallas_call(functools.partial(core_kernel, T, C, NC, NDP), out_shape=(...  191 us
    pallas_call x1, Pallas kernels, tail_call(): pl.pallas_call(functools.partial(tail_kernel, T, NC, NDP, KH, NS), out_sh...  150 us
    pallas_call x1, Pallas kernels, front_call(): pl.pallas_call(functools.partial(front_kernel, T, NC, NDP, KVd // HEAD, C...  57.2 us

profile of v5, /device:TPU:0, one launch (start us, length us, event | category | flops | bytes accessed | tf_op | source)
XLA Modules:
  0.0 406.5 jit_solution(13912040478390699048)
XLA Ops:
  0.6 0.5 multiply_power_fusion.freq_ref
  1.2 57.2 %front.1 = (bf16[512,512]{1,0:T(8,128)(2,1)}, bf16[512,512]{1,0:T(8,128)(2,1)}, f32[2,512]{1,0:T(2,128)}, f32[512,128]{1,0:T(8,128)}, f32[512,128]{1,0:T(8,128)}...) custom-call(bf16[128,2304]{1,0:T(8,128)(2,1)} %x_ref.5, ...), custom_call_target="tpu_custom_call" | custom-call | tf_op jit(solution)/shard_map/front/pallas_call | solution.py:977
  58.3 190.6 %core.1 = (bf16[128,2304]{1,0:T(8,128)(2,1)}, f32[128,2304]{1,0:T(8,128)}, f32[3,2304]{1,0:T(4,128)}, bf16[4,4,32,512]{3,2,1,0:T(8,128)(2,1)}, bf16[2,4,4,32,115...) custom-call(bf16[128,2304]{1,0:T(8,128)(2,1)} %x_ref.5, ...), custom_call_target="tpu_custom_call" | custom-call | tf_op jit(solution)/shard_map/core/pallas_call | solution.py:614
  248.9 149.6 %tail.1 = (f32[128,2304]{1,0:T(8,128)}, f32[4,2304]{1,0:T(4,128)}, bf16[288,2304]{1,0:T(8,128)(2,1)}, bf16[288,2304]{1,0:T(8,128)(2,1)}, bf16[288,512]{1,0:T(8,1...) custom-call(bf16[128,2304]{1,0:T(8,128)(2,1)} %x_ref.5, ...), custom_call_target="tpu_custom_call" | custom-call | tf_op jit(solution)/shard_map/tail/pallas_call | solution.py:1516
  398.6 7.7 %finish.1 = (f32[4,72]{1,0:T(4,128)}, bf16[128,2304]{1,0:T(8,128)(2,1)}, f32[128,2304]{1,0:T(8,128)}, f32[288,2304]{1,0:T(8,128)}, f32[288,2304]{1,0:T(8,128)}, ...) custom-call(f32[4,2304]{1,0:T(4,128)} %get-tuple-element.68.gains_re, ...), custom_call_target="tpu_custom_call" | custom-call | tf_op jit(solution)/shard_map/finish/pallas_call | solution.py:1583

commit v6 on v5

v6 whole, which is shorter than its diff:
```python
import functools

import jax
import jax.numpy as jnp
from jax import lax
from jax.experimental import pallas as pl
from jax.experimental.pallas import tpu as pltpu
from jax.sharding import PartitionSpec as P

HEAD = 256
EPS = 1e-06
CAP = 50.0
THETA = 10000.0
MESH = pl.DeviceIdType.MESH
BF = jnp.bfloat16
F32 = jnp.float32


def tile_of(width):
    for tile in (768, 512, 256, 128):
        if width % tile == 0:
            return tile
    return width


def inverse_rms(values):
    return lax.rsqrt(jnp.mean(values * values, axis=-1, keepdims=True) + EPS)


def rms_back(values, scale, gain, delta):
    weighted = delta * gain
    inner = jnp.mean(weighted * values, axis=-1, keepdims=True)
    grad = scale * weighted - values * (scale * scale * scale * inner)
    return grad, jnp.sum(delta * values * scale, axis=0, keepdims=True)


def dot_nt(former, latter):
    return lax.dot_general(former, latter, (((1,), (1,)), ((), ())), preferred_element_type=F32)


def dot_nn(former, latter):
    return jnp.dot(former, latter, preferred_element_type=F32)


def flip(index, bit):
    return index + bit * (1 - 2 * lax.rem(index // bit, 2))


def flips(index, mask):
    bit = 1
    while bit <= mask:
        if mask & bit:
            index = flip(index, bit)
        bit *= 2
    return index


def dot_tn(former, latter):
    return lax.dot_general(former, latter, (((0,), (0,)), ((), ())), preferred_element_type=F32)


def sub_sums(bits):
    sums = [0]
    for bit in bits:
        sums = sums + [s + bit for s in sums]
    return sums


def bits_below(count):
    return [1 << i for i in range(count.bit_length() - 1)]


def main_kernel(
    T, C, NC, NDP, KH, NP, NR,
    x_ref, ct_ref, gain_ref, heads_ref,
    wo_ref, wg_ref, wo_other, wg_other, wut_ref, wdt_ref, q_ref, logt_ref, cos_ref, sin_ref, kv_ref, rows1_ref,
    wq_ref, wk_ref, wv_ref,
    out_ref, igrad_ref, gains_ref,
    down_o, gate_o, up_o, out_o, q_o, k_o, v_o,
    rows_pair, hid_pair, branch_pair, gate_pair, up_pair, attn_pair, head_pair,
    wo_v, wd_v, X, Pb, Rb, att, mid, acc, mdelta, gsum, hdelta, Ab, Bb, L0, Rc, st, G, GR,
    w_sem, f_sem, rs_send, rs_recv, ag_send, ag_recv, pair_sem, l_sem, r_sem, e_send, e_recv, st_sem,
    s_sem, q_sem, kv_send, kv_recv, last_send, last_recv, g_send, g_recv, kvb_sem, free_sem, enter_sem,
):
    t, c, dp = lax.axis_index("tp"), lax.axis_index("ctx"), lax.axis_index("dp")
    Lr, D = x_ref.shape
    rc = Lr // C
    R, Hq = q_ref.shape
    KVd = KH * HEAD
    GS = Hq // KVd
    Dh, RB = D // NDP, D // NDP // NC
    F = wg_ref.shape[1]
    M = T * rc
    tokens = NDP * R
    W = Rc.shape[-1] // 2
    m = NC.bit_length() - 1
    NF = F // (2 * W)
    narrow = min(W, Hq // 2)
    wide_units = 3 * NF
    n_out, n_kv = Hq // (2 * narrow), KVd // narrow
    q_first, kv_first = wide_units + n_out, wide_units + 2 * n_out
    units = kv_first + n_kv
    begin = 3 * C - 1
    scale = HEAD**-0.5
    has_left, has_right = t > 0, t < T - 1
    left, right = {"tp": jnp.maximum(t - 1, 0)}, {"tp": jnp.minimum(t + 1, T - 1)}
    partners = [{"dp": lax.rem(dp + o, NDP)} for o in range(1, NDP)]
    later = [{"ctx": lax.rem(c + o, NC)} for o in range(1, NC)]
    others = [{"tp": lax.rem(t + o, T)} for o in range(1, T)] + later + partners
    ctx_meets = [{"ctx": flip(c, bit)} for bit in bits_below(NC)]

    def along(axis, index):
        return {axis: index}

    def remote(src, dst, send, recv, peer):
        return pltpu.make_async_remote_copy(src, dst, send, recv, device_id=peer, device_id_type=MESH)

    def signal_all(sem, peers):
        for peer in peers:
            pl.semaphore_signal(sem, inc=1, device_id=peer, device_id_type=MESH)

    def columns_of(ref, owner):
        return ref.at[:, pl.ds(pl.multiple_of(owner * Dh, 128), Dh)]

    owners = [p["dp"] for p in partners]
    out_loads = [pltpu.make_async_copy(wo_ref, columns_of(wo_v, dp), w_sem.at[0])] + [
        pltpu.make_async_copy(columns_of(wo_other, p), columns_of(wo_v, p), w_sem.at[1 + o])
        for o, p in enumerate(owners)
    ]
    for copy in out_loads:
        copy.start()
    entry = pltpu.get_barrier_semaphore()
    signal_all(entry, others)
    gsum[...] = jnp.zeros_like(gsum)
    pl.semaphore_wait(entry, len(others))

    def pair_copies(kind, s, src, half, dst):
        def cut(owner):
            if half:
                return src.at[..., pl.ds(pl.multiple_of(owner * Dh, 128), Dh)]
            return src

        copies = [pltpu.make_async_copy(cut(dp), dst.at[dp, s], pair_sem.at[0, kind, s])]
        for o, partner in enumerate(partners):
            copies.append(
                pltpu.make_async_remote_copy(
                    cut(partner["dp"]), dst.at[dp, s],
                    pair_sem.at[1 + 2 * o, kind, s], pair_sem.at[2 + 2 * o, kind, s],
                    device_id=partner, device_id_type=MESH,
                )
            )
        return copies

    env = {}

    def pair_of(kind, s):
        src = [
            lambda: X.at[s], lambda: env["hid"].at[s], lambda: X.at[s], lambda: Ab.at[s],
            lambda: Bb.at[s], lambda: X.at[s], lambda: heads_ref.at[:, s],
        ][kind]()
        return pair_copies(kind, s, src, kind in (0, 2, 5), pairs[kind])

    pairs = [rows_pair, hid_pair, branch_pair, gate_pair, up_pair, attn_pair, head_pair]

    def pair_start(kind, s):
        for copy in pair_of(kind, s):
            copy.start()

    def pair_kept(kind, s):
        pair_of(kind, s)[0].wait()

    def pair_away(kind, s):
        for copy in pair_of(kind, s)[1:]:
            copy.wait_send()

    def pair_received(kind, s):
        for o, partner in enumerate(partners):
            place = pairs[kind].at[dp, s]
            remote(
                place, place, pair_sem.at[1 + 2 * o, kind, s], pair_sem.at[2 + 2 * o, kind, s], partner
            ).wait_recv()

    def rs_copy(s, side, k, j):
        if side == 0:
            slot, peer = j, right
        else:
            slot, peer = jnp.where(j == t - 1, T, j), left
        return pltpu.make_async_remote_copy(
            Pb.at[s, j], Rb.at[s, slot], rs_send.at[s, side, k], rs_recv.at[s, side, k],
            device_id=peer, device_id_type=MESH,
        )

    def rs_block(side, k):
        return (T - 1 - k + t) if side == 0 else (k - (T - 1 - t))

    def rs_sends(side, k):
        return (t <= k) if side == 0 else (T - 1 - t <= k)

    def ag_copy(s, side, k, j):
        return pltpu.make_async_remote_copy(
            X.at[s, j], X.at[s, j], ag_send.at[s, side, k], ag_recv.at[s, side, k],
            device_id=right if side == 0 else left, device_id_type=MESH,
        )

    def ag_block(side, k):
        return (t - k) if side == 0 else (t + k)

    def ag_sends(side, k):
        return (t >= k) & has_right if side == 0 else (t + k <= T - 1) & has_left

    def rs_start(s):
        for side in (0, 1):

            @pl.when(rs_sends(side, 0))
            def _():
                rs_copy(s, side, 0, rs_block(side, 0)).start()

    def rs_step(s, k):
        for side in (0, 1):
            j = rs_block(side, k)
            came = has_left if side == 0 else has_right

            @pl.when(rs_sends(side, k))
            def _():
                @pl.when(came)
                def _():
                    rs_copy(s, side, k - 1, j).wait_recv()
                    Pb[s, j] = (Pb[s, j].astype(F32) + Rb[s, j].astype(F32)).astype(BF)

                rs_copy(s, side, k, j).start()

    def rs_sent(s):
        for side in (0, 1):
            for k in range(T - 1):

                @pl.when(rs_sends(side, k))
                def _():
                    rs_copy(s, side, k, rs_block(side, k)).wait_send()

    def rs_finish(s):
        acc[...] = Pb[s, t].astype(F32)

        @pl.when(has_left)
        def _():
            rs_copy(s, 0, T - 2, t).wait_recv()
            acc[...] += Rb[s, t].astype(F32)

        @pl.when(has_right)
        def _():
            rs_copy(s, 1, T - 2, t).wait_recv()
            acc[...] += Rb[s, T].astype(F32)

    def ag_start(s):
        for side in (0, 1):

            @pl.when(ag_sends(side, 0))
            def _():
                ag_copy(s, side, 0, t).start()

    def ag_step(s, k):
        for side in (0, 1):
            j = ag_block(side, k)
            there = (j >= 0) if side == 0 else (j <= T - 1)

            @pl.when(there)
            def _():
                ag_copy(s, side, k - 1, j).wait_recv()
                if k <= T - 2:

                    @pl.when(has_right if side == 0 else has_left)
                    def _():
                        ag_copy(s, side, k, j).start()

    def ag_sent(s):
        for side in (0, 1):
            for k in range(T - 1):

                @pl.when(ag_sends(side, k))
                def _():
                    ag_copy(s, side, k, ag_block(side, k)).wait_send()

    def local_rows(n, s):
        own = pl.ds(pl.multiple_of(s * rc, rc), rc)
        total = acc[...]

        @pl.when(n == 0)
        def _():
            att[s] = total
            middle = x_ref[own].astype(F32) + total * inverse_rms(total) * gain_ref[1:2]
            mid[s] = middle
            X[s, t] = (middle * inverse_rms(middle) * gain_ref[2:3]).astype(BF)

        @pl.when(n == 1)
        def _():
            scale = inverse_rms(total)
            out_ref[own] = (mid[s] + total * scale * gain_ref[3:4]).astype(BF)
            grad, terms = rms_back(total, scale, gain_ref[3:4], ct_ref[own].astype(F32))
            gsum[2:3] += terms
            X[s, t] = grad.astype(BF)

        @pl.when(n == 2)
        def _():
            middle, attention = mid[s], att[s]
            grad, terms = rms_back(middle, inverse_rms(middle), gain_ref[2:3], total)
            gsum[1:2] += terms
            middle_delta = ct_ref[own].astype(F32) + grad
            mdelta[own] = middle_delta
            grad, terms = rms_back(attention, inverse_rms(attention), gain_ref[1:2], middle_delta)
            gsum[0:1] += terms
            X[s, t] = grad.astype(BF)

    def comm(tau, w, a):
        back = tau - a

        @pl.when((back >= 0) & (back < 3 * C))
        def _():
            n, s = back // C, lax.rem(back, C)
            if w <= T - 2:
                rs_step(s, w)
            elif w == T - 1:
                rs_finish(s)
                local_rows(n, s)
                ag_start(s)
            else:
                ag_step(s, w - (T - 1))

    def tiles(width, body):
        tile = tile_of(width)

        def step(i, carry):
            body(pl.ds(pl.multiple_of(i * tile, tile), tile), tile)
            return carry

        lax.fori_loop(0, width // tile, step, 0)

    def rows_of(s):
        return X[s].reshape(M, D)

    def store_part(s, at, tile, value):
        Pb[s, :, :, at] = value.astype(BF).reshape(T, rc, tile)

    pitch = -(-RB // 16) * 16
    orders = [bits_below(NC), bits_below(NC)[::-1]]
    first_of = [sum(NC >> (i + 1) for i in range(k)) for k in range(m)]

    def block_of(i, w):
        down = D // pitch
        row = pl.multiple_of(lax.rem(i, down) * pitch, 16)
        return wd_v.at[pl.ds(row, RB), pl.ds(pl.multiple_of((i // down) * W, 128), w)]

    def part_of(u, par, owner, w):
        return block_of((lax.rem(u, NP) * 2 + par) * NC + owner, w)

    def came_of(u, par, at, w):
        return block_of(NP * 2 * NC + (lax.rem(u, NR) * 2 + par) * (NC - 1) + at, w)

    def e_copy(u, par, k, n, w):
        order = orders[par]
        at = first_of[k] + n
        return remote(
            part_of(u, par, flips(c, sub_sums(order[k + 1:])[n] + order[k]), w), came_of(u, par, at, w),
            e_send.at[lax.rem(u, NP), par, at], e_recv.at[lax.rem(u, NR), par, at],
            along("ctx", flip(c, order[k])),
        )

    def e_each(k, act):
        for par in (0, 1):
            for n in range(NC >> (k + 1)):
                act(par, n)

    def e_sent(u, w):
        for k in range(m):
            e_each(k, lambda par, n: e_copy(u, par, k, n, w).wait_send())

    def e_send_step(u, k, w):
        e_each(k, lambda par, n: e_copy(u, par, k, n, w).start())

    def e_add(u, k, w):
        def one(par, n):
            e_copy(u, par, k, n, w).wait_recv()
            if k < m - 1:
                ref = part_of(u, par, flips(c, sub_sums(orders[par][k + 1:])[n]), w)
                ref[...] = (ref[...].astype(F32) + came_of(u, par, first_of[k] + n, w)[...].astype(F32)).astype(BF)

        e_each(k, one)

    chunks = [hid_pair, gate_pair, up_pair]

    def chunk_copy(u, kind):
        at = pl.ds(pl.multiple_of((u - kind * NF) * 2 * W, 128), 2 * W)
        return pltpu.make_async_copy(chunks[kind].at[:, :, :, at], Rc, r_sem.at[0])

    def for_kind(u, act):
        for kind in range(3):

            @pl.when((u >= kind * NF) & (u < (kind + 1) * NF))
            def _():
                act(kind)

    branch_load = pltpu.make_async_copy(branch_pair, L0, l_sem.at[0])

    def store(u, par, w, first, second):
        product = dot_tn(first.reshape(tokens, Dh), second)
        for owner in range(NC):
            part_of(u, par, owner, w)[...] = product[owner * RB:(owner + 1) * RB].astype(BF)

    def wide_product(u):
        for_kind(u, lambda kind: chunk_copy(u, kind).wait())
        def each(par, carry):
            second = Rc[:, :, :, pl.ds(pl.multiple_of(par * W, 128), W)].reshape(tokens, W)

            @pl.when(u < NF)
            def _():
                store(u, par, W, L0[...], second)

            if "L" in env:

                @pl.when(u >= NF)
                def _():
                    store(u, par, W, env["L"][0], second)

            return carry

        lax.fori_loop(0, 2, each, 0)
        for_kind(u + 1, lambda kind: chunk_copy(u + 1, kind).start())

    def out_copies(u, w):
        two = lax.rem(u, 2)

        def copy(par, dst):
            return pltpu.make_async_copy(st.at[two, par, :, pl.ds(0, w)], dst, st_sem.at[two, par])

        def columns(dst, base):
            return dst.at[:, pl.ds(pl.multiple_of(base, 128), w)]

        if w == W and w != narrow:
            spans = [(0, NF, down_o), (NF, 2 * NF, gate_o), (2 * NF, 3 * NF, up_o)]
        elif w == W:
            spans = [(0, NF, down_o), (NF, 2 * NF, gate_o), (2 * NF, 3 * NF, up_o)]
            spans += [(wide_units, q_first, out_o), (q_first, kv_first, q_o)]
        else:
            spans = [(wide_units, q_first, out_o), (q_first, kv_first, q_o)]
        found = [
            (
                (u >= low) & (u < high),
                [copy(p, columns(dst, (u - low) * 2 * w + p * w)) for p in (0, 1)],
            )
            for low, high, dst in spans
        ]
        if w == narrow:
            base = (u - kv_first) * w
            found.append(((u >= kv_first) & (u < units), [copy(0, columns(k_o, base)), copy(1, columns(v_o, base))]))
        return found

    widths = [W] if W == narrow else [W, narrow]

    def out_wait(u):
        for w in widths:
            for here, copies in out_copies(u, w):

                @pl.when(here)
                def _():
                    for copy in copies:
                        copy.wait()

    def e_finish(u, w):
        e_add(u, m - 1, w)
        out_wait(u - 2)
        for par in (0, 1):
            total = part_of(u, par, c, w)[...].astype(F32) + came_of(u, par, first_of[m - 1], w)[...].astype(F32)
            st[lax.rem(u, 2), par, :, :w] = total.astype(BF)
        for here, copies in out_copies(u, w):

            @pl.when(here)
            def _():
                for copy in copies:
                    copy.start()

    def by_width(u, body):
        @pl.when((u >= 0) & (u < wide_units))
        def _():
            body(W)

        @pl.when((u >= wide_units) & (u < units))
        def _():
            body(narrow)

    def compute_open(s):
        signal_all(free_sem, ctx_meets)
        pair_kept(2, s)

        def each(i, carry):
            pair_kept(1, i)
            pair_received(1, i)
            pair_received(2, i)
            return carry

        lax.fori_loop(0, C, each, 0)
        branch_load.start()
        chunk_copy(jnp.int32(0), 0).start()

    def stages(wg_v, wu_v, hid):
        env.update(hid=hid)
        def load_copies(i):
            height, turned_height = D // (2 * T), F // (2 * T)
            part = pl.ds(pl.multiple_of(i * height, 16), height)
            turned_part = pl.ds(pl.multiple_of(i * turned_height, 16), turned_height)
            inner = pl.ds(pl.multiple_of(lax.rem(i * height, Dh), 16), height)
            return (
                pltpu.make_async_copy(wg_ref.at[inner], wg_v.at[part], f_sem.at[0, i]),
                pltpu.make_async_copy(wg_other.at[part], wg_v.at[part], f_sem.at[0, i]),
                pltpu.make_async_copy(wut_ref.at[turned_part], wu_v.at[turned_part], f_sem.at[1, i]),
                pltpu.make_async_copy(wdt_ref.at[part], wd_v.at[part], f_sem.at[2, i]),
            )

        def load_start(i):
            own, other, up_part, down_part = load_copies(i)
            here = (i * (D // (2 * T))) // Dh == dp
            pl.when(here)(own.start)
            pl.when(jnp.logical_not(here))(other.start)
            up_part.start()
            down_part.start()

        def load_wait(which):
            def each(i, carry):
                load_copies(i)[which + 1].wait()
                return carry

            lax.fori_loop(0, 2 * T, each, 0)

        def gate_up(s, at):
            gate = dot_nn(rows_of(s), wg_v[:, at])
            up = dot_nt(rows_of(s), wu_v[at, :])
            inner = jnp.tanh(0.7978845608028654 * (gate + 0.044715 * gate * gate * gate))
            half = 0.5 * (1.0 + inner)
            gelu = gate * half
            slope = half + 0.5 * gate * (1.0 - inner * inner) * (
                0.7978845608028654 * (1.0 + 0.134145 * gate * gate)
            )
            hid[s, :, at] = (gelu * up).astype(BF)
            Ab[s, :, at] = (up * slope).astype(BF)
            Bb[s, :, at] = gelu.astype(BF)

        def gate_up_delta(s, at):
            delta = dot_nn(rows_of(s), wd_v[:, at])
            Ab[s, :, at] = (delta * Ab[s, :, at].astype(F32)).astype(BF)
            Bb[s, :, at] = (delta * Bb[s, :, at].astype(F32)).astype(BF)

        def tick(tau, carry):
            n, s = tau // C, lax.rem(tau, C)

            @pl.when(n >= 1)
            def _():
                rs_sent(s)

            @pl.when(n == 0)
            def _():
                load_start(2 * tau)

            @pl.when(n == 1)
            def _():
                @pl.when(s == 0)
                def _():
                    load_wait(0)
                    load_wait(1)

                pair_start(0, s)
                tiles(F, lambda at, tile: gate_up(s, at))
                pair_start(1, s)

            @pl.when(n == 2)
            def _():
                pair_start(2, s)
                tiles(F, lambda at, tile: gate_up_delta(s, at))
                pair_start(3, s)
                pair_start(4, s)

            @pl.when(tau == begin)
            def _():
                compute_open(s)
                branch_load.wait()
                wide_product(jnp.int32(0))
                pl.semaphore_wait(free_sem, len(ctx_meets))
                e_send_step(jnp.int32(0), 0, W)

            for a in range(1, T):
                comm(tau, 2 * a - 1, a)

            @pl.when(n == 0)
            def _():
                load_start(2 * tau + 1)
                pair_start(6, s)
                heads = heads_ref[:, s].reshape(M, Hq)
                tiles(D, lambda at, tile: store_part(s, at, tile, dot_nn(heads, wo_v[:, at])))

            @pl.when(n == 1)
            def _():
                @pl.when(s == 0)
                def _():
                    load_wait(2)

                tiles(D, lambda at, tile: store_part(s, at, tile, dot_nt(hid[s], wd_v[at, :])))
                pair_kept(0, s)
                pair_away(0, s)
                ag_sent(s)

            @pl.when(n == 2)
            def _():
                tiles(
                    D,
                    lambda at, tile: store_part(
                        s, at, tile, dot_nt(Ab[s], wg_v[at, :]) + dot_nn(Bb[s], wu_v[:, at])
                    ),
                )
                pair_away(2, s)

                @pl.when(s < C - 1)
                def _():
                    pair_kept(2, s)

                ag_sent(s)

            rs_start(s)
            for a in range(1, T):
                comm(tau, 2 * a, a)
            return carry

        lax.fori_loop(0, 3 * C, tick, 0)

        def leave(s, carry):
            pair_away(1, s)
            return carry

        lax.fori_loop(0, C, leave, 0)
        del env["hid"]

    def finishing(L, Hd, RQ, RKV, WQ, WK, WV, dq, rdelta, kvb, kvs, kvr, acc2, qv, cos_v, sin_v):
        env["L"] = L
        signal_all(enter_sem, later + partners)
        rows_load = pltpu.make_async_copy(rows_pair, L.at[0], l_sem.at[1])
        attn_load = pltpu.make_async_copy(attn_pair, L.at[1], l_sem.at[2])
        rows1_load = pltpu.make_async_copy(rows1_ref, L.at[0], l_sem.at[1])
        head_load = pltpu.make_async_copy(head_pair, Hd, l_sem.at[3])
        small_loads = [
            pltpu.make_async_copy(src, dst, q_sem.at[i])
            for i, (src, dst) in enumerate([(q_ref, qv), (cos_ref, cos_v), (sin_ref, sin_v)])
        ]
        for copy in small_loads:
            copy.start()

        rows_at = pl.ds(pl.multiple_of(dp * Dh, 128), Dh)
        spread = [(wq_ref, WQ.at[rows_at]), (wk_ref, WK.at[rows_at]), (wv_ref, WV.at[rows_at])]

        def spread_local(i):
            return pltpu.make_async_copy(*spread[i], s_sem.at[0, i])

        def spread_remote(i, o):
            return remote(*spread[i], s_sem.at[1 + 2 * o, i], s_sem.at[2 + 2 * o, i], partners[o])

        def pair_remote(i, o):
            ref = [RQ, RKV][i]
            return remote(ref.at[dp], ref.at[dp], q_sem.at[3 + 4 * o + 2 * i], q_sem.at[4 + 4 * o + 2 * i], partners[o])

        def deltas_of(head):
            return hdelta[:, :, :, head].reshape(R, HEAD)

        per = max(1, 256 // Lr)
        key_tile = per * Lr

        def kv_copy(d):
            return remote(
                kvs.at[lax.rem(d, kvs.shape[0])], kvr.at[d - 1], kv_send.at[d - 1], kv_recv.at[d - 1],
                along("ctx", jnp.maximum(c - d, 0)),
            )

        def block_copy(block):
            two = lax.rem(block, 2)
            return pltpu.make_async_copy(kv_ref.at[block], kvb.at[two], kvb_sem.at[two])

        def attend(two, masked, dst):
            for kh in range(KH):
                cols = slice(kh * HEAD, (kh + 1) * HEAD)

                def key_step(i, carry):
                    start = pl.multiple_of(i * key_tile, key_tile)
                    at = pl.ds(i * per, per)
                    keys = kvb[two, at, 0, :, cols].reshape(key_tile, HEAD)
                    values = kvb[two, at, 1, :, cols].reshape(key_tile, HEAD)
                    key_sum = jnp.zeros((key_tile, HEAD), F32)
                    value_sum = jnp.zeros((key_tile, HEAD), F32)
                    for g in range(GS):
                        h = kh * GS + g
                        head = slice(h * HEAD, (h + 1) * HEAD)
                        query, delta = qv[:, head], deltas_of(head)
                        bent = jnp.tanh(dot_nt(keys, query) * (scale / CAP))
                        prob = jnp.exp(CAP * bent - logt_ref[h:h + 1, :])
                        if masked:
                            key_pos = start + lax.broadcasted_iota(jnp.int32, prob.shape, 0)
                            prob = jnp.where(key_pos <= lax.broadcasted_iota(jnp.int32, prob.shape, 1), prob, 0.0)
                        grad = prob * (dot_nt(values, delta) - rdelta[h:h + 1, :]) * (1.0 - bent * bent)
                        grad = grad.astype(BF)
                        value_sum += dot_nn(prob.astype(BF), delta)
                        key_sum += dot_nn(grad, query)
                        dq[:, head] += dot_tn(grad, keys)
                    rows = pl.ds(start, key_tile)
                    kvs[dst, 0, rows, cols] = (key_sum * scale).astype(BF)
                    kvs[dst, 1, rows, cols] = value_sum.astype(BF)
                    return carry

                lax.fori_loop(0, R // key_tile, key_step, 0)

        def attention():
            dq[...] = jnp.zeros_like(dq)
            for h in range(Hq // HEAD):
                head = slice(h * HEAD, (h + 1) * HEAD)
                product = deltas_of(head).astype(F32) * heads_ref[:, :, :, head].reshape(R, HEAD).astype(F32)
                rdelta[h:h + 1] = jnp.sum(product.T, axis=0, keepdims=True)
            block_copy(0).start()

            def far(block, carry):
                d = c - block

                @pl.when(block < c)
                def _():
                    slot = lax.rem(d, kvs.shape[0])
                    block_copy(block).wait()
                    block_copy(block + 1).start()

                    @pl.when(d + kvs.shape[0] <= c)
                    def _():
                        kv_copy(d + kvs.shape[0]).wait_send()

                    attend(lax.rem(block, 2), False, slot)
                    kv_copy(d).start()

                return carry

            lax.fori_loop(0, NC - 1, far, 0)

            @pl.when(c >= kvs.shape[0])
            def _():
                kv_copy(kvs.shape[0]).wait_send()

            block_copy(c).wait()
            attend(lax.rem(c, 2), True, 0)

        def turned(values, h):
            a, b = values[:, h * HEAD:h * HEAD + HEAD // 2], values[:, h * HEAD + HEAD // 2:(h + 1) * HEAD]
            cosine, sine = cos_v[...], sin_v[...]
            return jnp.concatenate([a * cosine + b * sine, b * cosine - a * sine], axis=1).astype(BF)

        def last_copy(side, k, j):
            if side == 0:
                slot, peer = j, right
            else:
                slot, peer = jnp.where(j == t - 1, T, j), left
            return remote(Pb.at[:, j], Rb.at[:, slot], last_send.at[side, k], last_recv.at[side, k], peer)

        def last_step(k):
            for side in (0, 1):
                j = rs_block(side, k)

                @pl.when(rs_sends(side, k))
                def _():
                    if k:

                        @pl.when(has_left if side == 0 else has_right)
                        def _():
                            last_copy(side, k - 1, j).wait_recv()
                            Pb[:, j] = (Pb[:, j].astype(F32) + Rb[:, j].astype(F32)).astype(BF)

                    last_copy(side, k, j).start()

        def own_keys():
            for which in range(2):
                dst = []
                for kh in range(KH):
                    dst.append(kvs[0, which, :, kh * HEAD:(kh + 1) * HEAD].astype(F32))
                acc2[which] = jnp.concatenate(dst, axis=1) if KH > 1 else dst[0]

            def come(i, carry):
                d = i + 1

                @pl.when(c + d <= NC - 1)
                def _():
                    kv_copy(d).wait_recv()
                    for which in range(2):
                        acc2[which] += kvr[d - 1, which].astype(F32)

                return carry

            lax.fori_loop(0, NC - 1, come, 0)
            for kh in range(KH):
                cols = slice(kh * HEAD, (kh + 1) * HEAD)
                RKV[dp, 0, :, cols] = turned(acc2[0], kh)
            RKV[dp, 1] = acc2[1].astype(BF)
            for h in range(Hq // HEAD):
                RQ[dp, :, h * HEAD:(h + 1) * HEAD] = turned(dq[...] * scale, h)
            for i in range(2):
                for o in range(NDP - 1):
                    pair_remote(i, o).start()
            for i in range(3):
                spread_local(i).wait()
                for o in range(NDP - 1):
                    spread_remote(i, o).wait_recv()
            tile = tile_of(D)

            def part(i, carry):
                at = pl.ds(pl.multiple_of(i * tile, tile), tile)
                terms = dot_nt(RQ[dp], WQ[at, :]) + dot_nt(RKV[dp, 0], WK[at, :]) + dot_nt(RKV[dp, 1], WV[at, :])
                terms = terms.astype(BF).reshape(T, C, rc, tile)
                for s in range(C):
                    Pb[s, :, :, at] = terms[:, s]
                return carry

            lax.fori_loop(0, D // tile, part, 0)
            last_step(0)

        def last_finish():
            igrad_ref[...] = Pb[:, t].reshape(Lr, D).astype(F32)

            @pl.when(has_left)
            def _():
                last_copy(0, T - 2, t).wait_recv()
                igrad_ref[...] += Rb[:, t].reshape(Lr, D).astype(F32)

            @pl.when(has_right)
            def _():
                last_copy(1, T - 2, t).wait_recv()
                igrad_ref[...] += Rb[:, T].reshape(Lr, D).astype(F32)

            rows = x_ref[...].astype(F32)
            grad, terms = rms_back(rows, inverse_rms(rows), gain_ref[0:1], igrad_ref[...])
            igrad_ref[...] = mdelta[...] + grad
            G[0, 0:1] = terms
            G[0, 1:4] = gsum[...]

        meets = [("tp", t, b) for b in bits_below(T)] + [("ctx", c, b) for b in bits_below(NC)]
        meets += [("dp", dp, b) for b in bits_below(NDP)]

        def g_copy(k):
            axis, index, bit = meets[k]
            return remote(G.at[k], GR.at[k], g_send.at[k], g_recv.at[k], along(axis, flip(index, bit)))

        def g_steps(i, half):
            for k in range(half, len(meets), 2):

                @pl.when(i == C + T + 2 + k // 2)
                def _():
                    g_copy(k).wait_recv()
                    G[k + 1] = G[k] + GR[k]
                    if k + 1 < len(meets):
                        g_copy(k + 1).start()

        def up_open():
            def each(s, carry):
                for kind in (3, 4):
                    pair_kept(kind, s)
                    pair_received(kind, s)
                pair_received(0, s)
                return carry

            lax.fori_loop(0, C, each, 0)
            rows_load.start()

        def attn_open():
            def each(s, carry):
                for kind in (5, 6):
                    pair_kept(kind, s)
                    pair_received(kind, s)
                return carry

            lax.fori_loop(0, C, each, 0)
            attn_load.start()
            head_load.start()

        def product(u, w):
            @pl.when(u < wide_units)
            def _():
                @pl.when(u == NF)
                def _():
                    rows_load.wait()

                @pl.when(u == NF - 1)
                def _():
                    up_open()

                wide_product(u)

                @pl.when(u == wide_units - 1)
                def _():
                    attn_open()

            if w == narrow:

                def columns(first, par):
                    return pl.ds(pl.multiple_of(((u - first) * 2 + par) * narrow, 128), narrow)

                @pl.when((u >= wide_units) & (u < q_first))
                def _():
                    @pl.when(u == wide_units)
                    def _():
                        attn_load.wait()
                        head_load.wait()
                        rows1_load.start()

                    def out_part(par, carry):
                        second = Hd[:, :, :, :, columns(wide_units, par)]
                        store(u, par, narrow, L[1], second.reshape(tokens, narrow))
                        return carry

                    lax.fori_loop(0, 2, out_part, 0)

                @pl.when(u == q_first)
                def _():
                    rows1_load.wait()
                    for p in range(2):
                        for o in range(NDP - 1):
                            pair_remote(p, o).wait_recv()

                @pl.when((u >= q_first) & (u < kv_first))
                def _():
                    def query_part(par, carry):
                        store(u, par, narrow, L[0], RQ[:, :, columns(q_first, par)].reshape(tokens, narrow))
                        return carry

                    lax.fori_loop(0, 2, query_part, 0)

                @pl.when(u >= kv_first)
                def _():
                    at = pl.ds(pl.multiple_of((u - kv_first) * narrow, 128), narrow)
                    def key_part(par, carry):
                        store(u, par, narrow, L[0], RKV[:, par, :, at].reshape(tokens, narrow))
                        return carry

                    lax.fori_loop(0, 2, key_part, 0)

        def tick(i, carry):
            u = i + 1

            def start(w):
                @pl.when(u >= NP)
                def _():
                    by_width(u - NP, lambda before: e_sent(u - NP, before))

                product(u, w)
                e_send_step(u, 0, w)

            by_width(u, start)
            g_steps(i, 0)

            @pl.when(i == 1)
            def _():
                pl.semaphore_wait(enter_sem, len(later + partners))
                for w in range(3):
                    spread_local(w).start()
                    for o in range(NDP - 1):
                        spread_remote(w, o).start()

            @pl.when(i < C)
            def _():
                tau = 3 * C + i
                for a in range(1, T):
                    comm(tau, 2 * a - 1, a)
                pair_start(5, i)
                hdelta[:, i] = dot_nt(rows_of(i), wo_v[...]).astype(BF).reshape(T, rc, Hq)
                rs_sent(i)
                for a in range(1, T):
                    comm(tau, 2 * a, a)

            @pl.when(i == C)
            def _():
                for copy in small_loads:
                    copy.wait()
                attention()

            @pl.when(i == C + 2)
            def _():
                own_keys()

            for k in range(1, T - 1):

                @pl.when(i == C + 2 + k)
                def _():
                    last_step(k)

            @pl.when(i == C + T + 1)
            def _():
                last_finish()
                g_copy(0).start()

            for k in range(1, m):

                def middle(w):
                    e_add(u - k, k - 1, w)
                    e_send_step(u - k, k, w)

                by_width(u - k, middle)
            by_width(u - m, lambda w: e_finish(u - m, w))
            g_steps(i, 1)
            return carry

        lax.fori_loop(0, units + m - 1, tick, 0)
        gains_ref[...] = G[len(meets)]

        for u in (units - 2, units - 1):
            out_wait(jnp.int32(u))
        for u in range(units - NP, units):
            by_width(jnp.int32(u), lambda w: e_sent(jnp.int32(u), w))
        for side in (0, 1):
            for k in range(T - 1):

                @pl.when(rs_sends(side, k))
                def _():
                    last_copy(side, k, rs_block(side, k)).wait_send()

        for k in range(len(meets)):
            g_copy(k).wait_send()
        for o in range(NDP - 1):
            for i in range(3):
                spread_remote(i, o).wait_send()
            for i in range(2):
                pair_remote(i, o).wait_send()

        def kv_close(i, carry):
            d = i + 1

            @pl.when((d <= c) & (d < kvs.shape[0]))
            def _():
                kv_copy(d).wait_send()

            return carry

        lax.fori_loop(0, min(NC - 1, kvs.shape[0] - 1), kv_close, 0)

        def close(s, carry):
            for kind in (3, 4, 5, 6):
                pair_away(kind, s)
            ag_sent(s)
            return carry

        lax.fori_loop(0, C, close, 0)

    for copy in out_loads:
        copy.wait()
    vmem = pltpu.VMEM
    pl.run_scoped(
        stages, vmem((D, F), BF), vmem((F, D), BF), vmem((C, M, F), BF)
    )
    kv_slots = min(NC, 3)
    pl.run_scoped(
        finishing,
        vmem((2, NDP, C, T, rc, Dh), BF), vmem((NDP, C, T, rc, Hq), BF),
        vmem((NDP, R, Hq), BF), vmem((NDP, 2, R, KVd), BF),
        vmem((D, Hq), BF), vmem((D, KVd), BF), vmem((D, KVd), BF),
        vmem((R, Hq), F32), vmem((Hq // HEAD, R), F32), vmem((2, T, 2, Lr, KVd), BF),
        vmem((kv_slots, 2, R, KVd), BF), vmem((NC - 1, 2, R, KVd), BF), vmem((2, R, KVd), F32),
        vmem((R, Hq), BF), vmem((R, HEAD // 2), F32), vmem((R, HEAD // 2), F32),
    )


def main_call(
    layer_in, cotangent, norm_gains, head_rows, w_out, w_gate, out_other, gate_other, up_turned, down_turned,
    query, log_totals, cosine, sine, keys_values, rows_one, w_query, w_key, w_value,
):
    T, NC, NDP = lax.axis_size("tp"), lax.axis_size("ctx"), lax.axis_size("dp")
    C = T
    Lr, D = layer_in.shape
    rc = Lr // C
    R, Hq = query.shape
    KVd = w_key.shape[1]
    Dh, RB = D // NDP, D // NDP // NC
    F = w_gate.shape[1]
    M = T * rc
    m = NC.bit_length() - 1
    NP, NR = m + 1, 4
    pitch = -(-RB // 16) * 16
    blocks = NP * 2 * NC + NR * 2 * (NC - 1)
    W = next(w for w in (tile_of(F) // 2, 256, 128) if F % (2 * w) == 0 and blocks <= (D // pitch) * (F // w))
    meets = sum(n.bit_length() - 1 for n in (T, NC, NDP))
    any_spec = pl.BlockSpec(memory_space=pl.ANY)
    vm = pl.BlockSpec(memory_space=pltpu.VMEM)
    sds = jax.ShapeDtypeStruct
    dma = pltpu.SemaphoreType.DMA
    vmem = pltpu.VMEM
    half_rows = sds((NDP, C, T, rc, Dh), BF)
    hidden_rows = sds((NDP, C, M, F), BF)
    outs = pl.pallas_call(
        functools.partial(main_kernel, T, C, NC, NDP, KVd // HEAD, NP, NR),
        out_shape=(
            sds((Lr, D), BF), sds((Lr, D), F32), sds((4, D), F32),
            sds((RB, F), BF), sds((RB, F), BF), sds((RB, F), BF), sds((RB, Hq), BF),
            sds((RB, Hq), BF), sds((RB, KVd), BF), sds((RB, KVd), BF),
            half_rows, hidden_rows, half_rows, hidden_rows, hidden_rows, half_rows, sds((NDP, C, T, rc, Hq), BF),
        ),
        in_specs=[vm] * 4 + [any_spec] * 7 + [vm] + [any_spec] * 7,
        out_specs=[vm] * 3 + [any_spec] * 14,
        scratch_shapes=[
            vmem((Hq, D), BF), vmem((D, F), BF), vmem((C, T, rc, D), BF), vmem((C, T, rc, D), BF),
            vmem((C, T + 1, rc, D), BF), vmem((C, rc, D), F32), vmem((C, rc, D), F32), vmem((rc, D), F32),
            vmem((Lr, D), F32), vmem((3, D), F32), vmem((T, C, rc, Hq), BF), vmem((C, M, F), BF), vmem((C, M, F), BF),
            vmem((NDP, C, T, rc, Dh), BF), vmem((NDP, C, M, 2 * W), BF), vmem((2, 2, RB, W), BF),
            vmem((meets + 1, 4, D), F32), vmem((meets, 4, D), F32),
            dma((NDP,)), dma((3, 2 * T)), dma((C, 2, T - 1)), dma((C, 2, T - 1)), dma((C, 2, T - 1)), dma((C, 2, T - 1)),
            dma((2 * NDP - 1, 7, C)), dma((4,)), dma((1,)), dma((NP, 2, NC - 1)), dma((NR, 2, NC - 1)), dma((2, 2)),
            dma((2 * NDP - 1, 3)), dma((3 + 4 * (NDP - 1),)), dma((NC - 1,)), dma((NC - 1,)),
            dma((2, T - 1)), dma((2, T - 1)), dma((meets,)), dma((meets,)), dma((2,)),
            pltpu.SemaphoreType.REGULAR, pltpu.SemaphoreType.REGULAR,
        ],
        compiler_params=pltpu.CompilerParams(
            collective_id=0, has_side_effects=True, vmem_limit_bytes=67_043_328
        ),
        name="main",
    )(
        layer_in, cotangent, norm_gains, head_rows.reshape(T, C, rc, Hq), w_out, w_gate, out_other, gate_other,
        up_turned, down_turned, query, log_totals, cosine, sine, keys_values,
        rows_one.reshape(NDP, C, T, rc, Dh), w_query, w_key, w_value,
    )
    return outs[:10]


def front_kernel(
    T, NC, NDP, KH, C,
    x_ref, gain_ref, freq_ref, wq_ref, wk_ref, wv_ref, wo_ref, wg_ref, wu_ref, wd_ref,
    q_o, heads_o, logt_o, cos_o, sin_o, kv_o, rows1_o, wo_o, wg_o, wut_o, wdt_o,
    X, WQ, WK, WV, KV, turned_sum, totals, up_v, upt_v, down_v, downt_v,
    w_sem, ag_send, ag_recv, pair_sem, kv_send, kv_recv, out_sem, t_sem, p_sem,
):
    t, c, dp = lax.axis_index("tp"), lax.axis_index("ctx"), lax.axis_index("dp")
    Lr, D = x_ref.shape
    R, Hq = q_o.shape
    rc = Lr // C
    KVd = KH * HEAD
    GS = Hq // KVd
    Dh = D // NDP
    scale = HEAD**-0.5
    has_left, has_right = t > 0, t < T - 1

    def remote(src, dst, send, recv, axis, index):
        return pltpu.make_async_remote_copy(
            src, dst, send, recv, device_id={axis: index}, device_id_type=MESH
        )

    partners = [lax.rem(dp + o, NDP) for o in range(1, NDP)]
    peers = [("tp", lax.rem(t + o, T)) for o in range(1, T)]
    peers += [("ctx", lax.rem(c + o, NC)) for o in range(1, NC)]
    peers += [("dp", p) for p in partners]
    sem = pltpu.get_barrier_semaphore()
    for axis, index in peers:
        pl.semaphore_signal(sem, inc=1, device_id={axis: index}, device_id_type=MESH)

    rows_at = pl.ds(pl.multiple_of(dp * Dh, 128), Dh)
    weights = [(wq_ref, WQ), (wk_ref, WK), (wv_ref, WV)]

    def weight_local(i):
        return pltpu.make_async_copy(weights[i][0], weights[i][1].at[rows_at], w_sem.at[0, i])

    def weight_remote(i, o):
        return remote(
            weights[i][0], weights[i][1].at[rows_at], w_sem.at[1 + 2 * o, i], w_sem.at[2 + 2 * o, i],
            "dp", partners[o],
        )

    turns = [
        pltpu.make_async_copy(wu_ref, up_v, t_sem.at[0]),
        pltpu.make_async_copy(wd_ref, down_v, t_sem.at[1]),
    ]
    for i in range(3):
        weight_local(i).start()
    for copy in turns:
        copy.start()
    rows = x_ref[...].astype(F32)
    X[t] = (rows * inverse_rms(rows) * gain_ref[0:1]).astype(BF)
    pl.semaphore_wait(sem, len(peers))

    def ag_copy(s, side, k, j):
        at = pl.ds(s * rc, rc)
        peer = jnp.minimum(t + 1, T - 1) if side == 0 else jnp.maximum(t - 1, 0)
        return remote(X.at[j, at], X.at[j, at], ag_send.at[s, side, k], ag_recv.at[s, side, k], "tp", peer)

    def ag_block(side, k):
        return (t - k) if side == 0 else (t + k)

    def ag_there(side, k):
        return (t >= k) if side == 0 else (t + k <= T - 1)

    def onward(side):
        return has_right if side == 0 else has_left

    for s in range(C):
        for side in (0, 1):

            @pl.when(onward(side))
            def _():
                ag_copy(s, side, 0, t).start()

    for i in range(3):
        for o in range(NDP - 1):
            weight_remote(i, o).start()

    def parts(ref, i):
        height = ref.shape[0] // T
        return pl.ds(pl.multiple_of(i * height, 16), height), height

    def part_dst(dst, ref, i, columns):
        at, height = parts(ref, i)
        if columns:
            return dst.at[at, rows_at]
        return dst.at[pl.ds(pl.multiple_of(dp * Dh + i * height, 16), height)]

    moved = [(wo_ref, wo_o, True, False), (wg_ref, wg_o, False, False)]
    moved += [(upt_v, wut_o, True, True), (downt_v, wdt_o, False, True)]

    def part_remote(w, i, o):
        src, dst, columns, _ = moved[w]
        return remote(
            src.at[parts(src, i)[0]], part_dst(dst, src, i, columns),
            p_sem.at[1 + 2 * o, w, i], p_sem.at[2 + 2 * o, w, i], "dp", partners[o],
        )

    def part_local(w, i):
        src, dst, columns, _ = moved[w]
        return pltpu.make_async_copy(src.at[parts(src, i)[0]], part_dst(dst, src, i, columns), p_sem.at[0, w, i])

    def part_start(w, i):
        for o in range(NDP - 1):
            part_remote(w, i, o).start()
        if moved[w][3]:
            part_local(w, i).start()

    def turn():
        for copy, src, dst in zip(turns, (up_v, down_v), (upt_v, downt_v), strict=True):
            copy.wait()
            height = src.shape[0] // T

            def some(i, carry):
                at = pl.ds(pl.multiple_of(i * height, 128), height)
                dst[:, at] = src[at, :].T
                return carry

            if height % 128 == 0:
                lax.fori_loop(0, T, some, 0)
            else:
                dst[...] = src[...].T

    position = (c * R + lax.broadcasted_iota(jnp.int32, (R, HEAD // 2), 0)).astype(F32)
    angles = position * freq_ref[...]
    cos_o[...] = jnp.cos(angles)
    sin_o[...] = jnp.sin(angles)
    for i in range(3):
        weight_local(i).wait()
        for o in range(NDP - 1):
            weight_remote(i, o).wait_recv()

    def kv_copy(d, j):
        return remote(
            KV.at[c, j], KV.at[c, j], kv_send.at[d - 1, j], kv_recv.at[d - 1, j],
            "ctx", jnp.minimum(c + d, NC - 1),
        )

    def kv_from(b, j):
        d = c - b
        return remote(KV.at[b, j], KV.at[b, j], kv_send.at[d - 1, j], kv_recv.at[d - 1, j], "ctx", c)

    def pair_copies(j):
        def half(owner):
            return X.at[j, :, pl.ds(pl.multiple_of(owner * Dh, 128), Dh)]

        copies = [pltpu.make_async_copy(half(dp), rows1_o.at[dp, j], pair_sem.at[0, j])]
        for o, partner in enumerate(partners):
            copies.append(
                remote(
                    half(partner), rows1_o.at[dp, j], pair_sem.at[1 + 2 * o, j], pair_sem.at[2 + 2 * o, j],
                    "dp", partner,
                )
            )
        return copies

    def turned(values, h, at):
        a, b = values[:, h * HEAD:h * HEAD + HEAD // 2], values[:, h * HEAD + HEAD // 2:(h + 1) * HEAD]
        cosine, sine = cos_o[at], sin_o[at]
        return jnp.concatenate([a * cosine - b * sine, b * cosine + a * sine], axis=1).astype(BF)

    def project(j):
        for copy in pair_copies(j):
            copy.start()
        at = pl.ds(pl.multiple_of(j * Lr, Lr), Lr)
        values = dot_nn(X[j], WK[...])
        for kh in range(KH):
            KV[c, j, 0, :, kh * HEAD:(kh + 1) * HEAD] = turned(values, kh, at)
        KV[c, j, 1] = dot_nn(X[j], WV[...]).astype(BF)

        def push(i, carry):
            @pl.when(c + 1 + i <= NC - 1)
            def _():
                kv_copy(i + 1, j).start()

            return carry

        lax.fori_loop(0, NC - 1, push, 0)
        values = dot_nn(X[j], WQ[...])
        for h in range(Hq // HEAD):
            q_o[at, h * HEAD:(h + 1) * HEAD] = turned(values, h, at)

    def gather(k, carry):
        for side in (0, 1):

            @pl.when(ag_there(side, k) & (k > 0))
            def _():
                for s in range(C):
                    ag_copy(s, side, k - 1, ag_block(side, k)).wait_recv()

                    @pl.when(onward(side) & (k <= T - 2))
                    def _():
                        ag_copy(s, side, k, ag_block(side, k)).start()

        for side in (0, 1):

            @pl.when(ag_there(side, k) & ((k > 0) | (side == 0)))
            def _():
                project(ag_block(side, k))

        part_start(0, k)
        part_start(1, k)

        @pl.when(k == 0)
        def _():
            turn()

        part_start(2, k)
        part_start(3, k)
        return carry

    lax.fori_loop(0, T, gather, 0)

    per = max(1, 256 // Lr)
    tile = per * Lr
    turned_sum[...] = jnp.zeros_like(turned_sum)
    totals[...] = jnp.zeros_like(totals)

    def out_copy(b):
        return pltpu.make_async_copy(KV.at[b], kv_o.at[b], out_sem.at[b])

    def key_step(b, p, masked):
        for kh in range(KH):
            cols = slice(kh * HEAD, (kh + 1) * HEAD)
            keys = KV[b, pl.ds(p * per, per), 0, :, cols].reshape(tile, HEAD)
            values = KV[b, pl.ds(p * per, per), 1, :, cols].reshape(tile, HEAD)
            for g in range(GS):
                h = kh * GS + g
                scores = dot_nt(keys, q_o[:, h * HEAD:(h + 1) * HEAD])
                weights = jnp.exp(CAP * jnp.tanh(scores * (scale / CAP)))
                if masked:
                    key_pos = p * tile + lax.broadcasted_iota(jnp.int32, weights.shape, 0)
                    allowed = key_pos <= lax.broadcasted_iota(jnp.int32, weights.shape, 1)
                    weights = jnp.where(allowed, weights, 0.0)
                totals[h:h + 1] += jnp.sum(weights, axis=0, keepdims=True)
                turned_sum[h] += dot_tn(values, weights.astype(BF))

    def own_step(p, carry):
        key_step(c, p, True)
        return carry

    out_copy(c).start()
    lax.fori_loop(0, T // per, own_step, 0)

    def far_block(i, carry):
        @pl.when(i < c)
        def _():
            b = c - 1 - i
            for j in range(T):
                kv_from(b, j).wait_recv()
            out_copy(b).start()

            def far_step(p, carry):
                key_step(b, p, False)
                return carry

            lax.fori_loop(0, T // per, far_step, 0)

        return carry

    lax.fori_loop(0, NC - 1, far_block, 0)
    for h in range(Hq // HEAD):
        heads_o[:, h * HEAD:(h + 1) * HEAD] = (turned_sum[h] / totals[h:h + 1]).T.astype(BF)
    logt_o[...] = jnp.log(totals[...])

    for i in range(3):
        for o in range(NDP - 1):
            weight_remote(i, o).wait_send()

    def close_parts(i, carry):
        for w in range(4):
            for o in range(NDP - 1):
                part_remote(w, i, o).wait()
            if moved[w][3]:
                part_local(w, i).wait()
        return carry

    lax.fori_loop(0, T, close_parts, 0)
    for s in range(C):
        for side in (0, 1):
            for k in range(T - 1):

                @pl.when(ag_there(side, k) & onward(side))
                def _():
                    ag_copy(s, side, k, ag_block(side, k)).wait_send()

    for j in range(T):
        copies = pair_copies(j)
        copies[0].wait()
        for copy in copies[1:]:
            copy.wait()

    def close(i, carry):
        @pl.when(c + 1 + i <= NC - 1)
        def _():
            for j in range(T):
                kv_copy(i + 1, j).wait_send()

        return carry

    lax.fori_loop(0, NC - 1, close, 0)

    def close_out(b, carry):
        @pl.when(b <= c)
        def _():
            out_copy(b).wait()

        return carry

    lax.fori_loop(0, NC, close_out, 0)


def front_call(layer_in, norm_gains, frequency, w_query, w_key, w_value, w_out, w_gate, w_up, w_down):
    T, NC, NDP = lax.axis_size("tp"), lax.axis_size("ctx"), lax.axis_size("dp")
    C = T
    Lr, D = layer_in.shape
    R = T * Lr
    Hq, KVd = w_query.shape[1], w_key.shape[1]
    Dh = D // NDP
    F = w_gate.shape[1]
    H = Hq // HEAD
    any_spec = pl.BlockSpec(memory_space=pl.ANY)
    vm = pl.BlockSpec(memory_space=pltpu.VMEM)
    sds = jax.ShapeDtypeStruct
    dma = pltpu.SemaphoreType.DMA
    return pl.pallas_call(
        functools.partial(front_kernel, T, NC, NDP, KVd // HEAD, C),
        out_shape=(
            sds((R, Hq), BF), sds((R, Hq), BF), sds((H, R), F32),
            sds((R, HEAD // 2), F32), sds((R, HEAD // 2), F32),
            sds((NC, T, 2, Lr, KVd), BF), sds((NDP, T, Lr, Dh), BF),
            sds((Hq, D), BF), sds((D, F), BF), sds((F, D), BF), sds((D, F), BF),
        ),
        in_specs=[vm] * 3 + [any_spec] * 7,
        out_specs=[vm] * 5 + [any_spec] * 6,
        scratch_shapes=[
            pltpu.VMEM((T, Lr, D), BF), pltpu.VMEM((D, Hq), BF), pltpu.VMEM((D, KVd), BF), pltpu.VMEM((D, KVd), BF),
            pltpu.VMEM((NC, T, 2, Lr, KVd), BF), pltpu.VMEM((H, HEAD, R), F32), pltpu.VMEM((H, R), F32),
            pltpu.VMEM((Dh, F), BF), pltpu.VMEM((F, Dh), BF), pltpu.VMEM((F, Dh), BF), pltpu.VMEM((Dh, F), BF),
            dma((2 * NDP - 1, 3)), dma((C, 2, T - 1)), dma((C, 2, T - 1)), dma((2 * NDP - 1, T)),
            dma((NC - 1, T)), dma((NC - 1, T)), dma((NC,)), dma((2,)), dma((2 * NDP - 1, 4, T)),
        ],
        compiler_params=pltpu.CompilerParams(
            collective_id=2, has_side_effects=True, vmem_limit_bytes=66_000_000
        ),
        name="front",
    )(layer_in, norm_gains, frequency, w_query, w_key, w_value, w_out, w_gate, w_up, w_down)


def finish_kernel(width, count, gains_ref, *refs):
    n = count
    srcs, gain_o, dsts = refs[:n], refs[n], refs[n + 1:2 * n + 1]
    held, wide, sems = refs[2 * n + 1:3 * n + 1], refs[3 * n + 1:-1], refs[-1]
    for i in range(n):
        pltpu.make_async_copy(srcs[i], held[i], sems.at[0, i]).start()
    rank = lax.axis_index("dp")
    for axis in ("ctx", "tp"):
        rank = rank * lax.axis_size(axis) + lax.axis_index(axis)
    gains = gains_ref[...]
    total = gains.shape[1]
    gain_o[...] = pltpu.roll(gains, lax.rem(total - rank * width, total), axis=1)[:4, :width]
    buffers = []
    for i in range(n):
        pltpu.make_async_copy(srcs[i], held[i], sems.at[0, i]).wait()
        buffer = held[i]
        if held[i].dtype != dsts[i].dtype:
            buffer = wide[len([b for b in buffers if b])]
            buffer[...] = held[i][...].astype(buffer.dtype)
        buffers.append(buffer is not held[i])
        pltpu.make_async_copy(buffer, dsts[i], sems.at[1, i]).start()
    used = 0
    for i in range(n):
        buffer = wide[used] if buffers[i] else held[i]
        used += buffers[i]
        pltpu.make_async_copy(buffer, dsts[i], sems.at[1, i]).wait()


def finish_call(gains, arrays, dtypes):
    width = gains.shape[1] // (lax.axis_size("tp") * lax.axis_size("ctx") * lax.axis_size("dp"))
    any_spec = pl.BlockSpec(memory_space=pl.ANY)
    vm = pl.BlockSpec(memory_space=pltpu.VMEM)
    sds = jax.ShapeDtypeStruct
    n = len(arrays)
    return pl.pallas_call(
        functools.partial(finish_kernel, width, n),
        out_shape=[sds((4, width), F32)] + [sds(a.shape, d) for a, d in zip(arrays, dtypes, strict=True)],
        in_specs=[vm] + [any_spec] * n,
        out_specs=[vm] + [any_spec] * n,
        scratch_shapes=[pltpu.VMEM(a.shape, a.dtype) for a in arrays]
        + [pltpu.VMEM(a.shape, d) for a, d in zip(arrays, dtypes, strict=True) if a.dtype != d]
        + [pltpu.SemaphoreType.DMA((2, n))],
        compiler_params=pltpu.CompilerParams(vmem_limit_bytes=66_000_000),
        name="finish",
    )(gains, *arrays)


def shards(layer_in, cotangent, norm_gains, w_query, w_key, w_value, w_out, w_gate, w_up, w_down):
    half_width = HEAD // 2
    frequency = THETA ** (-(jnp.arange(half_width, dtype=F32) * 2.0) / HEAD)
    query, head_rows, log_totals, cosine, sine, keys_values, rows_one, *weights = front_call(
        layer_in, norm_gains, frequency[None, :], w_query, w_key, w_value, w_out, w_gate, w_up, w_down
    )
    layer_out, input_grad, gains, down_sum, *sums = main_call(
        layer_in, cotangent, norm_gains, head_rows, w_out, w_gate, *weights,
        query, log_totals, cosine, sine, keys_values, rows_one, w_query, w_key, w_value,
    )
    arrays = [layer_out, input_grad, down_sum, *sums]
    gain_grads, layer_out, input_grad, down_turned, grad_gate, grad_up, out_turned, *rest = finish_call(
        gains, arrays, [BF] + [F32] * (len(arrays) - 1)
    )
    return (layer_out, input_grad, gain_grads, *rest, out_turned.T, grad_gate, grad_up, down_turned.T)


def solution(mesh):
    return jax.shard_map(
        shards,
        mesh=mesh,
        in_specs=(
            P(("dp", "ctx", "tp"), None),
            P(("dp", "ctx", "tp"), None),
            P(),
            P("dp", "tp"),
            P("dp", "tp"),
            P("dp", "tp"),
            P("tp", "dp"),
            P("dp", "tp"),
            P("dp", "tp"),
            P("tp", "dp"),
        ),
        out_specs=(
            P(("dp", "ctx", "tp"), None),
            P(("dp", "ctx", "tp"), None),
            P(None, ("dp", "ctx", "tp")),
            P(("dp", "ctx"), "tp"),
            P(("dp", "ctx"), "tp"),
            P(("dp", "ctx"), "tp"),
            P("tp", ("dp", "ctx")),
            P(("dp", "ctx"), "tp"),
            P(("dp", "ctx"), "tp"),
            P("tp", ("dp", "ctx")),
        ),
        check_vma=False,
    )
```

time: 407 us -> 398 us (0.978)
  Pallas kernels: 405 us -> 397 us
    pallas_call x2 -> x1, Pallas kernels: 340 us -> 332 us  [main_call(): pl.pallas_call(functools.partial(main_kernel, T, C, NC, NDP, KVd // HEAD,...]
where the time goes in v6:
time: 398 us
  Pallas kernels  397 us (100%)
    pallas_call x1, Pallas kernels, main_call(): pl.pallas_call(functools.partial(main_kernel, T, C, NC, NDP, KVd // HEAD,...  332 us
    pallas_call x1, Pallas kernels, front_call(): pl.pallas_call(functools.partial(front_kernel, T, NC, NDP, KVd // HEAD, C...  57.2 us

profile of v6, /device:TPU:0, one launch (start us, length us, event | category | flops | bytes accessed | tf_op | source)
XLA Modules:
  0.0 397.9 jit_solution(1755280179309694307)
XLA Ops:
  0.6 0.5 multiply_power_fusion.freq_ref
  1.2 57.2 %front.1 = (bf16[512,512]{1,0:T(8,128)(2,1)}, bf16[512,512]{1,0:T(8,128)(2,1)}, f32[2,512]{1,0:T(2,128)}, f32[512,128]{1,0:T(8,128)}, f32[512,128]{1,0:T(8,128)}...) custom-call(bf16[128,2304]{1,0:T(8,128)(2,1)} %x_ref.3, ...), custom_call_target="tpu_custom_call" | custom-call | tf_op jit(solution)/shard_map/front/pallas_call | solution.py:1448
  58.4 331.7 %main.1 = (bf16[128,2304]{1,0:T(8,128)(2,1)}, f32[128,2304]{1,0:T(8,128)}, f32[4,2304]{1,0:T(4,128)}, bf16[288,2304]{1,0:T(8,128)(2,1)}, bf16[288,2304]{1,0:T(8,...) custom-call(bf16[128,2304]{1,0:T(8,128)(2,1)} %x_ref.3, ...), custom_call_target="tpu_custom_call" | custom-call | tf_op jit(solution)/shard_map/main/pallas_call | solution.py:1088
  390.1 7.7 %finish.1 = (f32[4,72]{1,0:T(4,128)}, bf16[128,2304]{1,0:T(8,128)(2,1)}, f32[128,2304]{1,0:T(8,128)}, f32[288,2304]{1,0:T(8,128)}, f32[288,2304]{1,0:T(8,128)}, ...) custom-call(f32[4,2304]{1,0:T(4,128)} %get-tuple-element.52.gains_re, ...), custom_call_target="tpu_custom_call" | custom-call | tf_op jit(solution)/shard_map/finish/pallas_call | solution.py:1506

commit v7 on v6

--- a/solution.py
+++ b/solution.py
@@ -75,11 +75,11 @@
     x_ref, ct_ref, gain_ref, heads_ref,
     wo_ref, wg_ref, wo_other, wg_other, wut_ref, wdt_ref, q_ref, logt_ref, cos_ref, sin_ref, kv_ref, rows1_ref,
     wq_ref, wk_ref, wv_ref,
-    out_ref, igrad_ref, gains_ref,
-    down_o, gate_o, up_o, out_o, q_o, k_o, v_o,
+    out_o, igrad_o, gains_ref,
+    down_o, gate_o, up_o, wout_o, q_o, k_o, v_o,
     rows_pair, hid_pair, branch_pair, gate_pair, up_pair, attn_pair, head_pair,
-    wo_v, wd_v, X, Pb, Rb, att, mid, acc, mdelta, gsum, hdelta, Ab, Bb, L0, Rc, st, G, GR,
-    w_sem, f_sem, rs_send, rs_recv, ag_send, ag_recv, pair_sem, l_sem, r_sem, e_send, e_recv, st_sem,
+    out_ref, igrad_ref, wo_v, wd_v, X, Pb, Rb, att, mid, acc, mdelta, gsum, hdelta, Ab, Bb, L0, Rc, st, G, GR,
+    w_sem, f_sem, b_sem, rs_send, rs_recv, ag_send, ag_recv, pair_sem, l_sem, r_sem, e_send, e_recv, st_sem,
     s_sem, q_sem, kv_send, kv_recv, last_send, last_recv, g_send, g_recv, kvb_sem, free_sem, enter_sem,
 ):
     t, c, dp = lax.axis_index("tp"), lax.axis_index("ctx"), lax.axis_index("dp")
@@ -312,9 +312,10 @@
     def comm(tau, w, a):
         back = tau - a
 
-        @pl.when((back >= 0) & (back < 3 * C))
+        @pl.when(((back >= 0) & (back < 2 * C)) | ((back >= begin) & (back < begin + C)))
         def _():
-            n, s = back // C, lax.rem(back, C)
+            n = jnp.where(back < 2 * C, back // C, 2)
+            s = jnp.where(back < 2 * C, lax.rem(back, C), back - begin)
             if w <= T - 2:
                 rs_step(s, w)
             elif w == T - 1:
@@ -397,7 +398,8 @@
             def _():
                 act(kind)
 
-    branch_load = pltpu.make_async_copy(branch_pair, L0, l_sem.at[0])
+    def branch_load(s):
+        return pltpu.make_async_copy(branch_pair.at[:, s], L0.at[:, s], b_sem.at[s])
 
     def store(u, par, w, first, second):
         product = dot_tn(first.reshape(tokens, Dh), second)
@@ -437,9 +439,9 @@
             spans = [(0, NF, down_o), (NF, 2 * NF, gate_o), (2 * NF, 3 * NF, up_o)]
         elif w == W:
             spans = [(0, NF, down_o), (NF, 2 * NF, gate_o), (2 * NF, 3 * NF, up_o)]
-            spans += [(wide_units, q_first, out_o), (q_first, kv_first, q_o)]
+            spans += [(wide_units, q_first, wout_o), (q_first, kv_first, q_o)]
         else:
-            spans = [(wide_units, q_first, out_o), (q_first, kv_first, q_o)]
+            spans = [(wide_units, q_first, wout_o), (q_first, kv_first, q_o)]
         found = [
             (
                 (u >= low) & (u < high),
@@ -487,17 +489,12 @@
 
     def compute_open(s):
         signal_all(free_sem, ctx_meets)
-        pair_kept(2, s)
 
         def each(i, carry):
-            pair_kept(1, i)
-            pair_received(1, i)
-            pair_received(2, i)
+            branch_load(i).wait()
             return carry
 
         lax.fori_loop(0, C, each, 0)
-        branch_load.start()
-        chunk_copy(jnp.int32(0), 0).start()
 
     def stages(wg_v, wu_v, hid):
         env.update(hid=hid)
@@ -574,11 +571,23 @@
                 tiles(F, lambda at, tile: gate_up_delta(s, at))
                 pair_start(3, s)
                 pair_start(4, s)
+                pair_kept(2, s)
+                pair_received(2, s)
+                branch_load(s).start()
+
+                @pl.when(s == 0)
+                def _():
+                    def each(i, carry):
+                        pair_kept(1, i)
+                        pair_received(1, i)
+                        return carry
+
+                    lax.fori_loop(0, C, each, 0)
+                    chunk_copy(jnp.int32(0), 0).start()
 
             @pl.when(tau == begin)
             def _():
                 compute_open(s)
-                branch_load.wait()
                 wide_product(jnp.int32(0))
                 pl.semaphore_wait(free_sem, len(ctx_meets))
                 e_send_step(jnp.int32(0), 0, W)
@@ -613,14 +622,12 @@
                     ),
                 )
                 pair_away(2, s)
-
-                @pl.when(s < C - 1)
-                def _():
-                    pair_kept(2, s)
-
                 ag_sent(s)
 
-            rs_start(s)
+            @pl.when((n < 2) | (tau == begin))
+            def _():
+                rs_start(jnp.where(n < 2, s, 0))
+
             for a in range(1, T):
                 comm(tau, 2 * a, a)
             return carry
@@ -647,6 +654,9 @@
         ]
         for copy in small_loads:
             copy.start()
+        out_copy = pltpu.make_async_copy(out_ref, out_o, l_sem.at[4])
+        igrad_copy = pltpu.make_async_copy(igrad_ref, igrad_o, l_sem.at[5])
+        out_copy.start()
 
         rows_at = pl.ds(pl.multiple_of(dp * Dh, 128), Dh)
         spread = [(wq_ref, WQ.at[rows_at]), (wk_ref, WK.at[rows_at]), (wv_ref, WV.at[rows_at])]
@@ -835,22 +845,37 @@
             G[0, 0:1] = terms
             G[0, 1:4] = gsum[...]
 
-        meets = [("tp", t, b) for b in bits_below(T)] + [("ctx", c, b) for b in bits_below(NC)]
-        meets += [("dp", dp, b) for b in bits_below(NDP)]
-
-        def g_copy(k):
-            axis, index, bit = meets[k]
-            return remote(G.at[k], GR.at[k], g_send.at[k], g_recv.at[k], along(axis, flip(index, bit)))
-
-        def g_steps(i, half):
-            for k in range(half, len(meets), 2):
-
-                @pl.when(i == C + T + 2 + k // 2)
-                def _():
-                    g_copy(k).wait_recv()
-                    G[k + 1] = G[k] + GR[k]
+        meets = [("tp", t, T), ("ctx", c, NC), ("dp", dp, NDP)]
+        g_base = [0, T - 1, T + NC - 2]
+
+        def g_copies(k):
+            axis, index, count = meets[k]
+            return [
+                remote(
+                    G.at[k], GR.at[g_base[k] + o - 1], g_send.at[g_base[k] + o - 1], g_recv.at[g_base[k] + o - 1],
+                    along(axis, lax.rem(index + o, count)),
+                )
+                for o in range(1, count)
+            ]
+
+        def g_start(k):
+            for copy in g_copies(k):
+                copy.start()
+
+        def g_steps(i, place):
+            for k in range(len(meets)):
+                if k != place:
+                    continue
+
+                @pl.when(i == attend_at + T + 2)
+                def _():
+                    total = G[k]
+                    for o, copy in enumerate(g_copies(k)):
+                        copy.wait_recv()
+                        total += GR[g_base[k] + o]
+                    G[k + 1] = total
                     if k + 1 < len(meets):
-                        g_copy(k + 1).start()
+                        g_start(k + 1)
 
         def up_open():
             def each(s, carry):
@@ -935,6 +960,29 @@
 
                     lax.fori_loop(0, 2, key_part, 0)
 
+        attend_at = C + 1
+
+        def first_tick(i):
+            return begin + 1 + i + jnp.minimum(i // 2, C - 2)
+
+        def line_tick(tau):
+            for a in range(1, T):
+                comm(tau, 2 * a - 1, a)
+
+            @pl.when(tau < begin + C)
+            def _():
+                rs_start(tau - begin)
+
+            @pl.when(tau >= begin + C)
+            def _():
+                s = tau - begin - C
+                pair_start(5, s)
+                hdelta[:, s] = dot_nt(rows_of(s), wo_v[...]).astype(BF).reshape(T, rc, Hq)
+                rs_sent(s)
+
+            for a in range(1, T):
+                comm(tau, 2 * a, a)
+
         def tick(i, carry):
             u = i + 1
 
@@ -957,37 +1005,31 @@
                     for o in range(NDP - 1):
                         spread_remote(w, o).start()
 
-            @pl.when(i < C)
-            def _():
-                tau = 3 * C + i
-                for a in range(1, T):
-                    comm(tau, 2 * a - 1, a)
-                pair_start(5, i)
-                hdelta[:, i] = dot_nt(rows_of(i), wo_v[...]).astype(BF).reshape(T, rc, Hq)
-                rs_sent(i)
-                for a in range(1, T):
-                    comm(tau, 2 * a, a)
-
-            @pl.when(i == C)
+            @pl.when(i < attend_at)
+            def _():
+                line_tick(first_tick(i))
+
+            @pl.when(i == attend_at)
             def _():
                 for copy in small_loads:
                     copy.wait()
                 attention()
 
-            @pl.when(i == C + 2)
+            @pl.when(i == attend_at + 2)
             def _():
                 own_keys()
 
             for k in range(1, T - 1):
 
-                @pl.when(i == C + 2 + k)
+                @pl.when(i == attend_at + 2 + k)
                 def _():
                     last_step(k)
 
-            @pl.when(i == C + T + 1)
+            @pl.when(i == attend_at + T + 1)
             def _():
                 last_finish()
-                g_copy(0).start()
+                igrad_copy.start()
+                g_start(0)
 
             for k in range(1, m):
 
@@ -996,12 +1038,20 @@
                     e_send_step(u - k, k, w)
 
                 by_width(u - k, middle)
+
+            @pl.when((lax.rem(i, 2) == 1) & (i <= 2 * C - 5))
+            def _():
+                line_tick(first_tick(i) + 1)
+
+            g_steps(i, 1)
             by_width(u - m, lambda w: e_finish(u - m, w))
-            g_steps(i, 1)
+            g_steps(i, 2)
             return carry
 
         lax.fori_loop(0, units + m - 1, tick, 0)
         gains_ref[...] = G[len(meets)]
+        out_copy.wait()
+        igrad_copy.wait()
 
         for u in (units - 2, units - 1):
             out_wait(jnp.int32(u))
@@ -1015,7 +1065,8 @@
                     last_copy(side, k, rs_block(side, k)).wait_send()
 
         for k in range(len(meets)):
-            g_copy(k).wait_send()
+            for copy in g_copies(k):
+                copy.wait_send()
         for o in range(NDP - 1):
             for i in range(3):
                 spread_remote(i, o).wait_send()
@@ -1047,7 +1098,7 @@
     pl.run_scoped(
         stages, vmem((D, F), BF), vmem((F, D), BF), vmem((C, M, F), BF)
     )
-    kv_slots = min(NC, 3)
+    kv_slots = NC if NC <= 4 else 3
     pl.run_scoped(
         finishing,
         vmem((2, NDP, C, T, rc, Dh), BF), vmem((NDP, C, T, rc, Hq), BF),
@@ -1077,7 +1128,7 @@
     pitch = -(-RB // 16) * 16
     blocks = NP * 2 * NC + NR * 2 * (NC - 1)
     W = next(w for w in (tile_of(F) // 2, 256, 128) if F % (2 * w) == 0 and blocks <= (D // pitch) * (F // w))
-    meets = sum(n.bit_length() - 1 for n in (T, NC, NDP))
+    meets = T + NC + NDP - 3
     any_spec = pl.BlockSpec(memory_space=pl.ANY)
     vm = pl.BlockSpec(memory_space=pltpu.VMEM)
     sds = jax.ShapeDtypeStruct
@@ -1094,15 +1145,16 @@
             half_rows, hidden_rows, half_rows, hidden_rows, hidden_rows, half_rows, sds((NDP, C, T, rc, Hq), BF),
         ),
         in_specs=[vm] * 4 + [any_spec] * 7 + [vm] + [any_spec] * 7,
-        out_specs=[vm] * 3 + [any_spec] * 14,
+        out_specs=[any_spec] * 2 + [vm] + [any_spec] * 14,
         scratch_shapes=[
+            vmem((Lr, D), BF), vmem((Lr, D), F32),
             vmem((Hq, D), BF), vmem((D, F), BF), vmem((C, T, rc, D), BF), vmem((C, T, rc, D), BF),
             vmem((C, T + 1, rc, D), BF), vmem((C, rc, D), F32), vmem((C, rc, D), F32), vmem((rc, D), F32),
             vmem((Lr, D), F32), vmem((3, D), F32), vmem((T, C, rc, Hq), BF), vmem((C, M, F), BF), vmem((C, M, F), BF),
             vmem((NDP, C, T, rc, Dh), BF), vmem((NDP, C, M, 2 * W), BF), vmem((2, 2, RB, W), BF),
-            vmem((meets + 1, 4, D), F32), vmem((meets, 4, D), F32),
-            dma((NDP,)), dma((3, 2 * T)), dma((C, 2, T - 1)), dma((C, 2, T - 1)), dma((C, 2, T - 1)), dma((C, 2, T - 1)),
-            dma((2 * NDP - 1, 7, C)), dma((4,)), dma((1,)), dma((NP, 2, NC - 1)), dma((NR, 2, NC - 1)), dma((2, 2)),
+            vmem((4, 4, D), F32), vmem((meets, 4, D), F32),
+            dma((NDP,)), dma((3, 2 * T)), dma((C,)), dma((C, 2, T - 1)), dma((C, 2, T - 1)), dma((C, 2, T - 1)), dma((C, 2, T - 1)),
+            dma((2 * NDP - 1, 7, C)), dma((6,)), dma((1,)), dma((NP, 2, NC - 1)), dma((NR, 2, NC - 1)), dma((2, 2)),
             dma((2 * NDP - 1, 3)), dma((3 + 4 * (NDP - 1),)), dma((NC - 1,)), dma((NC - 1,)),
             dma((2, T - 1)), dma((2, T - 1)), dma((meets,)), dma((meets,)), dma((2,)),
             pltpu.SemaphoreType.REGULAR, pltpu.SemaphoreType.REGULAR,

time: 398 us -> 391 us (0.982)
  Pallas kernels: 397 us -> 390 us
    pallas_call x1, Pallas kernels: 332 us -> 325 us  [main_call(): pl.pallas_call(functools.partial(main_kernel, T, C, NC, NDP, KVd // HEAD,...]
where the time goes in v7:
time: 391 us
  Pallas kernels  390 us (100%)
    pallas_call x1, Pallas kernels, main_call(): pl.pallas_call(functools.partial(main_kernel, T, C, NC, NDP, KVd // HEAD,...  325 us
    pallas_call x1, Pallas kernels, front_call(): pl.pallas_call(functools.partial(front_kernel, T, NC, NDP, KVd // HEAD, C...  57.2 us

profile of v7, /device:TPU:0, one launch (start us, length us, event | category | flops | bytes accessed | tf_op | source)
XLA Modules:
  0.0 391.1 jit_solution(1930303036106039658)
XLA Ops:
  0.6 0.5 multiply_power_fusion.freq_ref
  1.2 57.2 %front.1 = (bf16[512,512]{1,0:T(8,128)(2,1)}, bf16[512,512]{1,0:T(8,128)(2,1)}, f32[2,512]{1,0:T(2,128)}, f32[512,128]{1,0:T(8,128)}, f32[512,128]{1,0:T(8,128)}...) custom-call(bf16[128,2304]{1,0:T(8,128)(2,1)} %x_ref.3, ...), custom_call_target="tpu_custom_call" | custom-call | tf_op jit(solution)/shard_map/front/pallas_call | solution.py:1500
  58.4 324.9 %main.1 = (bf16[128,2304]{1,0:T(8,128)(2,1)}, f32[128,2304]{1,0:T(8,128)}, f32[4,2304]{1,0:T(4,128)}, bf16[288,2304]{1,0:T(8,128)(2,1)}, bf16[288,2304]{1,0:T(8,...) custom-call(bf16[128,2304]{1,0:T(8,128)(2,1)} %x_ref.3, ...), custom_call_target="tpu_custom_call" | custom-call | tf_op jit(solution)/shard_map/main/pallas_call | solution.py:1139
  383.3 7.7 %finish.1 = (f32[4,72]{1,0:T(4,128)}, bf16[128,2304]{1,0:T(8,128)(2,1)}, f32[128,2304]{1,0:T(8,128)}, f32[288,2304]{1,0:T(8,128)}, f32[288,2304]{1,0:T(8,128)}, ...) custom-call(f32[4,2304]{1,0:T(4,128)} %get-tuple-element.52.gains_re, ...), custom_call_target="tpu_custom_call" | custom-call | tf_op jit(solution)/shard_map/finish/pallas_call | solution.py:1558

commit v8 on v7

--- a/solution.py
+++ b/solution.py
@@ -1251,7 +1251,7 @@
             weight_remote(i, o).start()
 
     def parts(ref, i):
-        height = ref.shape[0] // T
+        height = ref.shape[0] // (2 * T)
         return pl.ds(pl.multiple_of(i * height, 16), height), height
 
     def part_dst(dst, ref, i, columns):
@@ -1354,7 +1354,93 @@
         for h in range(Hq // HEAD):
             q_o[at, h * HEAD:(h + 1) * HEAD] = turned(values, h, at)
 
+    has_late = (t == 0) | (t == T - 1)
+    late = jnp.where(t == 0, T - 1, 0)
+    late_at = pl.ds(pl.multiple_of(late * Lr, Lr), Lr)
+
+    def out_copy(b):
+        return pltpu.make_async_copy(KV.at[b], kv_o.at[b], out_sem.at[b])
+
+    def key_step(b, first, count, masked, queries):
+        tile = count * Lr
+        for kh in range(KH):
+            cols = slice(kh * HEAD, (kh + 1) * HEAD)
+            keys = KV[b, pl.ds(first, count), 0, :, cols].reshape(tile, HEAD)
+            values = KV[b, pl.ds(first, count), 1, :, cols].reshape(tile, HEAD)
+            for g in range(GS):
+                h = kh * GS + g
+                head = slice(h * HEAD, (h + 1) * HEAD)
+                query = q_o[late_at, head] if queries == "late" else q_o[:, head]
+                weights = jnp.exp(CAP * jnp.tanh(dot_nt(keys, query) * (scale / CAP)))
+                query_pos = lax.broadcasted_iota(jnp.int32, weights.shape, 1)
+                if queries == "late":
+                    query_pos += late * Lr
+                if masked:
+                    key_pos = first * Lr + lax.broadcasted_iota(jnp.int32, weights.shape, 0)
+                    weights = jnp.where(key_pos <= query_pos, weights, 0.0)
+                if queries == "early":
+                    weights = jnp.where(query_pos // Lr == late, 0.0, weights)
+                at = late_at if queries == "late" else slice(None)
+                totals[h:h + 1, at] += jnp.sum(weights, axis=0, keepdims=True)
+                turned_sum[h, :, at] += dot_tn(values, weights.astype(BF))
+
+    def by_block(b, body):
+        pl.when(b == c)(lambda: body(True))
+        pl.when(b < c)(lambda: body(False))
+
+    def early_rows():
+        turned_sum[...] = jnp.zeros_like(turned_sum)
+        totals[...] = jnp.zeros_like(totals)
+
+        def block(i, carry):
+            b = c - i
+
+            @pl.when(b >= 0)
+            def _():
+                def rows_of(j, inner):
+                    @pl.when(jnp.logical_not(has_late) | (j != late))
+                    def _():
+                        pl.when(b < c)(lambda: kv_from(b, j).wait_recv())
+                        by_block(b, lambda masked: key_step(b, j, 1, masked, "all"))
+
+                    return inner
+
+                lax.fori_loop(0, T, rows_of, 0)
+
+            return carry
+
+        lax.fori_loop(0, NC, block, 0)
+
+    def late_rows():
+        @pl.when(has_late)
+        def _():
+            for h in range(Hq // HEAD):
+                turned_sum[h, :, late_at] = jnp.zeros((HEAD, Lr), F32)
+                totals[h:h + 1, late_at] = jnp.zeros((1, Lr), F32)
+
+        def block(i, carry):
+            b = c - i
+
+            @pl.when(b >= 0)
+            def _():
+                @pl.when(has_late)
+                def _():
+                    pl.when(b < c)(lambda: kv_from(b, late).wait_recv())
+
+                    def both(masked):
+                        key_step(b, 0, T, masked, "late")
+                        key_step(b, late, 1, masked, "early")
+
+                    by_block(b, both)
+
+                out_copy(b).start()
+
+            return carry
+
+        lax.fori_loop(0, NC, block, 0)
+
     def gather(k, carry):
+        pl.when(k == T - 1)(early_rows)
         for side in (0, 1):
 
             @pl.when(ag_there(side, k) & (k > 0))
@@ -1372,67 +1458,19 @@
             def _():
                 project(ag_block(side, k))
 
-        part_start(0, k)
-        part_start(1, k)
-
-        @pl.when(k == 0)
-        def _():
-            turn()
-
-        part_start(2, k)
-        part_start(3, k)
+        pl.when(k == 0)(turn)
+
+        def send_parts(i, inner):
+            for w in range(4):
+                part_start(w, i)
+            return inner
+
+        lax.fori_loop((2 * T * k) // (T - 1), jnp.minimum((2 * T * (k + 1)) // (T - 1), 2 * T), send_parts, 0)
         return carry
 
     lax.fori_loop(0, T, gather, 0)
 
-    per = max(1, 256 // Lr)
-    tile = per * Lr
-    turned_sum[...] = jnp.zeros_like(turned_sum)
-    totals[...] = jnp.zeros_like(totals)
-
-    def out_copy(b):
-        return pltpu.make_async_copy(KV.at[b], kv_o.at[b], out_sem.at[b])
-
-    def key_step(b, p, masked):
-        for kh in range(KH):
-            cols = slice(kh * HEAD, (kh + 1) * HEAD)
-            keys = KV[b, pl.ds(p * per, per), 0, :, cols].reshape(tile, HEAD)
-            values = KV[b, pl.ds(p * per, per), 1, :, cols].reshape(tile, HEAD)
-            for g in range(GS):
-                h = kh * GS + g
-                scores = dot_nt(keys, q_o[:, h * HEAD:(h + 1) * HEAD])
-                weights = jnp.exp(CAP * jnp.tanh(scores * (scale / CAP)))
-                if masked:
-                    key_pos = p * tile + lax.broadcasted_iota(jnp.int32, weights.shape, 0)
-                    allowed = key_pos <= lax.broadcasted_iota(jnp.int32, weights.shape, 1)
-                    weights = jnp.where(allowed, weights, 0.0)
-                totals[h:h + 1] += jnp.sum(weights, axis=0, keepdims=True)
-                turned_sum[h] += dot_tn(values, weights.astype(BF))
-
-    def own_step(p, carry):
-        key_step(c, p, True)
-        return carry
-
-    out_copy(c).start()
-    lax.fori_loop(0, T // per, own_step, 0)
-
-    def far_block(i, carry):
-        @pl.when(i < c)
-        def _():
-            b = c - 1 - i
-            for j in range(T):
-                kv_from(b, j).wait_recv()
-            out_copy(b).start()
-
-            def far_step(p, carry):
-                key_step(b, p, False)
-                return carry
-
-            lax.fori_loop(0, T // per, far_step, 0)
-
-        return carry
-
-    lax.fori_loop(0, NC - 1, far_block, 0)
+    late_rows()
     for h in range(Hq // HEAD):
         heads_o[:, h * HEAD:(h + 1) * HEAD] = (turned_sum[h] / totals[h:h + 1]).T.astype(BF)
     logt_o[...] = jnp.log(totals[...])
@@ -1449,7 +1487,7 @@
                 part_local(w, i).wait()
         return carry
 
-    lax.fori_loop(0, T, close_parts, 0)
+    lax.fori_loop(0, 2 * T, close_parts, 0)
     for s in range(C):
         for side in (0, 1):
             for k in range(T - 1):
@@ -1512,7 +1550,7 @@
             pltpu.VMEM((NC, T, 2, Lr, KVd), BF), pltpu.VMEM((H, HEAD, R), F32), pltpu.VMEM((H, R), F32),
             pltpu.VMEM((Dh, F), BF), pltpu.VMEM((F, Dh), BF), pltpu.VMEM((F, Dh), BF), pltpu.VMEM((Dh, F), BF),
             dma((2 * NDP - 1, 3)), dma((C, 2, T - 1)), dma((C, 2, T - 1)), dma((2 * NDP - 1, T)),
-            dma((NC - 1, T)), dma((NC - 1, T)), dma((NC,)), dma((2,)), dma((2 * NDP - 1, 4, T)),
+            dma((NC - 1, T)), dma((NC - 1, T)), dma((NC,)), dma((2,)), dma((2 * NDP - 1, 4, 2 * T)),
         ],
         compiler_params=pltpu.CompilerParams(
             collective_id=2, has_side_effects=True, vmem_limit_bytes=66_000_000

time: 391 us -> 390 us (level)
  no operation moved by 1% of the time
where the time goes in v8:
time: 390 us
  Pallas kernels  389 us (100%)
    pallas_call x1, Pallas kernels, main_call(): pl.pallas_call(functools.partial(main_kernel, T, C, NC, NDP, KVd // HEAD,...  327 us
    pallas_call x1, Pallas kernels, front_call(): pl.pallas_call(functools.partial(front_kernel, T, NC, NDP, KVd // HEAD, C...  54.2 us

profile of v8, /device:TPU:0, one launch (start us, length us, event | category | flops | bytes accessed | tf_op | source)
XLA Modules:
  0.0 390.1 jit_solution(16633907230705625679)
XLA Ops:
  0.6 0.5 multiply_power_fusion.freq_ref
  1.2 54.2 %front.1 = (bf16[512,512]{1,0:T(8,128)(2,1)}, bf16[512,512]{1,0:T(8,128)(2,1)}, f32[2,512]{1,0:T(2,128)}, f32[512,128]{1,0:T(8,128)}, f32[512,128]{1,0:T(8,128)}...) custom-call(bf16[128,2304]{1,0:T(8,128)(2,1)} %x_ref.3, ...), custom_call_target="tpu_custom_call" | custom-call | tf_op jit(solution)/shard_map/front/pallas_call | solution.py:1538
  55.4 326.8 %main.1 = (bf16[128,2304]{1,0:T(8,128)(2,1)}, f32[128,2304]{1,0:T(8,128)}, f32[4,2304]{1,0:T(4,128)}, bf16[288,2304]{1,0:T(8,128)(2,1)}, bf16[288,2304]{1,0:T(8,...) custom-call(bf16[128,2304]{1,0:T(8,128)(2,1)} %x_ref.3, ...), custom_call_target="tpu_custom_call" | custom-call | tf_op jit(solution)/shard_map/main/pallas_call | solution.py:1139
  382.2 7.7 %finish.1 = (f32[4,72]{1,0:T(4,128)}, bf16[128,2304]{1,0:T(8,128)(2,1)}, f32[128,2304]{1,0:T(8,128)}, f32[288,2304]{1,0:T(8,128)}, f32[288,2304]{1,0:T(8,128)}, ...) custom-call(f32[4,2304]{1,0:T(4,128)} %get-tuple-element.52.gains_re, ...), custom_call_target="tpu_custom_call" | custom-call | tf_op jit(solution)/shard_map/finish/pallas_call | solution.py:1596
